TPU v7x, 128 devices: a whole 4x4x4 slice. The times are simulated.
128 devices in a mesh: ka: 16 (over y, z), row: 8 (over x, core).
Axes of the slice: x: 4, y: 4, z: 4, core: 2. Of those that a mesh axis runs over, the one named last changes fastest.
Arguments:
- base_k: float32 [128, 3], P('ka'), may hold values from 0 to 1
- counts: int32 [128], P('ka'), may hold values from 1 to 4, 320 in all
- block_order: int32 [128], P(('ka', 'row')), may hold values from 0 to 127, each once
- lattice: int32 [4096, 3], P('row'), may hold values from -8 to 7, as said below
- real_space: bfloat16 [4096, 3, 128, 2, 128], P('row', None, 'ka'), may hold values from -0.09375 to 0.09375
- eigvecs: bfloat16 [512, 128, 2, 128], P(('ka', 'row')), may hold values from -0.5 to 0.5
- occupied: int32 [512, 128], P(('ka', 'row')), may hold values 0 or 1
Outputs:
- curvature: float32 [512], P(('ka', 'row'))
Inputs may be any that keep to these rules, and one draw needn't show every extreme that they name: The counts sum to 320, and some block has count 4. `block_order`: each block stands at exactly one position. `lattice`: all 4096 R-vectors are distinct.
All inputs are finite; a program needn't handle non-finite values. No bound on the sum of `occupied` on one device may be relied on, other than what follows from the above.
Results may differ from a plain program's by a relative error of at most 0.012.
The roundings to bfloat16 on the way count: a program that leaves them out, or rounds other values in their place, can miss the bound.
Values sent between devices are 32-bit elements; how exact they have to be, the bound alone decides.
No kernel may reach another device: no remote copies, remote signals or barrier semaphores. Data moves between devices by JAX's collectives and lax.ppermute only.
A program may use at most 128 MiB of HBM per device.

v0:
```python
import math

import jax
import jax.numpy as jnp
from jax import lax
from jax.sharding import Mesh
from jax.sharding import PartitionSpec as P

SUB = 4
KA = ("ka_0", "ka_1")
KA_ROW = ("ka_0", "ka_1", "row_0", "row_1")
ROW = ("row_0", "row_1")


broadening = 1.0
refine_step = (0.05, 0.03, 0.02)


def sent_to_all(value, axis):
    copies = jnp.broadcast_to(value, (lax.axis_size(axis), *value.shape))
    return lax.all_to_all(copies, axis, split_axis=0, concat_axis=0, tiled=True)


def laid_out(pieces, dim):
    lengths = list(pieces.shape[1:])
    lengths[dim] *= pieces.shape[0]
    return jnp.moveaxis(pieces, 0, dim).reshape(lengths)


def gather_directly(value, axis, dim):
    pieces = sent_to_all(value, axis)
    return laid_out(pieces, dim)


def gather_in_order(value, axes, sequence):
    pieces = value[None]
    for k in sequence:
        pieces = lax.all_gather(pieces, axes[k], axis=0, tiled=True)
    held = [lax.axis_size(axes[k]) for k in reversed(sequence)]
    pieces = pieces.reshape(*held, *value.shape)
    turned = sorted(range(len(sequence)), key=lambda place: sequence[len(sequence) - 1 - place])
    return pieces.transpose(*turned, *range(len(sequence), pieces.ndim)).reshape(-1, *value.shape)


def gathered_by_axis(value, axes, sequence, dim):
    return laid_out(gather_in_order(value, axes, sequence), dim)


def slot_points(base_points, block_counts):
    count_float = block_counts.astype(jnp.float32)
    sub_index = jnp.arange(SUB, dtype=jnp.float32)
    fraction = (sub_index[None, :] + 0.5) / count_float[:, None] - 0.5
    refine = jnp.array(refine_step, dtype=jnp.float32)
    kpoints = base_points[:, None, :] + fraction[:, :, None] * refine[None, None, :]
    alive = jnp.arange(SUB, dtype=jnp.int32)[None, :] < block_counts[:, None]
    weight = jnp.where(alive, 1.0 / count_float[:, None], 0.0)
    block_total = base_points.shape[0]
    return (kpoints.reshape(block_total * SUB, 3), weight.reshape(block_total * SUB))


def make_phases(kpoints, lattice):
    coords = lattice.astype(jnp.float32)
    angles = (
        2.0
        * math.pi
        * (
            kpoints[:, 0:1] * coords[None, :, 0]
            + kpoints[:, 1:2] * coords[None, :, 1]
            + kpoints[:, 2:3] * coords[None, :, 2]
        )
    )
    cosines = jnp.cos(angles)
    sines = jnp.sin(angles)
    coord_x = coords[None, :, 0]
    coord_y = coords[None, :, 1]
    return jnp.stack(
        [cosines, sines, -coord_x * sines, coord_x * cosines, -coord_y * sines, coord_y * cosines]
    ).astype(jnp.bfloat16)


def combine(first_part, second_part):
    real_part = first_part[..., 0, :] - second_part[..., 1, :]
    imag_part = second_part[..., 0, :] + first_part[..., 1, :]
    return jnp.stack([real_part, imag_part], axis=-2)


def fourier(kpoints, lattice, real_space):
    phase_rows = make_phases(kpoints, lattice)
    row_count = kpoints.shape[0]
    r_count = real_space.shape[0]
    slab_rows = real_space.shape[2]
    width = real_space.shape[4]
    matrix_h = real_space[:, 0].reshape(r_count, slab_rows * 2 * width)
    matrix_a = real_space[:, 1:3].reshape(r_count, 2 * slab_rows * 2 * width)
    product_h = jnp.dot(
        phase_rows.reshape(6 * row_count, r_count), matrix_h, preferred_element_type=jnp.float32
    ).reshape(6, row_count, slab_rows, 2, width)
    product_a = jnp.dot(
        phase_rows[0:2].reshape(2 * row_count, r_count),
        matrix_a,
        preferred_element_type=jnp.float32,
    ).reshape(2, row_count, 2, slab_rows, 2, width)
    pieces = [
        combine(product_h[0], product_h[1]),
        combine(product_h[2], product_h[3]),
        combine(product_h[4], product_h[5]),
        combine(product_a[0, :, 0], product_a[1, :, 0]),
        combine(product_a[0, :, 1], product_a[1, :, 1]),
    ]
    return jnp.stack(pieces, axis=1)


def curvature(k_field, vectors, occupied, weight):
    best = lax.Precision.HIGHEST
    width = k_field.shape[-1]
    vectors_f = vectors.astype(jnp.float32)
    mat_real = k_field[:, :, :, 0, :]
    mat_imag = k_field[:, :, :, 1, :]
    vec_real = vectors_f[:, :, 0, :]
    vec_imag = vectors_f[:, :, 1, :]
    turned_real = jnp.einsum("ncij,njb->ncib", mat_real, vec_real, precision=best) - jnp.einsum(
        "ncij,njb->ncib", mat_imag, vec_imag, precision=best
    )
    turned_imag = jnp.einsum("ncij,njb->ncib", mat_real, vec_imag, precision=best) + jnp.einsum(
        "ncij,njb->ncib", mat_imag, vec_real, precision=best
    )
    energy = jnp.sum(vec_real * turned_real[:, 0] + vec_imag * turned_imag[:, 0], axis=1)
    bar_real = jnp.einsum(
        "nia,ncib->ncab", vec_real, turned_real[:, 1:], precision=best
    ) + jnp.einsum("nia,ncib->ncab", vec_imag, turned_imag[:, 1:], precision=best)
    bar_imag = jnp.einsum(
        "nia,ncib->ncab", vec_real, turned_imag[:, 1:], precision=best
    ) - jnp.einsum("nia,ncib->ncab", vec_imag, turned_real[:, 1:], precision=best)
    spacing = energy[:, None, :] - energy[:, :, None]
    smoothed = spacing / (spacing * spacing + broadening)
    xcov_real = bar_real[:, 2] + smoothed * bar_real[:, 0]
    xcov_imag = bar_imag[:, 2] + smoothed * bar_imag[:, 0]
    ycov_real = bar_real[:, 3] + smoothed * bar_real[:, 1]
    ycov_imag = bar_imag[:, 3] + smoothed * bar_imag[:, 1]
    product_im = xcov_real * jnp.swapaxes(ycov_imag, 1, 2) + xcov_imag * jnp.swapaxes(
        ycov_real, 1, 2
    )
    filled = occupied.astype(jnp.float32)
    pairing = filled[:, :, None] * (1.0 - filled[:, None, :])
    berry_sum = -2.0 / width * jnp.sum(pairing * product_im, axis=(1, 2))
    return weight * berry_sum


def on_device(base_k, counts, block_order, lattice, real_space, eigvecs, occupied):
    all_base, all_counts = (gather_directly(base_k, KA, 0), gather_directly(counts, KA, 0))
    all_order = gathered_by_axis(block_order, (("ka_0", "ka_1", "row_0"), "row_1"), (0, 1), 0)
    block_total = all_order.shape[0]
    chosen = all_order[:, None] == jnp.arange(block_total, dtype=jnp.int32)[None, :]
    block_counts = jnp.sum(jnp.where(chosen, all_counts[None, :], 0), axis=1).astype(jnp.int32)
    base_points = jnp.sum(jnp.where(chosen[:, :, None], all_base[None, :, :], 0.0), axis=1)
    kpoints, weight = slot_points(base_points, block_counts)
    slot_count = kpoints.shape[0]
    ka_size = lax.axis_size(KA)
    row_size = lax.axis_size(ROW)
    per_device = slot_count // (ka_size * row_size)
    width = real_space.shape[4]
    slot_order = (
        jnp.arange(slot_count, dtype=jnp.int32)
        .reshape(ka_size, row_size, per_device)
        .transpose(1, 0, 2)
        .reshape(slot_count)
    )
    summed = lax.psum_scatter(
        fourier(kpoints[slot_order], lattice, real_space), ROW, scatter_dimension=0, tiled=True
    )
    reduced = summed.reshape((ka_size, per_device) + summed.shape[1:])
    arrived = lax.all_to_all(reduced, KA, split_axis=0, concat_axis=3, tiled=True)
    k_field = arrived.reshape(per_device, 5, width, 2, width)
    position = lax.axis_index(KA) * row_size + lax.axis_index(ROW)
    own_weight = lax.dynamic_slice_in_dim(weight, position * per_device, per_device)
    return curvature(k_field, eigvecs, occupied, own_weight)


def solution(mesh):
    finer = Mesh(mesh.devices.reshape(4, 4, 4, 2), ("ka_0", "ka_1", "row_0", "row_1"))
    placed = (
        P(KA, None),
        P(KA),
        P(KA_ROW),
        P(ROW, None),
        P(ROW, None, KA, None, None),
        P(KA_ROW, None, None, None),
        P(KA_ROW, None),
    )
    return jax.shard_map(
        on_device, mesh=finer, in_specs=placed, out_specs=P(KA_ROW), check_vma=False
    )
```

profile of v0, /device:TPU:83, one launch (start us, length us, event | category | flops | bytes accessed | tf_op | source)
XLA Modules:
  0.0 414.7 jit_solution(16123658147926405169)
XLA Ops:
  7.8 6.8 %all-to-all-start = ((s32[16,1,8]{2,1,0:T(1,128)}), s32[16,1,8]{2,1,0:T(1,128)S(1)}, u32[]{:S(2)}, u32[]{:S(2)}) async-start(s32[16,1,8]{2,1,0:T(1,128)} %broadcast_in_dim.73), calls=%async_computation | async-start | bytes 16384 | tf_op jit(solution)/shard_map/all_to_all | solution.py:21
  14.7 7.2 %slice.203 = bf16[512,2,8,2,128]{4,3,2,1,0:T(2,128)(2,1)} slice(bf16[512,3,8,2,128]{4,3,2,1,0:T(2,128)(2,1)} %param.12), slice={[0:512], [1:3], [0:8], [0:2], [0:128]} | slice | bytes 8388608 | tf_op jit(solution)/shard_map/slice | solution.py:94
  23.9 13.2 %all-reduce = s32[64]{0:T(128)S(1)} all-reduce(s32[64]{0:T(128)S(1)} %dynamic-update-slice), channel_id=2, replica_groups=mesh['ka_0'=4,'ka_1'=4,'row_0'=4,'row_1'=2] {'ka_0','ka_1','row_0'}, use_global_device_ids=true, to_apply=%add | all-reduce | flops 64 | bytes 512
  38.6 7.9 %all-reduce.1 = s32[128]{0:T(128)S(1)} all-reduce(s32[128]{0:T(128)S(1)} %dynamic-update-slice.1), channel_id=3, replica_groups=mesh['ka_0'=4,'ka_1'=4,'row_0'=4,'row_1'=2] {'row_1'}, use_global_device_ids=true, to_apply=%add.1 | all-reduce | flops 128 | bytes 1024
  47.2 2.8 reshape_squeeze.3
  50.0 11.2 %copy.186 = bf16[512,2,8,2,128]{0,4,3,2,1:T(8,128)(2,1)} copy(bf16[512,2,8,2,128]{4,3,2,1,0:T(2,128)(2,1)} %slice.203) | data formatting | bytes 8388608 | tf_op jit(solution)/shard_map/reshape | solution.py:94
  61.8 7.8 %all-to-all-start.1 = ((f32[16,8,3]{1,2,0:T(4,128)}), f32[16,8,3]{1,2,0:T(4,128)S(1)}, u32[]{:S(2)}, u32[]{:S(2)}) async-start(f32[16,8,3]{1,2,0:T(4,128)} %broadcast_in_dim.80), calls=%async_computation.1 | async-start | bytes 65536 | tf_op jit(solution)/shard_map/all_to_all | solution.py:21
  71.4 1.4 all-to-all-done.1
  75.1 4.3 %constant_dynamic-update-slice_fusion.1 = bf16[6,512,512]{2,1,0:T(8,128)(2,1)S(1)} fusion(f32[512]{0:T(512)S(1)} %bitcast.236, f32[512]{0:T(512)S(1)} %get-tuple-element.7, f32[512]{0:T(512)S(1)} %bitcast.229, f32[512]{0:T(512)S(1)} %get-tuple-element.6, f32[512]{0:T(512)S(1)} %bitcast.221, f32[512]{0:T(512)S(1)} %get-tuple-element.5), kind=kLoop, calls=%fused_computation.115 | loop fusion | flops 1835007 | bytes 536576
  79.4 5.7 %fusion.20 = (bf16[1,512,512]{2,1,0:T(8,128)(2,1)}, bf16[1,512,512]{2,1,0:T(8,128)(2,1)}) fusion(f32[512]{0:T(512)S(1)} %bitcast.237, f32[512]{0:T(512)S(1)} %get-tuple-element.7, f32[512]{0:T(512)S(1)} %bitcast.230, f32[512]{0:T(512)S(1)} %get-tuple-element.6, f32[512]{0:T(512)S(1)} %bitcast.222, f32[512]{0:T(512)S(1)} %get-tuple-element.5), kind=kLoop, calls=%fused_computation.47 | loop fusion | flops 2097152 | bytes 1060864 | tf_op jit(solution)/shard_map/convert
  85.0 4.3 %constant_dynamic-update-slice_fusion = bf16[6,512,512]{2,1,0:T(8,128)(2,1)S(1)} fusion(bf16[6,512,512]{2,1,0:T(8,128)(2,1)S(1)} %constant_dynamic-update-slice_fusion.1, f32[512]{0:T(512)S(1)} %bitcast.238, f32[512]{0:T(512)S(1)} %get-tuple-element.7, f32[512]{0:T(512)S(1)} %bitcast.231, f32[512]{0:T(512)S(1)} %get-tuple-element.6, f32[512]{0:T(512)S(1)} %bitcast.223, ...), kind=kLoop, calls=%fused_computation.114 | loop fusion | flops 1835008 | bytes 536576
  89.4 4.3 %fusion.22 = bf16[6,512,512]{2,1,0:T(8,128)(2,1)S(1)} fusion(bf16[6,512,512]{2,1,0:T(8,128)(2,1)S(1)} %constant_dynamic-update-slice_fusion, f32[512]{0:T(512)S(1)} %neg.16, f32[512]{0:T(512)S(1)} %bitcast.239, f32[512]{0:T(512)S(1)} %get-tuple-element.7, f32[512]{0:T(512)S(1)} %bitcast.232, f32[512]{0:T(512)S(1)} %get-tuple-element.6, f32[512]{0:T(512)S(1)} %bitcast.224, ...), kind=kLoop, calls=%fused_computation.49 | loop fusion | flops 2097152 | bytes 538624
  93.7 4.3 %fusion.23 = bf16[6,512,512]{2,1,0:T(8,128)(2,1)S(1)} fusion(bf16[6,512,512]{2,1,0:T(8,128)(2,1)S(1)} %fusion.22, f32[512]{0:T(512)S(1)} %bitcast.240, f32[512]{0:T(512)S(1)} %get-tuple-element.7, f32[512]{0:T(512)S(1)} %bitcast.233, f32[512]{0:T(512)S(1)} %get-tuple-element.6, f32[512]{0:T(512)S(1)} %bitcast.225, f32[512]{0:T(512)S(1)} %get-tuple-element.5), kind=kLoop, calls=%fused_computation.50 | loop fusion | flops 2097152 | bytes 536576
  98.0 4.3 %fusion.24 = bf16[6,512,512]{2,1,0:T(8,128)(2,1)S(1)} fusion(bf16[6,512,512]{2,1,0:T(8,128)(2,1)S(1)} %fusion.23, f32[512]{0:T(512)S(1)} %neg.17, f32[512]{0:T(512)S(1)} %bitcast.241, f32[512]{0:T(512)S(1)} %get-tuple-element.7, f32[512]{0:T(512)S(1)} %bitcast.234, f32[512]{0:T(512)S(1)} %get-tuple-element.6, f32[512]{0:T(512)S(1)} %bitcast.226, ...), kind=kLoop, calls=%fused_computation.51 | loop fusion | flops 2097152 | bytes 538624
  102.4 4.3 %fusion.25 = bf16[6,512,512]{2,1,0:T(8,128)(2,1)S(1)} fusion(bf16[6,512,512]{2,1,0:T(8,128)(2,1)S(1)} %fusion.24, f32[512]{0:T(512)S(1)} %bitcast.242, f32[512]{0:T(512)S(1)} %get-tuple-element.7, f32[512]{0:T(512)S(1)} %bitcast.235, f32[512]{0:T(512)S(1)} %get-tuple-element.6, f32[512]{0:T(512)S(1)} %bitcast.227, f32[512]{0:T(512)S(1)} %get-tuple-element.5), kind=kLoop, calls=%fused_computation.52 | loop fusion | flops 2097152 | bytes 536576 | tf_op jit(solution)/shard_map/stack | solution.py:76
  106.7 11.8 %fusion.73 = f32[3072,2048]{0,1:T(8,128)} fusion(bf16[3072,512]{1,0:T(8,128)(2,1)S(1)} %bitcast.243, bf16[512,2048]{1,0:T(8,128)(2,1)S(1)} %copy-done.12), kind=kOutput, calls=%fused_computation.133 | convolution fusion | flops 6442450944 | bytes 30408704 | tf_op jit(solution)/shard_map/dot_general | solution.py:95
  118.6 16.1 %fusion.65 = (f32[512,2048]{0,1:T(8,128)}, f32[512,2048]{0,1:T(8,128)}, f32[512,2048]{0,1:T(8,128)}, f32[512,2048]{0,1:T(8,128)}, f32[512,2048]{0,1:T(8,128)S(1)}, /*index=5*/f32[512,2048]{0,1:T(8,128)}) fusion(f32[3072,2048]{0,1:T(8,128)} %fusion.73), kind=kLoop, calls=%fused_computation.125 | loop fusion | bytes 50331648 | tf_op jit(solution)/shard_map/slice | solution.py:106
  134.7 1.8 fusion.70
  136.5 2.9 copy.191
  139.4 4.8 %fusion.71 = (f32[512,8,1,128]{0,3,2,1:T(8,128)}, f32[512,8,1,128]{0,3,2,1:T(8,128)}) fusion(f32[512,8,2,128]{0,3,2,1:T(8,128)} %bitcast.215), kind=kLoop, calls=%fused_computation.131 | loop fusion | bytes 8388608 | tf_op jit(solution)/shard_map/slice | solution.py:82
  144.2 2.9 copy.192
  147.1 2.9 copy.189
  150.0 1.8 copy.190
  151.9 4.2 %fusion.68 = (f32[512,8,1,128]{0,3,2,1:T(8,128)S(1)}, f32[512,8,1,128]{0,3,2,1:T(8,128)}) fusion(f32[512,8,2,128]{0,3,2,1:T(8,128)} %bitcast.214), kind=kLoop, calls=%fused_computation.128 | loop fusion | bytes 8388608 | tf_op jit(solution)/shard_map/slice | solution.py:82
  156.1 3.0 copy.195
  159.0 4.8 %fusion.69 = (f32[512,8,1,128]{0,3,2,1:T(8,128)}, f32[512,8,1,128]{0,3,2,1:T(8,128)}) fusion(f32[512,8,2,128]{0,3,2,1:T(8,128)} %bitcast.213), kind=kLoop, calls=%fused_computation.129 | loop fusion | bytes 8388608 | tf_op jit(solution)/shard_map/slice | solution.py:82
  163.8 2.9 copy.196
  166.7 2.9 copy.193
  169.6 1.8 copy.194
  171.4 4.2 %fusion.66 = (f32[512,8,1,128]{0,3,2,1:T(8,128)S(1)}, f32[512,8,1,128]{0,3,2,1:T(8,128)}) fusion(f32[512,8,2,128]{0,3,2,1:T(8,128)} %bitcast.212), kind=kLoop, calls=%fused_computation.126 | loop fusion | bytes 8388608 | tf_op jit(solution)/shard_map/slice | solution.py:82
  175.7 2.9 copy.199
  178.6 4.8 %fusion.67 = (f32[512,8,1,128]{0,3,2,1:T(8,128)}, f32[512,8,1,128]{0,3,2,1:T(8,128)}) fusion(f32[512,8,2,128]{0,3,2,1:T(8,128)} %bitcast.211), kind=kLoop, calls=%fused_computation.127 | loop fusion | bytes 8388608 | tf_op jit(solution)/shard_map/slice | solution.py:82
  183.3 2.9 copy.200
  186.3 2.9 copy.197
  189.2 1.8 copy.198
  191.0 6.4 %fusion.5 = f32[2,512,2,8,2,128]{5,1,4,3,2,0:T(8,128)S(1)} fusion(bf16[512,2,8,2,128]{0,4,3,2,1:T(8,128)(2,1)} %copy.186, bf16[1,512,512]{2,1,0:T(8,128)(2,1)S(1)} %copy-done.14, bf16[1,512,512]{2,1,0:T(8,128)(2,1)S(1)} %copy-done.13), kind=kOutput, calls=%fused_computation.15 | convolution fusion | flops 4297064448 | bytes 22020096 | tf_op jit(solution)/shard_map/dot_general | solution.py:98
  197.4 4.8 %slice_bitcast_fusion = (f32[512,8,2,128]{3,0,2,1:T(8,128)S(1)}, f32[512,8,2,128]{3,0,2,1:T(8,128)}, f32[512,8,2,128]{3,0,2,1:T(8,128)}, f32[512,8,2,128]{3,0,2,1:T(8,128)}) fusion(f32[2,512,2,8,2,128]{5,1,4,3,2,0:T(8,128)S(1)} %fusion.5), kind=kLoop, calls=%fused_computation.1 | loop fusion | bytes 33554432 | tf_op jit(solution)/shard_map/squeeze | solution.py:108
  202.3 2.6 add.198
  206.0 2.4 fusion
  216.6 2.3 fusion.1
  218.8 2.3 fusion.2
  221.1 8.4 %slice_subtract_fusion = (f32[512,8,1,128]{3,0,2,1:T(8,128)}, f32[512,8,1,128]{3,0,2,1:T(8,128)}, f32[512,8,1,128]{3,0,2,1:T(8,128)}, f32[512,8,1,128]{3,0,2,1:T(8,128)}) fusion(f32[512,8,2,128]{3,0,2,1:T(8,128)S(1)} %get-tuple-element.14, f32[512,8,2,128]{3,0,2,1:T(8,128)} %get-tuple-element.15, f32[512,8,2,128]{3,0,2,1:T(8,128)} %get-tuple-element.17, ...), kind=kLoop, calls=%fused_computation.19 | loop fusion | flops 2097152 | bytes 25165824 | tf_op jit(solution)/shard_map/sub | solution.py:82
  229.4 4.7 %fusion.3 = f32[512,5,8,2,128]{4,0,3,2,1:T(8,128)} fusion(f32[512,5,8,2,128]{4,0,3,2,1:T(8,128)} %fusion.2, f32[512,8,1,128]{3,0,2,1:T(8,128)} %get-tuple-element.45, f32[512,8,1,128]{3,0,2,1:T(8,128)} %get-tuple-element.46), kind=kLoop, calls=%fused_computation.12 | loop fusion | flops 1048576 | bytes 8388608
  234.2 2.2 fusion.4
  236.4 111.7 %reduce-scatter.2.cloned.1.call-done = f32[64,5,8,2,128]{4,0,3,2,1:T(8,128)} async-done(((f32[512,5,8,2,128]{4,0,3,2,1:T(8,128)}), f32[64,5,8,2,128]{4,0,3,2,1:T(8,128)}) %reduce-scatter.2.cloned.1.call-update) | async-done | bytes 2621456 | tf_op jit(solution)/shard_map/reduce_scatter | solution.py:168
  348.1 4.0 copy.155
  352.1 6.8 %all-to-all-start.2 = ((f32[16,4,5,8,2,128]{5,1,4,3,2,0:T(4,128)}), f32[16,4,5,8,2,128]{5,1,4,3,2,0:T(4,128)S(1)}, u32[]{:S(2)}, u32[]{:S(2)}) async-start(f32[16,4,5,8,2,128]{5,1,4,3,2,0:T(4,128)} %copy.155), calls=%async_computation.3 | async-start | bytes 5242880 | tf_op jit(solution)/shard_map/all_to_all | solution.py:172
  360.2 37.9 %all-to-all-done.2 = f32[16,4,5,8,2,128]{5,1,4,3,2,0:T(4,128)S(1)} async-done(((f32[16,4,5,8,2,128]{5,1,4,3,2,0:T(4,128)}), f32[16,4,5,8,2,128]{5,1,4,3,2,0:T(4,128)S(1)}, u32[]{:S(2)}, u32[]{:S(2)}) %all-to-all-start.2) | async-done | bytes 2621472 | tf_op jit(solution)/shard_map/all_to_all | solution.py:172
  (113 shorter events, 28.4 us)
Async XLA Ops:
  7.8 53.4 %all-to-all-start = ((s32[16,1,8]{2,1,0:T(1,128)}), s32[16,1,8]{2,1,0:T(1,128)S(1)}, u32[]{:S(2)}, u32[]{:S(2)}) async-start(s32[16,1,8]{2,1,0:T(1,128)} %broadcast_in_dim.73), calls=%async_computation | async-start | bytes 16384 | tf_op jit(solution)/shard_map/all_to_all | solution.py:21
  14.6 7.2 %copy-start.15 = (s32[512,3]{0,1:T(4,128)S(1)}, s32[512,3]{0,1:T(4,128)}, u32[]{:S(2)}) copy-start(s32[512,3]{0,1:T(4,128)} %param.11) | copy-start | bytes 18436
  14.7 7.9 %copy-start.20 = (u32[128]{0:T(128)S(1)}, u32[128]{0:T(128)}, u32[]{:S(2)}) copy-start(u32[128]{0:T(128)} %constant.56) | copy-start | bytes 1540
  14.7 22.5 %copy-start.19 = (u32[128]{0:T(128)S(1)}, u32[128]{0:T(128)}, u32[]{:S(2)}) copy-start(u32[128]{0:T(128)} %constant.61) | copy-start | bytes 1540
  14.7 32.5 %slice-start = ((bf16[512,3,8,2,128]{4,3,2,1,0:T(2,128)(2,1)}), bf16[512,1,8,2,128]{4,3,2,1,0:T(2,128)(2,1)S(1)}, s32[]{:S(2)}) async-start(bf16[512,3,8,2,128]{4,3,2,1,0:T(2,128)(2,1)} %param.12), calls=%async_computation.5 | async-start | bytes 4194304 | tf_op jit(solution)/shard_map/slice | solution.py:93
  50.0 11.2 %copy-start.17 = (f32[8,3]{0,1:T(4,128)S(1)}, f32[8,3]{0,1:T(4,128)}, u32[]{:S(2)}) copy-start(f32[8,3]{0,1:T(4,128)} %param.8) | copy-start | bytes 292
  50.0 23.2 %copy-start.18 = (f32[3]{0:T(128)S(1)}, f32[3]{0:T(128)}, u32[]{:S(2)}) copy-start(f32[3]{0:T(128)} %constant.47.clone) | copy-start | bytes 40
  61.8 11.0 %all-to-all-start.1 = ((f32[16,8,3]{1,2,0:T(4,128)}), f32[16,8,3]{1,2,0:T(4,128)S(1)}, u32[]{:S(2)}, u32[]{:S(2)}) async-start(f32[16,8,3]{1,2,0:T(4,128)} %broadcast_in_dim.80), calls=%async_computation.1 | async-start | bytes 65536 | tf_op jit(solution)/shard_map/all_to_all | solution.py:21
  69.7 278.5 %reduce-scatter.2.cloned.1.call-start = ((), (), s32[]{:S(2)}) async-start(), calls=%async_computation.4 | async-start | bytes 23592960 | tf_op jit(solution)/shard_map/reduce_scatter | solution.py:168
  75.0 31.7 %copy-start.12 = (bf16[512,2048]{1,0:T(8,128)(2,1)S(1)}, bf16[512,2048]{1,0:T(8,128)(2,1)}, u32[]{:S(2)}) copy-start(bf16[512,2048]{1,0:T(8,128)(2,1)} %reshape_squeeze.3) | copy-start | bytes 6291460
  189.2 1.8 copy-start.13
  189.2 1.8 copy-start.14
  202.2 2.9 copy-start
  202.2 3.5 copy-start.1
  205.9 2.4 copy-start.2
  206.0 3.7 copy-start.3
  209.7 1.6 copy-start.4
  209.7 2.2 copy-start.5
  211.9 1.6 copy-start.6
  211.9 2.2 copy-start.7
  214.1 1.6 copy-start.8
  214.1 2.2 copy-start.9
  229.4 4.7 %copy-start.10 = (f32[512,8,1,128]{3,0,2,1:T(8,128)S(1)}, f32[512,8,1,128]{3,0,2,1:T(8,128)}, u32[]{:S(2)}) copy-start(f32[512,8,1,128]{3,0,2,1:T(8,128)} %get-tuple-element.18) | copy-start | bytes 6291460
  229.4 4.7 %copy-start.11 = (f32[512,8,1,128]{3,0,2,1:T(8,128)S(1)}, f32[512,8,1,128]{3,0,2,1:T(8,128)}, u32[]{:S(2)}) copy-start(f32[512,8,1,128]{3,0,2,1:T(8,128)} %get-tuple-element.19) | copy-start | bytes 6291460
  352.1 6.8 %copy-start.16 = (s32[4,128]{1,0:T(4,128)S(1)}, s32[4,128]{1,0:T(4,128)}, u32[]{:S(2)}) copy-start(s32[4,128]{1,0:T(4,128)} %param.14) | copy-start | bytes 6148
  352.1 46.0 %all-to-all-start.2 = ((f32[16,4,5,8,2,128]{5,1,4,3,2,0:T(4,128)}), f32[16,4,5,8,2,128]{5,1,4,3,2,0:T(4,128)S(1)}, u32[]{:S(2)}, u32[]{:S(2)}) async-start(f32[16,4,5,8,2,128]{5,1,4,3,2,0:T(4,128)} %copy.155), calls=%async_computation.3 | async-start | bytes 5242880 | tf_op jit(solution)/shard_map/all_to_all | solution.py:172
Sparse Core Ops, SparseCore 0:
  236.5 111.5 reduce-scatter.1
where the time goes:
time: 420 us; the launch traced here: 415 us
  waiting for transfers between devices  151 us (36%)
  local copies, waits for them, and re-layouts  119 us (28%)
  other arithmetic  61 us (15%)
  matrix products  25.3 us (6%)
  starting transfers between devices  21.5 us (5%)
  blocking collectives  21.1 us (5%)
  between operations  15.7 us (4%)
    reduce_scatter x1, waiting for transfers between devices, on_device(): lax.psum_scatter(fourier(kpoints[slot_order], lattice, real_space), ROW,...  112 us
    unnamed x60, local copies, waits for them, and re-layouts  42.1 us
    all_to_all x1, waiting for transfers between devices, on_device(): lax.all_to_all(reduced, KA, split_axis=0, concat_axis=3, tiled=True)  37.9 us
    unnamed x9, other arithmetic  33.3 us
    slice x6, local copies, waits for them, and re-layouts, combine(): real_part = first_part[..., 0, :] - second_part[..., 1, :]  24.6 us
    unnamed x2, blocking collectives  21.1 us
    slice x1, local copies, waits for them, and re-layouts, fourier(): product_h[4]  16.1 us
    all_to_all x2, starting transfers between devices, sent_to_all(): return lax.all_to_all(copies, axis, split_axis=0, concat_axis=0, tiled=True)  14.7 us
  transfers between devices with their start and end apart: 4, of which 3 were waited for; matrix products, arithmetic and copies ran while one was open for 6% of the time, Pallas kernels for 0%

commit v1 on v0

v1 whole, which is shorter than its diff:
```python
import math

import jax
import jax.numpy as jnp
from jax import lax
from jax.experimental import pallas as pl
from jax.experimental.pallas import tpu as pltpu
from jax.sharding import Mesh
from jax.sharding import PartitionSpec as P

SUB = 4
KA = ("ka_0", "ka_1")
KA_ROW = ("ka_0", "ka_1", "row_0", "row_1")
ROW = ("row_0", "row_1")
PLANE = ("ka_0", "ka_1", "row_1")
INTERPRET = False

broadening = 1.0
refine_step = (0.05, 0.03, 0.02)

f32 = jnp.float32
bf16 = jnp.bfloat16
VMEM = pl.BlockSpec(memory_space=pltpu.VMEM)
SMEM = pl.BlockSpec(memory_space=pltpu.SMEM)
NX = 4
OWNERS = 32
BLOCKS = 128


def params(**more):
    return pltpu.CompilerParams(vmem_limit_bytes=56 << 20, **more)


def iota(shape, dim):
    return lax.broadcasted_iota(jnp.int32, shape, dim)


def place_of(position):
    plane = (position % 8) // 2
    owner = (position // 8) * 2 + position % 2
    return plane, owner


def index_kernel(place_ref, table_ref, points_ref, slots_ref, weight_ref):
    my_plane = place_ref[0]
    table = table_ref[...]
    turned = table.T
    square = (BLOCKS, BLOCKS)
    order_down = table[:, 4:5].astype(jnp.int32)
    order_along = turned[4:5, :].astype(jnp.int32)
    here_down = order_down == iota(square, 1)
    here_along = iota(square, 0) == order_along

    def along(column):
        return jnp.sum(jnp.where(here_along, table[:, column : column + 1], 0.0), axis=0, keepdims=True)

    base = [along(axis) for axis in range(3)]
    count = along(3)
    count_down = jnp.sum(jnp.where(here_down, turned[3:4, :], 0.0), axis=1, keepdims=True)

    plane_down, owner_down = place_of(iota(square, 0))
    plane_along, owner_along = place_of(iota(square, 1))
    mates = plane_down == plane_along
    ahead = mates & (owner_down < owner_along)
    plane_row, owner_row = place_of(iota((1, BLOCKS), 1))
    away = (plane_row - my_plane + NX) % NX

    rows = OWNERS * NX
    entry = iota((3 * rows, BLOCKS), 0)
    dense_entry = iota((rows, BLOCKS), 0)
    lane = iota((4 * rows, BLOCKS), 1)
    gathered = [jnp.zeros((3 * rows, BLOCKS), f32) for _ in range(3)]
    dense = []
    before = jnp.zeros((1, BLOCKS), f32)
    slots_ref[...] = jnp.zeros((8, BLOCKS), jnp.int32)
    weight_ref[...] = jnp.zeros((8, BLOCKS), f32)
    for s in range(SUB):
        fraction = (s + 0.5) / count - 0.5
        points = [base[axis] + fraction * refine_step[axis] for axis in range(3)]
        alive = count > s
        weight_ref[s : s + 1, :] = jnp.where(alive, 1.0 / count, 0.0)
        if s == 0:
            match = dense_entry == away * OWNERS + owner_row
            for axis in range(3):
                dense.append(jnp.where(match, points[axis], 0.0))
            continue
        live_down = count_down > s
        rank = before + jnp.sum(jnp.where(ahead & live_down, 1.0, 0.0), axis=0, keepdims=True)
        before = before + jnp.sum(jnp.where(mates & live_down, 1.0, 0.0), axis=0, keepdims=True)
        rank = rank.astype(jnp.int32)
        target = (rank // OWNERS) * rows + away * OWNERS + rank % OWNERS
        match = entry == jnp.where(alive, target, -1)
        for axis in range(3):
            gathered[axis] = gathered[axis] + jnp.where(match, points[axis], 0.0)
        slots_ref[s : s + 1, :] = jnp.where(alive, rank, 0)
    most = jnp.max(before, axis=1, keepdims=True)
    slots_ref[0:1, :] = jnp.broadcast_to(most, (1, BLOCKS)).astype(jnp.int32)
    points = jnp.zeros((4 * rows, BLOCKS), f32)
    for axis in range(3):
        column = jnp.concatenate([gathered[axis], dense[axis]], axis=0)
        points = jnp.where(lane == axis, jnp.sum(column, axis=1, keepdims=True), points)
    points_ref[...] = points


def find_points(table, plane):
    rows = OWNERS * NX
    return pl.pallas_call(
        index_kernel,
        out_shape=(
            jax.ShapeDtypeStruct((4 * rows, BLOCKS), f32),
            jax.ShapeDtypeStruct((8, BLOCKS), jnp.int32),
            jax.ShapeDtypeStruct((8, BLOCKS), f32),
        ),
        in_specs=[SMEM, VMEM],
        out_specs=(VMEM, VMEM, VMEM),
        compiler_params=params(),
        interpret=INTERPRET,
        name="find_points",
    )(plane, table)


def split_kernel(core_ref, space_ref, own_ref, send_ref, wide_ref):
    core = core_ref[0]
    depth, rows, width = space_ref.shape
    half = rows // 12
    wide_ref[...] = space_ref[...].astype(f32).reshape(depth * rows, width)
    for matrix in range(3):
        for part in range(2):
            for r in range(half):
                lanes = slice(r * width, (r + 1) * width)
                own_at = matrix * (rows // 3) + 2 * (half * core + r) + part
                send_at = matrix * (rows // 3) + 2 * (half * (1 - core) + r) + part
                own = wide_ref[pl.ds(own_at, depth, stride=rows), :]
                own_ref[matrix, part, :, lanes] = own.astype(bf16)
                send_ref[matrix, part, :, lanes] = wide_ref[pl.ds(send_at, depth, stride=rows), :]


def split_rows(space, core):
    depth, rows, width = space.shape
    block = min(depth, 128)
    lanes = rows // 12 * width
    shape = (3, 2, depth, lanes)
    spec = pl.BlockSpec((3, 2, block, lanes), lambda i: (0, 0, i, 0))
    return pl.pallas_call(
        split_kernel,
        grid=(depth // block,),
        out_shape=(jax.ShapeDtypeStruct(shape, bf16), jax.ShapeDtypeStruct(shape, f32)),
        in_specs=[SMEM, pl.BlockSpec((block, rows, width), lambda i: (i, 0, 0))],
        out_specs=(spec, spec),
        scratch_shapes=[pltpu.VMEM((block * rows, width), f32)],
        compiler_params=params(),
        interpret=INTERPRET,
        name="split_rows",
    )(core, space)


def narrow_kernel(wide_ref, narrow_ref):
    narrow_ref[...] = wide_ref[...].astype(bf16)


def narrow(wide):
    matrices, depth, lanes = wide.shape
    spec = pl.BlockSpec((1, depth, lanes), lambda i: (i, 0, 0))
    return pl.pallas_call(
        narrow_kernel,
        grid=(matrices,),
        out_shape=jax.ShapeDtypeStruct(wide.shape, bf16),
        in_specs=[spec],
        out_specs=spec,
        compiler_params=params(),
        interpret=INTERPRET,
        name="narrow",
    )(wide)


def turn(points, coords):
    turns = points[:, 0:1] * coords[0:1, :] + points[:, 1:2] * coords[1:2, :] + points[:, 2:3] * coords[2:3, :]
    rest = turns - jnp.floor(turns + 0.5)
    quarter = jnp.floor(4.0 * rest + 0.5)
    angle = (rest - 0.25 * quarter) * (2.0 * math.pi)
    square = angle * angle
    sine = angle * (1.0 + square * (-1.0 / 6 + square * (1.0 / 120 + square * (-1.0 / 5040 + square * (1.0 / 362880)))))
    cosine = 1.0 + square * (-0.5 + square * (1.0 / 24 + square * (-1.0 / 720 + square * (1.0 / 40320 - square / 3628800))))
    odd = jnp.abs(quarter) == 1.0
    first = jnp.where(odd, sine, cosine)
    second = jnp.where(odd, cosine, sine)
    cos_sign = jnp.where((quarter == 1.0) | (jnp.abs(quarter) == 2.0), -1.0, 1.0)
    sin_sign = jnp.where((quarter == -1.0) | (jnp.abs(quarter) == 2.0), -1.0, 1.0)
    return first * cos_sign, second * sin_sign


def fourier_kernel(points_ref, coords_ref, own_ref, other_ref, keep_ref, right_ref, near_ref, far_ref, left_ref, phase_ref):
    step = pl.program_id(0)
    count = points_ref.shape[0]
    depth = coords_ref.shape[1] // 2
    owners = count // NX

    @pl.when(step == 0)
    def _():
        points = points_ref[...]
        for source in range(2):
            coords = coords_ref[:, source * depth : (source + 1) * depth]
            cosine, sine = turn(points, coords)
            at_real = slice(source * 2 * depth, source * 2 * depth + depth)
            at_imag = slice(source * 2 * depth + depth, source * 2 * depth + 2 * depth)
            pairs = [(cosine, sine)]
            for axis in range(2):
                coord = coords[axis : axis + 1, :]
                pairs.append((-coord * sine, coord * cosine))
            for kind, (real, imag) in enumerate(pairs):
                phase_ref[(2 * kind) * count : (2 * kind + 1) * count, at_real] = real.astype(bf16)
                phase_ref[(2 * kind) * count : (2 * kind + 1) * count, at_imag] = (-imag).astype(bf16)
                phase_ref[(2 * kind + 1) * count : (2 * kind + 2) * count, at_real] = imag.astype(bf16)
                phase_ref[(2 * kind + 1) * count : (2 * kind + 2) * count, at_imag] = real.astype(bf16)

    def store(product, kinds, first_kind, first_row):
        width = product.shape[1] // 2
        for kind in range(kinds):
            for half in range(2):
                block = product[kind * count : (kind + 1) * count, half * width : (half + 1) * width]
                at = (first_kind + kind) * 4 + first_row + half
                start = 0
                for ref in (keep_ref, right_ref, near_ref, far_ref, left_ref):
                    size = ref.shape[0] // 40
                    ref[pl.ds(at, size, stride=40), :] = block[start : start + size]
                    start += size

    def product(kinds):
        rows = slice(0, kinds * count)
        return jnp.dot(phase_ref[rows, : 2 * depth], own_ref[0], preferred_element_type=f32) + jnp.dot(
            phase_ref[rows, 2 * depth :], other_ref[0], preferred_element_type=f32
        )

    @pl.when(step < 2)
    def _():
        store(product(6), 6, 0, 2 * step)

    @pl.when(step >= 2)
    def _():
        store(product(2), 2, 6 + 2 * (step // 2 - 1), 2 * (step % 2))


def fourier(points, coords, own, other):
    count = points.shape[0]
    depth2 = own.shape[1]
    width = own.shape[2] // 4
    owners = count // NX
    spec = pl.BlockSpec((1, depth2, 2 * width), lambda j: (j // 2, 0, j % 2))
    sizes = (owners, owners, owners // 2, owners // 2, owners)
    shapes = tuple(jax.ShapeDtypeStruct((size * 40, width), f32) for size in sizes)
    outs = pl.pallas_call(
        fourier_kernel,
        grid=(6,),
        out_shape=shapes,
        in_specs=[
            pl.BlockSpec(points.shape, lambda j: (0, 0)),
            pl.BlockSpec(coords.shape, lambda j: (0, 0)),
            spec,
            spec,
        ],
        out_specs=tuple(pl.BlockSpec(shape.shape, lambda j: (0, 0)) for shape in shapes),
        scratch_shapes=[pltpu.VMEM((6 * count, 2 * depth2), bf16)],
        compiler_params=params(),
        interpret=INTERPRET,
        name="fourier",
    )(points, coords, own, other)
    return tuple(out.reshape(-1, 40, width) for out in outs)


def to_right(value):
    return lax.ppermute(value, "row_0", [(i, (i + 1) % NX) for i in range(NX)])


def to_left(value):
    return lax.ppermute(value, "row_0", [(i, (i - 1) % NX) for i in range(NX)])


def first_hop(parts):
    keep, right, near, far, left = parts
    return to_right(near), to_left(far)


def second_hop(parts, arrived):
    keep, right, near, far, left = parts
    half = near.shape[0]
    right = jnp.concatenate([right[:half] + arrived[0], right[half:]], axis=0)
    left = jnp.concatenate([left[:half], left[half:] + arrived[1]], axis=0)
    return keep, to_right(right), to_left(left)


def place_kernel(units, place_ref, slots_ref, *refs):
    ins, outs = refs[:-1], refs[-1]
    plane = place_ref[0]
    tables = [ins[i] for i in range(len(ins))]

    def body(owner, carry):
        position = (owner // 2) * 8 + 2 * plane + owner % 2
        for u, s in enumerate(units):
            at = slots_ref[s, position]
            outs[owner, u] = tables[0][at]
        return carry

    lax.fori_loop(0, OWNERS, body, 0)


def place_slots(units, plane, slots, table):
    width = table.shape[-1]
    return pl.pallas_call(
        lambda *refs: place_kernel(units, *refs),
        out_shape=jax.ShapeDtypeStruct((OWNERS, len(units), 40, width), f32),
        in_specs=[SMEM, SMEM, VMEM],
        out_specs=VMEM,
        compiler_params=params(),
        interpret=INTERPRET,
        name="place_slots",
    )(plane, slots, table)


def to_owners(value):
    return lax.all_to_all(value, PLANE, split_axis=0, concat_axis=0, tiled=True)


def two_terms(value):
    high = value.astype(bf16)
    return high, (value - high.astype(f32)).astype(bf16)


def curvature_kernel(units, weight_ref, field_ref, turn_ref, back_ref, occupied_ref, out_ref):
    sources = field_ref.shape[0] // (len(units) * 40)
    width = field_ref.shape[1]
    lane = iota((1, BLOCKS), 1)
    total = jnp.zeros((1, BLOCKS), f32)
    for u, s in enumerate(units):
        stride = len(units) * 40

        def plane_of(kind):
            return jnp.concatenate(
                [field_ref[pl.ds(u * 40 + kind * 4 + r, sources, stride=stride), :] for r in range(4)], axis=0
            )

        matrices = jnp.concatenate(
            [jnp.concatenate([plane_of(2 * c), plane_of(2 * c + 1)], axis=1) for c in range(5)], axis=0
        )
        high, low = two_terms(matrices)
        vectors = turn_ref[s]
        rotated = jnp.dot(high, vectors, preferred_element_type=f32) + jnp.dot(
            low, vectors, preferred_element_type=f32
        )
        n = width
        back = back_ref[s]
        adjoint = back[:n, :].astype(f32)
        vec_real = adjoint[:, :n].T
        vec_imag = adjoint[:, n:].T
        energy = jnp.sum(vec_real * rotated[:n, :n] + vec_imag * rotated[:n, n:], axis=0, keepdims=True)
        stacked = jnp.concatenate(
            [
                jnp.concatenate([rotated[(c + 1) * n : (c + 2) * n, :n] for c in range(4)], axis=1),
                jnp.concatenate([rotated[(c + 1) * n : (c + 2) * n, n:] for c in range(4)], axis=1),
            ],
            axis=0,
        )
        high, low = two_terms(stacked)
        bar = jnp.dot(back, high, preferred_element_type=f32) + jnp.dot(back, low, preferred_element_type=f32)
        bar_real, bar_imag = bar[:n], bar[n:]
        across = jnp.broadcast_to(energy, (n, n))
        spacing = across - across.T
        smoothed = spacing / (spacing * spacing + broadening)

        def pick(value, c):
            return value[:, c * n : (c + 1) * n]

        xcov_real = pick(bar_real, 2) + smoothed * pick(bar_real, 0)
        xcov_imag = pick(bar_imag, 2) + smoothed * pick(bar_imag, 0)
        ycov_real = pick(bar_real, 3) + smoothed * pick(bar_real, 1)
        ycov_imag = pick(bar_imag, 3) + smoothed * pick(bar_imag, 1)
        filled = occupied_ref[s : s + 1, :].astype(f32)
        filled_down = jnp.broadcast_to(filled, (n, n)).T
        pairing = filled_down * (1.0 - filled)
        product = pairing * (xcov_real * ycov_imag.T + xcov_imag * ycov_real.T)
        berry = jnp.sum(jnp.sum(product, axis=0, keepdims=True), axis=1, keepdims=True) * (-2.0 / n)
        weight = weight_ref[s]
        total = jnp.where((lane == s) & (weight > 0.0), weight * berry, total)
    out_ref[...] = total


def curvature(units, weight, arrived, vectors, adjoint, occupied):
    width = arrived.shape[-1]
    return pl.pallas_call(
        lambda *refs: curvature_kernel(units, *refs),
        out_shape=jax.ShapeDtypeStruct((1, BLOCKS), f32),
        in_specs=[SMEM, VMEM, VMEM, VMEM, VMEM],
        out_specs=VMEM,
        compiler_params=params(),
        interpret=INTERPRET,
        name="curvature",
    )(weight, arrived.reshape(-1, width), vectors, adjoint, occupied)


def vector_matrices(eigvecs):
    slots, width = eigvecs.shape[0], eigvecs.shape[1]
    real, imag = eigvecs[:, :, 0, :], eigvecs[:, :, 1, :]
    turning = jnp.concatenate(
        [jnp.concatenate([real, imag], axis=2), jnp.concatenate([-imag, real], axis=2)], axis=1
    )

    def adjoint(value):
        return value.reshape(slots, OWNERS, width // OWNERS, width).transpose(0, 3, 2, 1).reshape(slots, width, width)

    real, imag = adjoint(real), adjoint(imag)
    back = jnp.concatenate(
        [jnp.concatenate([real, imag], axis=2), jnp.concatenate([-imag, real], axis=2)], axis=1
    )
    return turning, back


def on_device(base_k, counts, block_order, lattice, real_space, eigvecs, occupied):
    plane, core = lax.axis_index("row_0"), lax.axis_index("row_1")
    row = plane * 2 + core
    plane_ref = plane.reshape(1).astype(jnp.int32)
    core_ref = core.reshape(1).astype(jnp.int32)
    depth, _, slab, _, width = real_space.shape

    own_base = lax.dynamic_slice_in_dim(base_k, row, 1, 0)
    own_count = lax.dynamic_slice_in_dim(counts, row, 1, 0).astype(f32)[:, None]
    mine = jnp.concatenate([own_base, own_count, block_order.astype(f32)[:, None]], axis=1)
    mine = jnp.pad(mine, ((0, 0), (0, BLOCKS - 5)))
    line = lax.all_to_all(jnp.broadcast_to(mine[None], (8, 1, BLOCKS)), ROW, 0, 0, tiled=True)

    own, send = split_rows(real_space.reshape(depth, 6 * slab, width), core_ref)
    swap = [(0, 1), (1, 0)]
    other = lax.ppermute(send, "row_1", swap)
    own_coords = jnp.pad(lattice.T.astype(f32), ((0, 5), (0, 0)))
    coords = jnp.concatenate([own_coords, lax.ppermute(own_coords, "row_1", swap)], axis=1)

    lines = jnp.broadcast_to(line.reshape(1, 8, BLOCKS), (16, 8, BLOCKS))
    table = lax.all_to_all(lines, KA, 0, 0, tiled=True).reshape(BLOCKS, BLOCKS)
    points, slots, weights = find_points(table, plane_ref)
    position = (lax.axis_index(KA) * 8 + row).astype(jnp.int32)
    weight = lax.dynamic_slice(weights, (jnp.int32(0), position), (SUB, 1)).reshape(SUB)

    own = own.reshape(3, 2 * depth, -1)
    other = narrow(other.reshape(3, 2 * depth, -1))
    rows = OWNERS * NX

    def chunk(i):
        return fourier(points[i * rows : (i + 1) * rows], coords, own, other)

    turning, back = vector_matrices(eigvecs)

    parts0 = chunk(0)
    hop0 = first_hop(parts0)
    parts1 = chunk(1)
    hop1 = first_hop(parts1)
    sum0 = sum(second_hop(parts0, hop0))
    parts3 = chunk(3)
    hop3 = first_hop(parts3)
    sum1 = sum(second_hop(parts1, hop1))
    sum3 = sum(second_hop(parts3, hop3))

    def further(_):
        parts = chunk(2)
        return sum(second_hop(parts, first_hop(parts)))

    extra = lax.cond(slots[0, 0] > 2 * OWNERS, further, lambda _: jnp.zeros(sum0.shape, f32), 0)

    unit1 = to_owners(place_slots((1,), plane_ref, slots, sum0))
    unit23 = to_owners(place_slots((2, 3), plane_ref, slots, jnp.concatenate([sum0, sum1, extra], axis=0)))
    unit0 = to_owners(sum3)
    curve = (
        curvature((1,), weight, unit1, turning, back, occupied)
        + curvature((2, 3), weight, unit23, turning, back, occupied)
        + curvature((0,), weight, unit0, turning, back, occupied)
    )
    return curve[0, :SUB]


def solution(mesh):
    finer = Mesh(mesh.devices.reshape(4, 4, 4, 2), ("ka_0", "ka_1", "row_0", "row_1"))
    placed = (
        P(KA, None),
        P(KA),
        P(KA_ROW),
        P(ROW, None),
        P(ROW, None, KA, None, None),
        P(KA_ROW, None, None, None),
        P(KA_ROW, None),
    )
    return jax.shard_map(
        on_device, mesh=finer, in_specs=placed, out_specs=P(KA_ROW), check_vma=False
    )
```

time: 420 us -> 174 us (0.41)
  the two profiles are of different devices: /device:TPU:83 before, /device:TPU:7 now
where the time goes in v1:
time: 174 us; the launch traced here: 173 us
  Pallas kernels  56.4 us (32%)
  starting transfers between devices  41.6 us (24%)
  waiting for transfers between devices  36.6 us (21%)
  other arithmetic  18.2 us (10%)
  local copies, waits for them, and re-layouts  9.52 us (5%)
  blocking collectives  7.85 us (5%)
  between operations  2.29 us (1%)
    pallas_call x3, Pallas kernels, fourier(): pl.pallas_call(fourier_kernel, grid=(6,), out_shape=shapes, in_specs=[pl....  25.4 us
    all_to_all x3, starting transfers between devices, to_owners(): return lax.all_to_all(value, PLANE, split_axis=0, concat_axis=0, tiled=True)  22.3 us
    all_to_all x3, waiting for transfers between devices, to_owners(): return lax.all_to_all(value, PLANE, split_axis=0, concat_axis=0, tiled=True)  17.1 us
    pallas_call x1, Pallas kernels, split_rows(): pl.pallas_call(split_kernel, grid=(depth // block,), out_shape=(jax.Shape...  9.81 us
    pallas_call x3, Pallas kernels, curvature(): pl.pallas_call(lambda *refs: curvature_kernel(units, *refs), out_shape=ja...  9.7 us
    ppermute x6, starting transfers between devices, to_right(): return lax.ppermute(value, 'row_0', [(i, (i + 1) % NX) for i in range(NX)])  8.03 us
    all_to_all x1, blocking collectives, on_device(): lax.all_to_all(jnp.broadcast_to(mine[None], (8, 1, BLOCKS)), ROW, 0, 0, t...  7.85 us
    all_to_all x1, starting transfers between devices, on_device(): table = lax.all_to_all(lines, KA, 0, 0, tiled=True).reshape(BLOCKS, BLOCKS)  7.77 us
  transfers between devices with their start and end apart: 18, of which 9 were waited for; matrix products, arithmetic and copies ran while one was open for 14% of the time, Pallas kernels for 18%

profile of v1, /device:TPU:7, one launch (start us, length us, event | category | flops | bytes accessed | tf_op | source)
XLA Modules:
  0.0 172.5 jit_solution(12662925969683565847)
XLA Ops:
  0.0 9.8 %split_rows.1 = (bf16[3,2,512,512]{3,2,1,0:T(8,128)(2,1)}, f32[3,2,512,512]{3,2,1,0:T(8,128)}) custom-call(s32[1]{0:T(128)} %bitcast.13.core_ref, bf16[512,48,128]{2,1,0:T(8,128)(2,1)} %bitcast.62), custom_call_target="tpu_custom_call" | custom-call | tf_op jit(solution)/shard_map/split_rows/pallas_call | solution.py:144
  12.8 7.9 %all_to_all.25 = f32[8,1,128]{2,1,0:T(1,128)S(1)} all-to-all(f32[8,1,128]{2,1,0:T(1,128)S(1)} %broadcast_in_dim.24), channel_id=1, replica_groups=mesh['ka_0'=4,'ka_1'=4,'row_0'=4,'row_1'=2] {'row_0','row_1'}, dimensions={0} | all-to-all | bytes 8192 | tf_op jit(solution)/shard_map/all_to_all | solution.py:427
  21.3 7.8 %all-to-all-start.1 = ((f32[16,8,128]{2,1,0:T(8,128)}), f32[16,8,128]{2,1,0:T(8,128)S(1)}, u32[]{:S(2)}, u32[]{:S(2)}) async-start(f32[16,8,128]{2,1,0:T(8,128)} %broadcast_in_dim.26), calls=%async_computation.1 | async-start | bytes 131072 | tf_op jit(solution)/shard_map/all_to_all | solution.py:436
  29.1 6.5 %all-to-all-done.1 = f32[16,8,128]{2,1,0:T(8,128)S(1)} async-done(((f32[16,8,128]{2,1,0:T(8,128)}), f32[16,8,128]{2,1,0:T(8,128)S(1)}, u32[]{:S(2)}, u32[]{:S(2)}) %all-to-all-start.1) | async-done | bytes 65568 | tf_op jit(solution)/shard_map/all_to_all | solution.py:436
  36.2 1.9 %find_points.1 = (f32[512,128]{1,0:T(8,128)S(1)}, s32[8,128]{1,0:T(8,128)}, f32[8,128]{1,0:T(8,128)}) custom-call(s32[1]{0:T(128)} %bitcast.7.place_ref.refs_0_, f32[128,128]{1,0:T(8,128)} %bitcast.90), custom_call_target="tpu_custom_call" | custom-call | tf_op jit(solution)/shard_map/find_points/pallas_call | solution.py:107
  38.1 0.7 fusion.9
  38.9 3.8 %narrow.1.other_ref = bf16[3,1024,512]{2,1,0:T(8,128)(2,1)S(1)} custom-call(f32[3,1024,512]{2,1,0:T(8,128)} %bitcast.16.wide_ref), custom_call_target="tpu_custom_call" | custom-call | tf_op jit(solution)/shard_map/narrow/pallas_call | solution.py:164
  42.6 8.5 %fourier.5 = (f32[1280,128]{1,0:T(8,128)}, f32[1280,128]{1,0:T(8,128)}, f32[640,128]{1,0:T(8,128)}, f32[640,128]{1,0:T(8,128)}, f32[1280,128]{1,0:T(8,128)}) custom-call(f32[128,128]{1,0:T(8,128)} %get-tuple-element.87.points_ref, f32[8,1024]{1,0:T(8,128)S(1)} %pad_maximum_fusion.9.coords_ref, bf16[3,1024,512]{2,1,0:T(8,128)(2,1)S(1)} %bitcast.59, ...), custom_call_target="tpu_custom_call" | custom-call | tf_op jit(solution)/shard_map/fourier/pallas_call | solution.py:251
  51.1 1.5 collective-permute-start.6
  52.6 8.4 %fourier.6 = (f32[1280,128]{1,0:T(8,128)}, f32[1280,128]{1,0:T(8,128)}, f32[640,128]{1,0:T(8,128)}, f32[640,128]{1,0:T(8,128)}, f32[1280,128]{1,0:T(8,128)}) custom-call(f32[128,128]{1,0:T(8,128)} %get-tuple-element.85.points_ref, f32[8,1024]{1,0:T(8,128)S(1)} %pad_maximum_fusion.9.coords_ref, bf16[3,1024,512]{2,1,0:T(8,128)(2,1)S(1)} %bitcast.60, ...), custom_call_target="tpu_custom_call" | custom-call | tf_op jit(solution)/shard_map/fourier/pallas_call | solution.py:251
  61.4 1.2 collective-permute-start.8
  62.5 8.5 %fourier.7 = (f32[1280,128]{1,0:T(8,128)}, f32[1280,128]{1,0:T(8,128)}, f32[640,128]{1,0:T(8,128)}, f32[640,128]{1,0:T(8,128)}, f32[1280,128]{1,0:T(8,128)}) custom-call(f32[128,128]{1,0:T(8,128)} %get-tuple-element.86.points_ref, f32[8,1024]{1,0:T(8,128)S(1)} %pad_maximum_fusion.9.coords_ref, bf16[3,1024,512]{2,1,0:T(8,128)(2,1)S(1)} %bitcast.61, ...), custom_call_target="tpu_custom_call" | custom-call | tf_op jit(solution)/shard_map/fourier/pallas_call | solution.py:251
  71.1 1.5 collective-permute-start.14
  72.8 2.7 %collective-permute-start.7 = (f32[32,40,128]{2,1,0:T(8,128)S(1)}, f32[32,40,128]{2,1,0:T(8,128)S(1)}, u32[]{:S(2)}, u32[]{:S(2)}) collective-permute-start(f32[32,40,128]{2,1,0:T(8,128)S(1)} %pad_maximum_fusion.3), channel_id=1, source_target_pairs={{0,2},{2,4},{4,6},{6,0},{1,3},{3,5},{5,7},{7,1},{8,10},{10,12},{12... | collective-permute-start | bytes 1966088 | tf_op jit(solution)/shard_map/ppermute | solution.py:271
  75.5 1.0 add.81
  76.7 0.9 fusion.3
  78.3 0.9 pad_maximum_fusion.7
  79.9 2.0 %collective-permute-start.15 = (f32[32,40,128]{2,1,0:T(8,128)}, f32[32,40,128]{2,1,0:T(8,128)}, u32[]{:S(2)}, u32[]{:S(2)}) collective-permute-start(f32[32,40,128]{2,1,0:T(8,128)} %pad_maximum_fusion.7), channel_id=1, source_target_pairs={{0,2},{2,4},{4,6},{6,0},{1,3},{3,5},{5,7},{7,1},{8,10},{10,12},{12... | collective-permute-start | bytes 1966088 | tf_op jit(solution)/shard_map/ppermute | solution.py:271
  81.9 1.0 pad_maximum_fusion.8
  82.9 1.7 %add.83 = f32[16,40,128]{2,1,0:T(8,128)} add(f32[16,40,128]{2,1,0:T(8,128)S(1)} %bitcast.73, f32[16,40,128]{2,1,0:T(8,128)} %collective-permute-done.10) | non-fusion elementwise | flops 81920 | bytes 983040 | tf_op jit(solution)/shard_map/add | solution.py:286
  84.7 7.0 %collective-permute-done.7 = f32[32,40,128]{2,1,0:T(8,128)S(1)} collective-permute-done((f32[32,40,128]{2,1,0:T(8,128)S(1)}, f32[32,40,128]{2,1,0:T(8,128)S(1)}, u32[]{:S(2)}, u32[]{:S(2)}) %collective-permute-start.7) | collective-permute-done | bytes 655392 | tf_op jit(solution)/shard_map/ppermute | solution.py:271
  91.7 3.0 %collective-permute-done.9 = f32[32,40,128]{2,1,0:T(8,128)S(1)} collective-permute-done((f32[32,40,128]{2,1,0:T(8,128)S(1)}, f32[32,40,128]{2,1,0:T(8,128)S(1)}, u32[]{:S(2)}, u32[]{:S(2)}) %collective-permute-start.9) | collective-permute-done | bytes 655392 | tf_op jit(solution)/shard_map/ppermute | solution.py:275
  94.7 0.9 add_add_fusion.3.refs_2_
  95.6 2.6 %place_slots.2 = f32[32,1,40,128]{3,2,1,0:T(8,128)} custom-call(s32[1]{0:T(128)} %bitcast.7.place_ref.refs_0_, s32[8,128]{1,0:T(8,128)} %get-tuple-element.46.refs_1_, f32[32,40,128]{2,1,0:T(8,128)} %add_add_fusion.3.refs_2_), custom_call_target="tpu_custom_call" | custom-call | tf_op jit(solution)/shard_map/place_slots/pallas_call | solution.py:308
  98.2 11.1 %all-to-all-start.2 = ((f32[32,1,40,128]{3,2,1,0:T(8,128)}), f32[32,1,40,128]{3,2,1,0:T(8,128)}, u32[]{:S(2)}, u32[]{:S(2)}) async-start(f32[32,1,40,128]{3,2,1,0:T(8,128)} %place_slots.2), calls=%async_computation.2 | async-start | bytes 1310720 | tf_op jit(solution)/shard_map/all_to_all | solution.py:320
  109.4 2.0 %pad_maximum_fusion.5 = f32[32,40,128]{2,1,0:T(8,128)} fusion(f32[16,40,128]{2,1,0:T(8,128)} %bitcast.65, f32[16,40,128]{2,1,0:T(8,128)} %add.83), kind=kLoop, calls=%fused_computation.6 | loop fusion | flops 163840 | bytes 1310720 | tf_op jit(solution)/shard_map/concatenate | solution.py:286
  111.4 1.1 add.85
  112.5 0.9 pad_maximum_fusion.6
  113.4 1.5 collective-permute-start.13
  114.9 1.0 collective-permute-done.17
  115.8 2.3 %add_add_fusion.1 = f32[32,40,128]{2,1,0:T(8,128)} fusion(f32[32,40,128]{2,1,0:T(8,128)} %collective-permute-done.17, f32[32,40,128]{2,1,0:T(8,128)S(1)} %bitcast.83, f32[32,40,128]{2,1,0:T(8,128)} %collective-permute-done.15), kind=kLoop, calls=%fused_computation.10 | loop fusion | flops 327680 | bytes 2621440 | tf_op jit(solution)/shard_map/add | solution.py:458
  118.2 4.3 %all-to-all-done.2 = f32[32,1,40,128]{3,2,1,0:T(8,128)} async-done(((f32[32,1,40,128]{3,2,1,0:T(8,128)}), f32[32,1,40,128]{3,2,1,0:T(8,128)}, u32[]{:S(2)}, u32[]{:S(2)}) %all-to-all-start.2) | async-done | bytes 655392 | tf_op jit(solution)/shard_map/all_to_all | solution.py:320
  122.4 5.1 %all-to-all-start.4 = ((f32[32,40,128]{2,1,0:T(8,128)}), f32[32,40,128]{2,1,0:T(8,128)}, u32[]{:S(2)}, u32[]{:S(2)}) async-start(f32[32,40,128]{2,1,0:T(8,128)} %add_add_fusion.1), calls=%async_computation.4 | async-start | bytes 1310720 | tf_op jit(solution)/shard_map/all_to_all | solution.py:320
  127.5 1.3 slice.140
  129.4 0.9 conditional.1
  129.4 0.9 broadcast.3
  130.3 1.4 collective-permute-done.13
  131.7 1.6 add_add_fusion.2
  133.3 2.5 %pad_maximum_fusion.2.refs_2_ = f32[96,40,128]{2,1,0:T(8,128)} fusion(f32[32,40,128]{2,1,0:T(8,128)} %get-tuple-element.98, f32[32,40,128]{2,1,0:T(8,128)S(1)} %add_add_fusion.2, f32[32,40,128]{2,1,0:T(8,128)S(1)} %copy-done.3), kind=kLoop, calls=%fused_computation.3 | loop fusion | flops 983040 | bytes 3932160 | tf_op jit(solution)/shard_map/concatenate | solution.py:467
  135.8 3.2 %place_slots.3 = f32[32,2,40,128]{3,2,1,0:T(8,128)} custom-call(s32[1]{0:T(128)} %bitcast.7.place_ref.refs_0_, s32[8,128]{1,0:T(8,128)} %get-tuple-element.46.refs_1_, f32[96,40,128]{2,1,0:T(8,128)} %pad_maximum_fusion.2.refs_2_), custom_call_target="tpu_custom_call" | custom-call | tf_op jit(solution)/shard_map/place_slots/pallas_call | solution.py:308
  139.0 1.6 all-to-all-done.4
  140.6 6.0 %all-to-all-start.3 = ((f32[32,2,40,128]{3,2,1,0:T(8,128)}), f32[32,2,40,128]{3,2,1,0:T(8,128)S(1)}, u32[]{:S(2)}, u32[]{:S(2)}) async-start(f32[32,2,40,128]{3,2,1,0:T(8,128)} %place_slots.3), calls=%async_computation.3 | async-start | bytes 2621440 | tf_op jit(solution)/shard_map/all_to_all | solution.py:320
  147.5 1.1 maximum_maximum_fusion
  149.4 2.9 %curvature.3 = f32[1,128]{1,0:T(1,128)} custom-call(f32[4]{0:T(128)} %dynamic-slice_reduce_fusion.refs_0_, f32[1280,128]{1,0:T(8,128)} %bitcast.24.refs_1_, bf16[4,256,256]{2,1,0:T(8,128)(2,1)} %get-tuple-element.96.refs_2_, bf16[4,256,256]{2,1,0:T(8,128)(2,1)} %get-tuple-element.97.refs_3_, s32[4,128]{1,0:T(4,128)} %refs_4_.5), custom_call_target="tpu_custom_call" | custom-call | tf_op jit(solution)/shard_map/curvature/pallas_call | solution.py:388
  152.3 2.9 %curvature.5 = f32[1,128]{1,0:T(1,128)} custom-call(f32[4]{0:T(128)} %dynamic-slice_reduce_fusion.refs_0_, f32[1280,128]{1,0:T(8,128)} %bitcast.49.refs_1_, bf16[4,256,256]{2,1,0:T(8,128)(2,1)} %get-tuple-element.96.refs_2_, bf16[4,256,256]{2,1,0:T(8,128)(2,1)} %get-tuple-element.97.refs_3_, s32[4,128]{1,0:T(4,128)} %refs_4_.5), custom_call_target="tpu_custom_call" | custom-call | tf_op jit(solution)/shard_map/curvature/pallas_call | solution.py:388
  155.2 11.2 %all-to-all-done.3 = f32[32,2,40,128]{3,2,1,0:T(8,128)S(1)} async-done(((f32[32,2,40,128]{3,2,1,0:T(8,128)}), f32[32,2,40,128]{3,2,1,0:T(8,128)S(1)}, u32[]{:S(2)}, u32[]{:S(2)}) %all-to-all-start.3) | async-done | bytes 1310752 | tf_op jit(solution)/shard_map/all_to_all | solution.py:320
  166.5 1.1 copy-done.4
  167.6 3.8 %curvature.4 = f32[1,128]{1,0:T(1,128)} custom-call(f32[4]{0:T(128)} %dynamic-slice_reduce_fusion.refs_0_, f32[2560,128]{1,0:T(8,128)} %bitcast.63, bf16[4,256,256]{2,1,0:T(8,128)(2,1)} %get-tuple-element.96.refs_2_, bf16[4,256,256]{2,1,0:T(8,128)(2,1)} %get-tuple-element.97.refs_3_, s32[4,128]{1,0:T(4,128)} %refs_4_.5), custom_call_target="tpu_custom_call" | custom-call | tf_op jit(solution)/shard_map/curvature/pallas_call | solution.py:388
  (86 shorter events, 7.6 us)
Async XLA Ops:
  0.0 10.6 %copy-start = (f32[8,3]{0,1:T(4,128)S(1)}, f32[8,3]{0,1:T(4,128)}, u32[]{:S(2)}) copy-start(f32[8,3]{0,1:T(4,128)} %param.9) | copy-start | bytes 292
  0.0 10.5 %copy-start.17 = (s32[512,3]{0,1:T(4,128)S(1)}, s32[512,3]{0,1:T(4,128)}, u32[]{:S(2)}) copy-start(s32[512,3]{0,1:T(4,128)} %param.12) | copy-start | bytes 18436
  0.0 10.7 %copy-start.21 = (s32[8]{0:T(128)S(1)}, s32[8]{0:T(128)}, u32[]{:S(2)}) copy-start(s32[8]{0:T(128)} %param.10) | copy-start | bytes 100
  9.8 29.0 %collective-permute-start.5 = (f32[3,2,512,512]{3,2,1,0:T(8,128)}, f32[3,2,512,512]{3,2,1,0:T(8,128)}, u32[]{:S(2)}, u32[]{:S(2)}) collective-permute-start(f32[3,2,512,512]{3,2,1,0:T(8,128)} %get-tuple-element.49), channel_id=1, source_target_pairs={{0,1},{1,0},{2,3},{3,2},{4,5},{5,4},{6,7},{7,6},{8,9},{9,8},{10,11... | collective-permute-start | bytes 18874376 | tf_op jit(solution)/shard_map/ppermute | solution.py:431
  10.5 18.5 %collective-permute-start.4 = (f32[8,512]{1,0:T(8,128)S(1)}, f32[8,512]{1,0:T(8,128)S(1)}, u32[]{:S(2)}, u32[]{:S(2)}) collective-permute-start(f32[8,512]{1,0:T(8,128)S(1)} %pad.9), channel_id=1, source_target_pairs={{0,1},{1,0},{2,3},{3,2},{4,5},{5,4},{6,7},{7,6},{8,9},{9,8},{10,11... | collective-permute-start | bytes 49160 | tf_op jit(solution)/shard_map/ppermute | solution.py:433
  21.3 14.3 %all-to-all-start.1 = ((f32[16,8,128]{2,1,0:T(8,128)}), f32[16,8,128]{2,1,0:T(8,128)S(1)}, u32[]{:S(2)}, u32[]{:S(2)}) async-start(f32[16,8,128]{2,1,0:T(8,128)} %broadcast_in_dim.26), calls=%async_computation.1 | async-start | bytes 131072 | tf_op jit(solution)/shard_map/all_to_all | solution.py:436
  35.6 0.6 copy-start.16
  38.1 0.8 copy-start.15
  38.9 3.8 %copy-start.2 = (bf16[3,2,512,512]{3,2,1,0:T(8,128)(2,1)S(1)}, bf16[3,2,512,512]{3,2,1,0:T(8,128)(2,1)}, u32[]{:S(2)}) copy-start(bf16[3,2,512,512]{3,2,1,0:T(8,128)(2,1)} %get-tuple-element.48) | copy-start | bytes 9437188
  51.1 21.6 %collective-permute-start.6 = (f32[16,40,128]{2,1,0:T(8,128)}, f32[16,40,128]{2,1,0:T(8,128)S(1)}, u32[]{:S(2)}, u32[]{:S(2)}) collective-permute-start(f32[16,40,128]{2,1,0:T(8,128)} %bitcast.95), channel_id=1, source_target_pairs={{0,2},{2,4},{4,6},{6,0},{1,3},{3,5},{5,7},{7,1},{8,10},{10,12},{12... | collective-permute-start | bytes 983048 | tf_op jit(solution)/shard_map/ppermute | solution.py:271
  61.1 21.8 %collective-permute-start.10 = (f32[16,40,128]{2,1,0:T(8,128)}, f32[16,40,128]{2,1,0:T(8,128)}, u32[]{:S(2)}, u32[]{:S(2)}) collective-permute-start(f32[16,40,128]{2,1,0:T(8,128)} %bitcast.92), channel_id=1, source_target_pairs={{0,2},{2,4},{4,6},{6,0},{1,3},{3,5},{5,7},{7,1},{8,10},{10,12},{12... | collective-permute-start | bytes 983048 | tf_op jit(solution)/shard_map/ppermute | solution.py:271
  61.4 14.2 %collective-permute-start.8 = (f32[16,40,128]{2,1,0:T(8,128)}, f32[16,40,128]{2,1,0:T(8,128)}, u32[]{:S(2)}, u32[]{:S(2)}) collective-permute-start(f32[16,40,128]{2,1,0:T(8,128)} %bitcast.23), channel_id=1, source_target_pairs={{0,6},{2,0},{4,2},{6,4},{1,7},{3,1},{5,3},{7,5},{8,14},{10,8},{12,... | collective-permute-start | bytes 983048 | tf_op jit(solution)/shard_map/ppermute | solution.py:275
  62.5 10.0 %copy-start.13 = (f32[1280,128]{1,0:T(8,128)S(1)}, f32[1280,128]{1,0:T(8,128)}, u32[]{:S(2)}) copy-start(f32[1280,128]{1,0:T(8,128)} %get-tuple-element.51) | copy-start | bytes 1966084
  62.5 10.0 %copy-start.14 = (f32[1280,128]{1,0:T(8,128)S(1)}, f32[1280,128]{1,0:T(8,128)}, u32[]{:S(2)}) copy-start(f32[1280,128]{1,0:T(8,128)} %get-tuple-element.53) | copy-start | bytes 1966084
  71.1 7.1 %collective-permute-start.14 = (f32[16,40,128]{2,1,0:T(8,128)}, f32[16,40,128]{2,1,0:T(8,128)S(1)}, u32[]{:S(2)}, u32[]{:S(2)}) collective-permute-start(f32[16,40,128]{2,1,0:T(8,128)} %bitcast.94), channel_id=1, source_target_pairs={{0,2},{2,4},{4,6},{6,0},{1,3},{3,5},{5,7},{7,1},{8,10},{10,12},{12... | collective-permute-start | bytes 983048 | tf_op jit(solution)/shard_map/ppermute | solution.py:271
  72.6 7.3 %collective-permute-start.16 = (f32[16,40,128]{2,1,0:T(8,128)}, f32[16,40,128]{2,1,0:T(8,128)S(1)}, u32[]{:S(2)}, u32[]{:S(2)}) collective-permute-start(f32[16,40,128]{2,1,0:T(8,128)} %bitcast.93), channel_id=1, source_target_pairs={{0,6},{2,0},{4,2},{6,4},{1,7},{3,1},{5,3},{7,5},{8,14},{10,8},{12,... | collective-permute-start | bytes 983048 | tf_op jit(solution)/shard_map/ppermute | solution.py:275
  72.7 4.0 %copy-start.8 = (f32[1280,128]{1,0:T(8,128)S(1)}, f32[1280,128]{1,0:T(8,128)}, u32[]{:S(2)}) copy-start(f32[1280,128]{1,0:T(8,128)} %get-tuple-element.56) | copy-start | bytes 1966084
  72.7 4.0 %copy-start.9 = (f32[1280,128]{1,0:T(8,128)S(1)}, f32[1280,128]{1,0:T(8,128)}, u32[]{:S(2)}) copy-start(f32[1280,128]{1,0:T(8,128)} %get-tuple-element.58) | copy-start | bytes 1966084
  72.8 18.8 %collective-permute-start.7 = (f32[32,40,128]{2,1,0:T(8,128)S(1)}, f32[32,40,128]{2,1,0:T(8,128)S(1)}, u32[]{:S(2)}, u32[]{:S(2)}) collective-permute-start(f32[32,40,128]{2,1,0:T(8,128)S(1)} %pad_maximum_fusion.3), channel_id=1, source_target_pairs={{0,2},{2,4},{4,6},{6,0},{1,3},{3,5},{5,7},{7,1},{8,10},{10,12},{12... | collective-permute-start | bytes 1966088 | tf_op jit(solution)/shard_map/ppermute | solution.py:271
  76.6 1.1 copy-start.10
  76.6 1.5 copy-start.11
  76.6 18.0 %collective-permute-start.9 = (f32[32,40,128]{2,1,0:T(8,128)S(1)}, f32[32,40,128]{2,1,0:T(8,128)S(1)}, u32[]{:S(2)}, u32[]{:S(2)}) collective-permute-start(f32[32,40,128]{2,1,0:T(8,128)S(1)} %pad_maximum_fusion.4), channel_id=1, source_target_pairs={{0,6},{2,0},{4,2},{6,4},{1,7},{3,1},{5,3},{7,5},{8,14},{10,8},{12,... | collective-permute-start | bytes 1966088 | tf_op jit(solution)/shard_map/ppermute | solution.py:275
  78.2 33.2 %collective-permute-start.12 = (f32[16,40,128]{2,1,0:T(8,128)}, f32[16,40,128]{2,1,0:T(8,128)}, u32[]{:S(2)}, u32[]{:S(2)}) collective-permute-start(f32[16,40,128]{2,1,0:T(8,128)} %bitcast.39), channel_id=1, source_target_pairs={{0,6},{2,0},{4,2},{6,4},{1,7},{3,1},{5,3},{7,5},{8,14},{10,8},{12,... | collective-permute-start | bytes 983048 | tf_op jit(solution)/shard_map/ppermute | solution.py:275
  79.2 15.4 %copy-start.7 = (f32[1280,128]{1,0:T(8,128)S(1)}, f32[1280,128]{1,0:T(8,128)}, u32[]{:S(2)}) copy-start(f32[1280,128]{1,0:T(8,128)} %get-tuple-element.50) | copy-start | bytes 1966084
  79.9 34.9 %collective-permute-start.15 = (f32[32,40,128]{2,1,0:T(8,128)}, f32[32,40,128]{2,1,0:T(8,128)}, u32[]{:S(2)}, u32[]{:S(2)}) collective-permute-start(f32[32,40,128]{2,1,0:T(8,128)} %pad_maximum_fusion.7), channel_id=1, source_target_pairs={{0,2},{2,4},{4,6},{6,0},{1,3},{3,5},{5,7},{7,1},{8,10},{10,12},{12... | collective-permute-start | bytes 1966088 | tf_op jit(solution)/shard_map/ppermute | solution.py:271
  82.9 32.9 %collective-permute-start.17 = (f32[32,40,128]{2,1,0:T(8,128)}, f32[32,40,128]{2,1,0:T(8,128)}, u32[]{:S(2)}, u32[]{:S(2)}) collective-permute-start(f32[32,40,128]{2,1,0:T(8,128)} %pad_maximum_fusion.8), channel_id=1, source_target_pairs={{0,6},{2,0},{4,2},{6,4},{1,7},{3,1},{5,3},{7,5},{8,14},{10,8},{12,... | collective-permute-start | bytes 1966088 | tf_op jit(solution)/shard_map/ppermute | solution.py:275
  98.2 24.2 %all-to-all-start.2 = ((f32[32,1,40,128]{3,2,1,0:T(8,128)}), f32[32,1,40,128]{3,2,1,0:T(8,128)}, u32[]{:S(2)}, u32[]{:S(2)}) async-start(f32[32,1,40,128]{3,2,1,0:T(8,128)} %place_slots.2), calls=%async_computation.2 | async-start | bytes 1310720 | tf_op jit(solution)/shard_map/all_to_all | solution.py:320
  109.4 6.5 %copy-start.6 = (f32[1280,128]{1,0:T(8,128)S(1)}, f32[1280,128]{1,0:T(8,128)}, u32[]{:S(2)}) copy-start(f32[1280,128]{1,0:T(8,128)} %get-tuple-element.60) | copy-start | bytes 1966084
  111.4 18.9 %collective-permute-start.11 = (f32[32,40,128]{2,1,0:T(8,128)}, f32[32,40,128]{2,1,0:T(8,128)}, u32[]{:S(2)}, u32[]{:S(2)}) collective-permute-start(f32[32,40,128]{2,1,0:T(8,128)} %pad_maximum_fusion.5), channel_id=1, source_target_pairs={{0,2},{2,4},{4,6},{6,0},{1,3},{3,5},{5,7},{7,1},{8,10},{10,12},{12... | collective-permute-start | bytes 1966088 | tf_op jit(solution)/shard_map/ppermute | solution.py:271
  113.4 18.3 %collective-permute-start.13 = (f32[32,40,128]{2,1,0:T(8,128)}, f32[32,40,128]{2,1,0:T(8,128)}, u32[]{:S(2)}, u32[]{:S(2)}) collective-permute-start(f32[32,40,128]{2,1,0:T(8,128)} %pad_maximum_fusion.6), channel_id=1, source_target_pairs={{0,6},{2,0},{4,2},{6,4},{1,7},{3,1},{5,3},{7,5},{8,14},{10,8},{12,... | collective-permute-start | bytes 1966088 | tf_op jit(solution)/shard_map/ppermute | solution.py:275
  122.4 18.2 %all-to-all-start.4 = ((f32[32,40,128]{2,1,0:T(8,128)}), f32[32,40,128]{2,1,0:T(8,128)}, u32[]{:S(2)}, u32[]{:S(2)}) async-start(f32[32,40,128]{2,1,0:T(8,128)} %add_add_fusion.1), calls=%async_computation.4 | async-start | bytes 1310720 | tf_op jit(solution)/shard_map/all_to_all | solution.py:320
  130.3 3.0 %copy-start.3 = (f32[32,40,128]{2,1,0:T(8,128)S(1)}, f32[32,40,128]{2,1,0:T(8,128)}, u32[]{:S(2)}) copy-start(f32[32,40,128]{2,1,0:T(8,128)} %add_add_fusion.3.refs_2_) | copy-start | bytes 1966084
  139.0 7.6 %copy-start.5 = (bf16[4,128,2,128]{3,2,1,0:T(2,128)(2,1)S(1)}, bf16[4,128,2,128]{3,2,1,0:T(2,128)(2,1)}, u32[]{:S(2)}) copy-start(bf16[4,128,2,128]{3,2,1,0:T(2,128)(2,1)} %param.14) | copy-start | bytes 786436
  140.6 25.8 %all-to-all-start.3 = ((f32[32,2,40,128]{3,2,1,0:T(8,128)}), f32[32,2,40,128]{3,2,1,0:T(8,128)S(1)}, u32[]{:S(2)}, u32[]{:S(2)}) async-start(f32[32,2,40,128]{3,2,1,0:T(8,128)} %place_slots.3), calls=%async_computation.3 | async-start | bytes 2621440 | tf_op jit(solution)/shard_map/all_to_all | solution.py:320
  147.1 1.6 copy-start.20
  152.3 20.2 %copy-start.1 = (f32[8,3]{0,1:T(4,128)S(1)}, f32[8,3]{0,1:T(4,128)}, u32[]{:S(2)}) copy-start(f32[8,3]{0,1:T(4,128)} %param.9) | copy-start | bytes 292
  152.3 19.1 %copy-start.18 = (f32[1,128]{1,0:T(1,128)S(1)}, f32[1,128]{1,0:T(1,128)}, u32[]{:S(2)}) copy-start(f32[1,128]{1,0:T(1,128)} %curvature.3) | copy-start | bytes 1540
  155.2 16.2 %copy-start.19 = (f32[1,128]{1,0:T(1,128)S(1)}, f32[1,128]{1,0:T(1,128)}, u32[]{:S(2)}) copy-start(f32[1,128]{1,0:T(1,128)} %curvature.5) | copy-start | bytes 1540
  166.5 1.1 copy-start.4

commit v2 on v1

v2 whole, which is shorter than its diff:
```python
import math

import jax
import jax.numpy as jnp
from jax import lax
from jax.experimental import pallas as pl
from jax.experimental.pallas import tpu as pltpu
from jax.sharding import Mesh
from jax.sharding import PartitionSpec as P

SUB = 4
KA = ("ka_0", "ka_1")
KA_ROW = ("ka_0", "ka_1", "row_0", "row_1")
ROW = ("row_0", "row_1")
PLANE = ("ka_0", "ka_1", "row_1")
INTERPRET = False

broadening = 1.0
refine_step = (0.05, 0.03, 0.02)

f32 = jnp.float32
bf16 = jnp.bfloat16
VMEM = pl.BlockSpec(memory_space=pltpu.VMEM)
SMEM = pl.BlockSpec(memory_space=pltpu.SMEM)
NX = 4
OWNERS = 32
BLOCKS = 128


def params(**more):
    return pltpu.CompilerParams(vmem_limit_bytes=56 << 20, **more)


ANY = pl.BlockSpec(memory_space=pl.ANY)


def cost(microseconds):
    return pl.CostEstimate(flops=int(microseconds * 2.5e8), bytes_accessed=0, transcendentals=0)


def iota(shape, dim):
    return lax.broadcasted_iota(jnp.int32, shape, dim)


def place_of(position):
    plane = (position % 8) // 2
    owner = (position // 8) * 2 + position % 2
    return plane, owner


def index_kernel(place_ref, table_ref, points_ref, slots_ref, weight_ref):
    my_plane = place_ref[0]
    table = table_ref[...]
    turned = table.T
    square = (BLOCKS, BLOCKS)
    order_down = table[:, 4:5].astype(jnp.int32)
    order_along = turned[4:5, :].astype(jnp.int32)
    here_down = order_down == iota(square, 1)
    here_along = iota(square, 0) == order_along

    def along(column):
        return jnp.sum(jnp.where(here_along, table[:, column : column + 1], 0.0), axis=0, keepdims=True)

    base = [along(axis) for axis in range(3)]
    count = along(3)
    count_down = jnp.sum(jnp.where(here_down, turned[3:4, :], 0.0), axis=1, keepdims=True)

    plane_down, owner_down = place_of(iota(square, 0))
    plane_along, owner_along = place_of(iota(square, 1))
    mates = plane_down == plane_along
    ahead = mates & (owner_down < owner_along)
    plane_row, owner_row = place_of(iota((1, BLOCKS), 1))
    away = (plane_row - my_plane + NX) % NX
    seat = jnp.where(away == 1, 0, jnp.where(away == 3, 1, 2))

    def row_of(chunk, within):
        half = within // (OWNERS // 2)
        opposite = jnp.where(chunk == 0, within, OWNERS // 2 * (1 + chunk + half) + within)
        apart = 3 * OWNERS * (1 + chunk) + seat * OWNERS + within
        spare = 12 * OWNERS + jnp.where(away == 2, 0, 1 + seat) * OWNERS + within
        return jnp.where(chunk == 3, spare, jnp.where(away == 2, opposite, apart))

    rows = 4 * OWNERS * NX
    entry = iota((rows, BLOCKS), 0)
    lane = iota((rows, BLOCKS), 1)
    gathered = [jnp.zeros((rows, BLOCKS), f32) for _ in range(3)]
    before = jnp.zeros((1, BLOCKS), f32)
    slots_ref[...] = jnp.zeros((8, BLOCKS), jnp.int32)
    weight_ref[...] = jnp.zeros((8, BLOCKS), f32)
    for s in range(SUB):
        fraction = (s + 0.5) / count - 0.5
        points = [base[axis] + fraction * refine_step[axis] for axis in range(3)]
        alive = count > s
        weight_ref[s : s + 1, :] = jnp.where(alive, 1.0 / count, 0.0)
        if s == 0:
            chunk, within = jnp.full((1, BLOCKS), 2, jnp.int32), owner_row
        else:
            live_down = count_down > s
            rank = before + jnp.sum(jnp.where(ahead & live_down, 1.0, 0.0), axis=0, keepdims=True)
            before = before + jnp.sum(jnp.where(mates & live_down, 1.0, 0.0), axis=0, keepdims=True)
            rank = jnp.where(alive, rank, 0.0).astype(jnp.int32)
            slots_ref[s : s + 1, :] = rank
            chunk, within = rank // OWNERS, rank % OWNERS
            chunk = jnp.where(chunk == 2, 3, chunk)
        match = entry == jnp.where(alive, row_of(chunk, within), -1)
        for axis in range(3):
            gathered[axis] = gathered[axis] + jnp.where(match, points[axis], 0.0)
    most = jnp.max(before, axis=1, keepdims=True)
    slots_ref[0:1, :] = jnp.broadcast_to(most, (1, BLOCKS)).astype(jnp.int32)
    points = jnp.zeros((rows, BLOCKS), f32)
    for axis in range(3):
        points = jnp.where(lane == axis, jnp.sum(gathered[axis], axis=1, keepdims=True), points)
    points_ref[...] = points


def find_points(table, plane):
    rows = OWNERS * NX
    return pl.pallas_call(
        index_kernel,
        out_shape=(
            jax.ShapeDtypeStruct((4 * rows, BLOCKS), f32),
            jax.ShapeDtypeStruct((8, BLOCKS), jnp.int32),
            jax.ShapeDtypeStruct((8, BLOCKS), f32),
        ),
        in_specs=[SMEM, VMEM],
        out_specs=(VMEM, VMEM, VMEM),
        compiler_params=params(),
        cost_estimate=cost(2),
        interpret=INTERPRET,
        name="find_points",
    )(plane, table)


def split_kernel(core_ref, space_ref, own_ref, send_ref, wide_ref):
    core = core_ref[0]
    depth, rows, width = space_ref.shape
    half = rows // 12
    pitch = wide_ref.shape[0] // depth
    for first in range(0, depth, 8):
        wide = space_ref[first : first + 8].astype(f32)
        for r in range(8):
            wide_ref[(first + r) * pitch : (first + r) * pitch + rows, :] = wide[r]
    for matrix in range(3):
        for part in range(2):
            for r in range(half):
                lanes = slice(r * width, (r + 1) * width)
                own_at = matrix * (rows // 3) + 2 * (half * core + r) + part
                send_at = matrix * (rows // 3) + 2 * (half * (1 - core) + r) + part
                own = wide_ref[pl.ds(own_at, depth, stride=pitch), :]
                own_ref[matrix, part, :, lanes] = own.astype(bf16)
                send_ref[matrix, part, :, lanes] = wide_ref[pl.ds(send_at, depth, stride=pitch), :]


def split_rows(space, core):
    depth, rows, width = space.shape
    block = min(depth, 128)
    lanes = rows // 12 * width
    shape = (3, 2, depth, lanes)
    spec = pl.BlockSpec((3, 2, block, lanes), lambda i: (0, 0, i, 0))
    return pl.pallas_call(
        split_kernel,
        grid=(depth // block,),
        out_shape=(jax.ShapeDtypeStruct(shape, bf16), jax.ShapeDtypeStruct(shape, f32)),
        in_specs=[SMEM, pl.BlockSpec((block, rows, width), lambda i: (i, 0, 0))],
        out_specs=(spec, spec),
        scratch_shapes=[pltpu.VMEM((block * (rows + 8), width), f32)],
        compiler_params=params(),
        cost_estimate=cost(8),
        interpret=INTERPRET,
        name="split_rows",
    )(core, space)


def turn(points, coords):
    turns = points[:, 0:1] * coords[0:1, :] + points[:, 1:2] * coords[1:2, :] + points[:, 2:3] * coords[2:3, :]
    rest = turns - jnp.floor(turns + 0.5)
    quarter = jnp.floor(4.0 * rest + 0.5)
    angle = (rest - 0.25 * quarter) * (2.0 * math.pi)
    square = angle * angle
    sine = angle * (1.0 + square * (-1.0 / 6 + square * (1.0 / 120 + square * (-1.0 / 5040 + square * (1.0 / 362880)))))
    cosine = 1.0 + square * (-0.5 + square * (1.0 / 24 + square * (-1.0 / 720 + square * (1.0 / 40320 - square / 3628800))))
    odd = jnp.abs(quarter) == 1.0
    first = jnp.where(odd, sine, cosine)
    second = jnp.where(odd, cosine, sine)
    cos_sign = jnp.where((quarter == 1.0) | (jnp.abs(quarter) == 2.0), -1.0, 1.0)
    sin_sign = jnp.where((quarter == -1.0) | (jnp.abs(quarter) == 2.0), -1.0, 1.0)
    return first * cos_sign, second * sin_sign


def fourier_kernel(low, high, narrowing, waits, points_ref, coords_ref, own_ref, other_ref, *refs):
    out_refs, phase_ref = refs[waits:-1], refs[-1]
    step = pl.program_id(0)
    count = high - low
    depth = coords_ref.shape[1] // 2
    tile = 16

    @pl.when(step == 0)
    def _():
        def rows_of(i, carry):
            first = pl.multiple_of(i * tile, tile)
            points = points_ref[pl.ds(low + first, tile), :]
            for source in range(2):
                coords = coords_ref[:, source * depth : (source + 1) * depth]
                cosine, sine = turn(points, coords)
                at_real = slice(source * 2 * depth, source * 2 * depth + depth)
                at_imag = slice(source * 2 * depth + depth, source * 2 * depth + 2 * depth)
                pairs = [(cosine, sine)]
                for axis in range(2):
                    coord = coords[axis : axis + 1, :]
                    pairs.append((-coord * sine, coord * cosine))
                for kind, (real, imag) in enumerate(pairs):
                    real_rows = pl.ds(2 * kind * count + first, tile)
                    imag_rows = pl.ds((2 * kind + 1) * count + first, tile)
                    phase_ref[real_rows, at_real] = real.astype(bf16)
                    phase_ref[real_rows, at_imag] = (-imag).astype(bf16)
                    phase_ref[imag_rows, at_real] = imag.astype(bf16)
                    phase_ref[imag_rows, at_imag] = real.astype(bf16)
            return carry

        lax.fori_loop(0, count // tile, rows_of, 0)

    if narrowing:
        other_value = other_ref[0].astype(bf16)
        out_refs[-1][0] = other_value
    else:
        other_value = other_ref[0]

    def store(product, kinds, first_kind, first_row):
        width = product.shape[1] // 2
        for kind in range(kinds):
            for half in range(2):
                block = product[kind * count : (kind + 1) * count, half * width : (half + 1) * width]
                at = (first_kind + kind) * 4 + first_row + half
                start = 0
                for ref in out_refs[: len(out_refs) - narrowing]:
                    size = ref.shape[0] // 40
                    ref[pl.ds(at, size, stride=40), :] = block[start : start + size]
                    start += size

    def product(kinds):
        rows = slice(0, kinds * count)
        return jnp.dot(phase_ref[rows, : 2 * depth], own_ref[0], preferred_element_type=f32) + jnp.dot(
            phase_ref[rows, 2 * depth :], other_value, preferred_element_type=f32
        )

    @pl.when(step < 2)
    def _():
        store(product(6), 6, 0, 2 * step)

    @pl.when(step >= 2)
    def _():
        store(product(2), 2, 6 + 2 * (step // 2 - 1), 2 * (step % 2))


def fourier(points, low, high, sizes, coords, own, other, microseconds, after=(), narrowing=False):
    depth2 = own.shape[1]
    width = own.shape[2] // 4
    spec = pl.BlockSpec((1, depth2, 2 * width), lambda j: (j // 2, 0, j % 2))
    shapes = [jax.ShapeDtypeStruct((size * 40, width), f32) for size in sizes]
    specs = [pl.BlockSpec(shape.shape, lambda j: (0, 0)) for shape in shapes]
    if narrowing:
        shapes.append(jax.ShapeDtypeStruct(own.shape, bf16))
        specs.append(spec)
    outs = pl.pallas_call(
        lambda *refs: fourier_kernel(low, high, int(narrowing), len(after), *refs),
        grid=(6,),
        out_shape=tuple(shapes),
        in_specs=[
            pl.BlockSpec(points.shape, lambda j: (0, 0)),
            pl.BlockSpec(coords.shape, lambda j: (0, 0)),
            spec,
            spec,
        ]
        + [ANY] * len(after),
        out_specs=tuple(specs),
        scratch_shapes=[pltpu.VMEM((6 * (high - low), 2 * depth2), bf16)],
        compiler_params=params(),
        cost_estimate=cost(microseconds),
        interpret=INTERPRET,
        name="fourier",
    )(points, coords, own, other, *after)
    return tuple(out.reshape(-1, 40, width) for out in outs[: len(sizes)]) + tuple(outs[len(sizes) :])


def to_right(value):
    return lax.ppermute(value, "row_0", [(i, (i + 1) % NX) for i in range(NX)])


def to_left(value):
    return lax.ppermute(value, "row_0", [(i, (i - 1) % NX) for i in range(NX)])


def first_hop(near, far):
    return to_right(near), to_left(far)


def add_kernel(chunks, waits, near_ref, far_ref, *refs):
    ins, outs = refs[: 2 * chunks], refs[2 * chunks + waits :]
    size = near_ref.shape[0] // chunks
    for c in range(chunks):
        rows = slice(c * size, (c + 1) * size)
        outs[2 * c][...] = ins[2 * c][...] + near_ref[rows]
        outs[2 * c + 1][...] = ins[2 * c + 1][...] + far_ref[rows]


def add_arrived(near, far, sides, after=()):
    chunks = len(sides) // 2
    count, rows, width = near.shape
    size = count // chunks
    whole = pl.BlockSpec(near.shape, lambda i: (0, 0, 0))
    lower = pl.BlockSpec((size, rows, width), lambda i: (0, 0, 0))
    upper = pl.BlockSpec((size, rows, width), lambda i: (1, 0, 0))
    return pl.pallas_call(
        lambda *refs: add_kernel(chunks, len(after), *refs),
        grid=(1,),
        out_shape=tuple(jax.ShapeDtypeStruct(side.shape, f32) for side in sides),
        in_specs=[whole, whole] + [lower, upper] * chunks + [ANY] * len(after),
        out_specs=(lower, upper) * chunks,
        input_output_aliases={2 + i: i for i in range(2 * chunks)},
        compiler_params=params(),
        cost_estimate=cost(1.5 * chunks),
        interpret=INTERPRET,
        name="add_arrived",
    )(near, far, *sides, *after)


def second_hop(right, left):
    right = to_right(right)
    left = to_left(left)
    return right, left


def place_kernel(units, tables, waits, place_ref, slots_ref, *refs):
    ins = refs[: tables + 3]
    outs = refs[tables + 3 + waits :]
    out_ref, table_ref = outs[0], outs[1]
    plane = place_ref[0]
    size = ins[0].shape[0]
    for i in range(tables):
        table_ref[i * size : (i + 1) * size] = ins[i][...]
    keep, right, left = ins[tables:]
    if tables == 2:
        table_ref[2 * size : 3 * size] = ins[1][...]
    at = min(tables, 1) * size
    table_ref[at : at + size] = keep[...] + right[...] + left[...]

    def body(owner, carry):
        position = (owner // 2) * 8 + 2 * plane + owner % 2
        for u, s in enumerate(units):
            out_ref[owner, u] = table_ref[slots_ref[s, position]]
        return carry

    lax.fori_loop(0, OWNERS, body, 0)


def place_slots(units, plane, slots, tables, parts, keep_table, after=()):
    size, rows, width = parts[0].shape
    count = len(tables) + 1
    table = jax.ShapeDtypeStruct((count * size, rows, width), f32)
    out = jax.ShapeDtypeStruct((OWNERS, len(units), rows, width), f32)
    return pl.pallas_call(
        lambda *refs: place_kernel(units, len(tables), len(after), *refs),
        out_shape=(out, table) if keep_table else (out,),
        in_specs=[SMEM, SMEM] + [VMEM] * (len(tables) + 3) + [ANY] * len(after),
        out_specs=(VMEM, VMEM) if keep_table else (VMEM,),
        scratch_shapes=[] if keep_table else [pltpu.VMEM(table.shape, f32)],
        compiler_params=params(),
        cost_estimate=cost(3),
        interpret=INTERPRET,
        name="place_slots",
    )(plane, slots, *tables, *parts, *after)


def to_owners(value):
    return lax.all_to_all(value, PLANE, split_axis=0, concat_axis=0, tiled=True)


def two_terms(value):
    high = value.astype(bf16)
    return high, (value - high.astype(f32)).astype(bf16)


def curvature_kernel(first, units, weight_ref, field_ref, turn_ref, back_ref, occupied_ref, *refs):
    out_ref = refs[-1]
    unit = pl.program_id(0)
    sources = field_ref.shape[0] // (units * 40)
    n = field_ref.shape[1]
    stride = units * 40

    def plane_of(kind):
        return jnp.concatenate(
            [field_ref[pl.ds(unit * 40 + kind * 4 + r, sources, stride=stride), :] for r in range(4)], axis=0
        )

    matrices = jnp.concatenate(
        [jnp.concatenate([plane_of(2 * c), plane_of(2 * c + 1)], axis=1) for c in range(5)], axis=0
    )
    high, low = two_terms(matrices)
    vectors = turn_ref[0]
    rotated = jnp.dot(high, vectors, preferred_element_type=f32) + jnp.dot(low, vectors, preferred_element_type=f32)
    stacked = jnp.concatenate(
        [
            jnp.concatenate([rotated[c * n : (c + 1) * n, :n] for c in range(5)], axis=1),
            jnp.concatenate([rotated[c * n : (c + 1) * n, n:] for c in range(5)], axis=1),
        ],
        axis=0,
    )
    back = back_ref[0]
    high, low = two_terms(stacked)
    bar = jnp.dot(back, high, preferred_element_type=f32) + jnp.dot(back, low, preferred_element_type=f32)
    bar_real, bar_imag = bar[:n], bar[n:]
    diagonal = jnp.where(iota((n, n), 0) == iota((n, n), 1), bar_real[:, :n], 0.0)
    spacing = jnp.sum(diagonal, axis=0, keepdims=True) - jnp.sum(diagonal, axis=1, keepdims=True)
    smoothed = spacing / (spacing * spacing + broadening)

    def pick(value, c):
        return value[:, (c + 1) * n : (c + 2) * n]

    xcov_real = pick(bar_real, 2) + smoothed * pick(bar_real, 0)
    xcov_imag = pick(bar_imag, 2) + smoothed * pick(bar_imag, 0)
    ycov_real = pick(bar_real, 3) + smoothed * pick(bar_real, 1)
    ycov_imag = pick(bar_imag, 3) + smoothed * pick(bar_imag, 1)
    s = first + unit
    filled = occupied_ref[pl.ds(s, 1), :].astype(f32)
    filled_down = jnp.broadcast_to(filled, (n, n)).T
    pairing = filled_down * (1.0 - filled)
    product = pairing * (xcov_real * ycov_imag.T + xcov_imag * ycov_real.T)
    berry = jnp.sum(jnp.sum(product, axis=0, keepdims=True), axis=1, keepdims=True) * (-2.0 / n)
    weight = weight_ref[s]
    lane = iota((1, BLOCKS), 1)
    result = jnp.where((lane == s) & (weight > 0.0), weight * berry, 0.0)
    before = jnp.where(unit == 0, 0.0, out_ref[...])
    out_ref[...] = result + before


def curvature(first, units, weight, arrived, vectors, adjoint, occupied, after=()):
    width = arrived.shape[-1]
    flat = arrived.reshape(-1, width)
    matrix = pl.BlockSpec((1, 2 * width, 2 * width), lambda u: (first + u, 0, 0))
    return pl.pallas_call(
        lambda *refs: curvature_kernel(first, units, *refs),
        grid=(units,),
        out_shape=jax.ShapeDtypeStruct((1, BLOCKS), f32),
        in_specs=[
            SMEM,
            pl.BlockSpec(flat.shape, lambda u: (0, 0)),
            matrix,
            matrix,
            pl.BlockSpec(occupied.shape, lambda u: (0, 0)),
        ]
        + [ANY] * len(after),
        out_specs=pl.BlockSpec((1, BLOCKS), lambda u: (0, 0)),
        compiler_params=params(),
        cost_estimate=cost(2.5 * units),
        interpret=INTERPRET,
        name="curvature",
    )(weight, flat, vectors, adjoint, occupied, *after)


def vector_kernel(eigvecs_ref, turn_ref, back_ref, wide_ref):
    n = eigvecs_ref.shape[2]
    wide_ref[...] = eigvecs_ref[0].astype(f32)
    real, imag = (wide_ref[pl.ds(part, n, stride=2), :].astype(bf16) for part in range(2))
    turn_ref[0, :n, :n] = real
    turn_ref[0, :n, n:] = imag
    turn_ref[0, n:, :n] = -imag
    turn_ref[0, n:, n:] = real
    group = n // OWNERS
    for part in range(2):
        packed = jnp.concatenate(
            [wide_ref[pl.ds(2 * r + part, OWNERS, stride=2 * group), :] for r in range(group)], axis=0
        )
        turned = packed.T
        if part == 0:
            back_ref[0, :n, :n] = turned.astype(bf16)
            back_ref[0, n:, n:] = turned.astype(bf16)
        else:
            back_ref[0, :n, n:] = turned.astype(bf16)
            back_ref[0, n:, :n] = (-turned).astype(bf16)


def vector_matrices(eigvecs):
    slots, width = eigvecs.shape[0], eigvecs.shape[1]
    shape = jax.ShapeDtypeStruct((slots, 2 * width, 2 * width), bf16)
    square = pl.BlockSpec((1, 2 * width, 2 * width), lambda i: (i, 0, 0))
    return pl.pallas_call(
        vector_kernel,
        grid=(slots,),
        out_shape=(shape, shape),
        in_specs=[pl.BlockSpec((1, 2 * width, width), lambda i: (i, 0, 0))],
        out_specs=(square, square),
        scratch_shapes=[pltpu.VMEM((2 * width, width), f32)],
        compiler_params=params(),
        cost_estimate=cost(2),
        interpret=INTERPRET,
        name="vector_matrices",
    )(eigvecs.reshape(slots, 2 * width, width))


def body(base_k, counts, block_order, lattice, real_space, eigvecs, occupied):
    plane, core = lax.axis_index("row_0"), lax.axis_index("row_1")
    row = plane * 2 + core
    plane_ref = plane.reshape(1).astype(jnp.int32)
    core_ref = core.reshape(1).astype(jnp.int32)
    depth, _, slab, _, width = real_space.shape

    own_base = lax.dynamic_slice_in_dim(base_k, row, 1, 0)
    own_count = lax.dynamic_slice_in_dim(counts, row, 1, 0).astype(f32)[:, None]
    mine = jnp.concatenate([own_base, own_count, block_order.astype(f32)[:, None]], axis=1)
    mine = jnp.pad(mine, ((0, 0), (0, BLOCKS - 5)))
    line = lax.all_to_all(jnp.broadcast_to(mine[None], (8, 1, BLOCKS)), ROW, 0, 0, tiled=True)

    own, send = split_rows(real_space.reshape(depth, 6 * slab, width), core_ref)
    swap = [(0, 1), (1, 0)]
    other = lax.ppermute(send, "row_1", swap)
    own_coords = jnp.pad(lattice.T.astype(f32), ((0, 5), (0, 0)))
    coords = jnp.concatenate([own_coords, lax.ppermute(own_coords, "row_1", swap)], axis=1)

    lines = jnp.broadcast_to(line.reshape(1, 8, BLOCKS), (16, 8, BLOCKS))
    table = lax.all_to_all(lines, KA, 0, 0, tiled=True).reshape(BLOCKS, BLOCKS)
    turning, back = vector_matrices(eigvecs)
    points, slots, weights = find_points(table, plane_ref)
    position = (lax.axis_index(KA) * 8 + row).astype(jnp.int32)
    weight = lax.dynamic_slice(weights, (jnp.int32(0), position), (SUB, 1)).reshape(SUB)

    own = own.reshape(3, 2 * depth, -1)
    other = other.reshape(3, 2 * depth, -1)
    half = OWNERS // 2
    opposite = (half, half, OWNERS, OWNERS)
    others = (OWNERS, OWNERS, OWNERS)

    def rest(chunk, after):
        low = 3 * OWNERS * (1 + chunk)
        return fourier(points, low, low + 3 * OWNERS, others, coords, own, other, 6, after)

    near0, far0, near13, far13, other = fourier(
        points, 0, 3 * OWNERS, opposite, coords, own, other, 6, narrowing=True
    )
    hop0 = first_hop(near0, far0)
    hop13 = first_hop(near13, far13)
    right0, left0, keep0 = rest(0, ())
    right0, left0 = add_arrived(*hop0, (right0, left0))
    ring0 = second_hop(right0, left0)
    right1, left1, keep1 = rest(1, (right0,))
    right3, left3, keep3 = rest(2, (keep1,))
    right1, left1, right3, left3 = add_arrived(*hop13, (right1, left1, right3, left3))
    ring1 = second_hop(right1, left1)
    ring3 = second_hop(right3, left3)

    def further(_):
        low = 12 * OWNERS
        near, far, right, left, keep = fourier(
            points, low, low + 4 * OWNERS, (half, half) + others, coords, own, other, 8
        )
        right, left = second_hop(*add_arrived(*first_hop(near, far), (right, left)))
        return keep + right + left

    extra = lax.cond(slots[0, 0] > 2 * OWNERS, further, lambda _: jnp.zeros(keep0.shape, f32), 0)

    placed1, sum0 = place_slots((1,), plane_ref, slots, [], (keep0, *ring0), True, (right3,))
    unit1 = to_owners(placed1)
    (placed23,) = place_slots((2, 3), plane_ref, slots, [sum0, extra], (keep1, *ring1), False)
    unit23 = to_owners(placed23)
    curve1 = curvature(1, 1, weight, unit1, turning, back, occupied, (placed23,))
    unit0 = to_owners(keep3 + ring3[0] + ring3[1])
    curve23 = curvature(2, 2, weight, unit23, turning, back, occupied, (curve1,))
    curve0 = curvature(0, 1, weight, unit0, turning, back, occupied, (curve23,))
    return (curve1 + curve23 + curve0)[0, :SUB]


def solution(mesh):
    finer = Mesh(mesh.devices.reshape(4, 4, 4, 2), ("ka_0", "ka_1", "row_0", "row_1"))
    placed = (
        P(KA, None),
        P(KA),
        P(KA_ROW),
        P(ROW, None),
        P(ROW, None, KA, None, None),
        P(KA_ROW, None, None, None),
        P(KA_ROW, None),
    )
    return jax.shard_map(body, mesh=finer, in_specs=placed, out_specs=P(KA_ROW), check_vma=False)
```

time: 174 us -> 161 us (0.925)
  the two profiles are of different devices: /device:TPU:7 before, /device:TPU:1 now
where the time goes in v2:
time: 161 us; the launch traced here: 160 us
  Pallas kernels  62.9 us (39%)
  starting transfers between devices  43.7 us (27%)
  waiting for transfers between devices  33.6 us (21%)
  blocking collectives  9.29 us (6%)
  local copies, waits for them, and re-layouts  6.42 us (4%)
  between operations  2.13 us (1%)
  other arithmetic  1.75 us (1%)
    pallas_call x4, Pallas kernels, fourier(): pl.pallas_call(lambda *refs: fourier_kernel(low, high, int(narrowing), le...  28.5 us
    all_to_all x3, starting transfers between devices, to_owners(): return lax.all_to_all(value, PLANE, split_axis=0, concat_axis=0, tiled=True)  21 us
    ppermute x5, waiting for transfers between devices, to_left(): return lax.ppermute(value, 'row_0', [(i, (i - 1) % NX) for i in range(NX)])  13.9 us
    ppermute x5, starting transfers between devices, to_left(): return lax.ppermute(value, 'row_0', [(i, (i - 1) % NX) for i in range(NX)])  13.2 us
    pallas_call x3, Pallas kernels, curvature(): pl.pallas_call(lambda *refs: curvature_kernel(first, units, *refs), grid=...  9.66 us
    all_to_all x1, blocking collectives, body(): lax.all_to_all(jnp.broadcast_to(mine[None], (8, 1, BLOCKS)), ROW, 0, 0, t...  9.29 us
    all_to_all x3, waiting for transfers between devices, to_owners(): return lax.all_to_all(value, PLANE, split_axis=0, concat_axis=0, tiled=True)  9.19 us
    all_to_all x1, starting transfers between devices, body(): table = lax.all_to_all(lines, KA, 0, 0, tiled=True).reshape(BLOCKS, BLOCKS)  7.77 us
  transfers between devices with their start and end apart: 16, of which 6 were waited for; matrix products, arithmetic and copies ran while one was open for 3% of the time, Pallas kernels for 27%

profile of v2, /device:TPU:1, one launch (start us, length us, event | category | flops | bytes accessed | tf_op | source)
XLA Modules:
  0.0 159.9 jit_solution(13280753493048772348)
XLA Ops:
  0.0 7.6 %split_rows.1 = (bf16[3,2,512,512]{3,2,1,0:T(8,128)(2,1)S(1)}, f32[3,2,512,512]{3,2,1,0:T(8,128)}) custom-call(s32[1]{0:T(128)} %bitcast.11.core_ref, bf16[512,48,128]{2,1,0:T(8,128)(2,1)} %bitcast.57), custom_call_target="tpu_custom_call" | custom-call | flops 2000000000 | tf_op jit(solution)/shard_map/split_rows/pallas_call | solution.py:160
  7.6 1.4 collective-permute-start.5
  9.0 0.1 collective-permute-start.4
  9.1 0.1 constant_dynamic-slice_fusion
  9.8 0.6 dynamic_slice.10
  11.1 0.1 fusion
  11.2 9.3 %all_to_all.25 = f32[8,1,128]{2,1,0:T(1,128)S(1)} all-to-all(f32[8,1,128]{2,1,0:T(1,128)S(1)} %broadcast_in_dim.24), channel_id=1, replica_groups=mesh['ka_0'=4,'ka_1'=4,'row_0'=4,'row_1'=2] {'row_0','row_1'}, dimensions={0} | all-to-all | bytes 8192 | tf_op jit(solution)/shard_map/all_to_all | solution.py:511
  20.5 0.6 broadcast_in_dim.26
  21.2 7.8 %all-to-all-start.1 = ((f32[16,8,128]{2,1,0:T(8,128)}), f32[16,8,128]{2,1,0:T(8,128)S(1)}, u32[]{:S(2)}, u32[]{:S(2)}) async-start(f32[16,8,128]{2,1,0:T(8,128)} %broadcast_in_dim.26), calls=%async_computation.1 | async-start | bytes 131072 | tf_op jit(solution)/shard_map/all_to_all | solution.py:520
  28.9 0.0 collective-permute-done.4
  29.0 6.5 %all-to-all-done.1 = f32[16,8,128]{2,1,0:T(8,128)S(1)} async-done(((f32[16,8,128]{2,1,0:T(8,128)}), f32[16,8,128]{2,1,0:T(8,128)S(1)}, u32[]{:S(2)}, u32[]{:S(2)}) %all-to-all-start.1) | async-done | bytes 65568 | tf_op jit(solution)/shard_map/all_to_all | solution.py:520
  35.5 0.6 copy-done.11
  36.1 2.1 %find_points.1 = (f32[512,128]{1,0:T(8,128)S(1)}, s32[8,128]{1,0:T(8,128)}, f32[8,128]{1,0:T(8,128)}) custom-call(s32[1]{0:T(128)} %bitcast.5.place_ref.refs_0_, f32[128,128]{1,0:T(8,128)} %bitcast.55), custom_call_target="tpu_custom_call" | custom-call | flops 500000000 | tf_op jit(solution)/shard_map/find_points/pallas_call | solution.py:118
  38.2 9.2 %fourier.6 = (f32[640,128]{1,0:T(8,128)}, f32[640,128]{1,0:T(8,128)}, f32[1280,128]{1,0:T(8,128)}, f32[1280,128]{1,0:T(8,128)}, bf16[3,1024,512]{2,1,0:T(8,128)(2,1)S(1)}) custom-call(f32[512,128]{1,0:T(8,128)S(1)} %get-tuple-element.58.refs_0_, f32[8,1024]{1,0:T(8,128)S(1)} %pad_maximum_fusion.refs_1_, bf16[3,1024,512]{2,1,0:T(8,128)(2,1)S(1)} %bitcast.36, ...), custom_call_target="tpu_custom_call" | custom-call | flops 1500000000 | tf_op jit(solution)/shard_map/fourier/pallas_call | solution.py:264
  47.4 0.3 collective-permute-start.6
  47.7 2.4 %collective-permute-start.7 = (f32[16,40,128]{2,1,0:T(8,128)}, f32[16,40,128]{2,1,0:T(8,128)}, u32[]{:S(2)}, u32[]{:S(2)}) collective-permute-start(f32[16,40,128]{2,1,0:T(8,128)} %bitcast.61), channel_id=1, source_target_pairs={{0,6},{2,0},{4,2},{6,4},{1,7},{3,1},{5,3},{7,5},{8,14},{10,8},{12,... | collective-permute-start | bytes 983048 | tf_op jit(solution)/shard_map/ppermute | solution.py:290
  50.1 2.7 %collective-permute-start.11 = (f32[32,40,128]{2,1,0:T(8,128)}, f32[32,40,128]{2,1,0:T(8,128)S(1)}, u32[]{:S(2)}, u32[]{:S(2)}) collective-permute-start(f32[32,40,128]{2,1,0:T(8,128)} %bitcast.59), channel_id=1, source_target_pairs={{0,6},{2,0},{4,2},{6,4},{1,7},{3,1},{5,3},{7,5},{8,14},{10,8},{12,... | collective-permute-start | bytes 1966088 | tf_op jit(solution)/shard_map/ppermute | solution.py:290
  52.8 6.4 %fourier.7 = (f32[1280,128]{1,0:T(8,128)}, f32[1280,128]{1,0:T(8,128)}, f32[1280,128]{1,0:T(8,128)}) custom-call(f32[512,128]{1,0:T(8,128)S(1)} %get-tuple-element.58.refs_0_, f32[8,1024]{1,0:T(8,128)S(1)} %pad_maximum_fusion.refs_1_, bf16[3,1024,512]{2,1,0:T(8,128)(2,1)S(1)} %bitcast.37, bf16[3,1024,512]{2,1,0:T(8,128)(2,1)S(1)} %get-tuple-element.61.refs_3_), custom_call_target="tpu_custom_call" | custom-call | flops 1500000000 | tf_op jit(solution)/shard_map/fourier/pallas_call | solution.py:264
  59.2 2.2 %add_arrived.4 = (f32[32,40,128]{2,1,0:T(8,128)}, f32[32,40,128]{2,1,0:T(8,128)}) custom-call(f32[16,40,128]{2,1,0:T(8,128)} %collective-permute-done.6.refs_0_, f32[16,40,128]{2,1,0:T(8,128)} %collective-permute-done.7.refs_1_, f32[32,40,128]{2,1,0:T(8,128)} %bitcast.41, f32[32,40,128]{2,1,0:T(8,128)} %bitcast.50), custom_call_target="tpu_custom_call", output_to_operand_aliasing={{0}: (2, {}), {1}: (3, {})} | custom-call | flops 375000000 | tf_op jit(solution)/shard_map/add_arrived/pallas_call | solution.py:313
  61.4 2.7 %collective-permute-start.9 = (f32[32,40,128]{2,1,0:T(8,128)}, f32[32,40,128]{2,1,0:T(8,128)}, u32[]{:S(2)}, u32[]{:S(2)}) collective-permute-start(f32[32,40,128]{2,1,0:T(8,128)} %get-tuple-element.68), channel_id=1, source_target_pairs={{0,6},{2,0},{4,2},{6,4},{1,7},{3,1},{5,3},{7,5},{8,14},{10,8},{12,... | collective-permute-start | bytes 1966088 | tf_op jit(solution)/shard_map/ppermute | solution.py:290
  64.1 6.4 %fourier.8 = (f32[1280,128]{1,0:T(8,128)}, f32[1280,128]{1,0:T(8,128)}, f32[1280,128]{1,0:T(8,128)}) custom-call(f32[512,128]{1,0:T(8,128)S(1)} %get-tuple-element.58.refs_0_, f32[8,1024]{1,0:T(8,128)S(1)} %pad_maximum_fusion.refs_1_, bf16[3,1024,512]{2,1,0:T(8,128)(2,1)S(1)} %bitcast.38, bf16[3,1024,512]{2,1,0:T(8,128)(2,1)S(1)} %get-tuple-element.61.refs_3_, ...), custom_call_target="tpu_custom_call" | custom-call | flops 1500000000 | tf_op jit(solution)/shard_map/fourier/pallas_call | solution.py:264
  70.5 6.4 %fourier.9 = (f32[1280,128]{1,0:T(8,128)}, f32[1280,128]{1,0:T(8,128)}, f32[1280,128]{1,0:T(8,128)}) custom-call(f32[512,128]{1,0:T(8,128)S(1)} %get-tuple-element.58.refs_0_, f32[8,1024]{1,0:T(8,128)S(1)} %pad_maximum_fusion.refs_1_, bf16[3,1024,512]{2,1,0:T(8,128)(2,1)S(1)} %bitcast.39, bf16[3,1024,512]{2,1,0:T(8,128)(2,1)S(1)} %get-tuple-element.61.refs_3_, ...), custom_call_target="tpu_custom_call" | custom-call | flops 1500000000 | tf_op jit(solution)/shard_map/fourier/pallas_call | solution.py:264
  76.9 0.8 copy-done.5
  77.8 0.2 copy-done.6
  78.0 2.8 %add_arrived.5 = (f32[32,40,128]{2,1,0:T(8,128)}, f32[32,40,128]{2,1,0:T(8,128)}, f32[32,40,128]{2,1,0:T(8,128)}, f32[32,40,128]{2,1,0:T(8,128)}) custom-call(f32[32,40,128]{2,1,0:T(8,128)} %copy-done.5, f32[32,40,128]{2,1,0:T(8,128)} %copy-done.6, f32[32,40,128]{2,1,0:T(8,128)} %bitcast.51, ...), custom_call_target="tpu_custom_call", output_to_operand_aliasing={{0}: (2, {}), {1}: (3, {}), {2}: (4, {}), {3}: (5, {})} | custom-call | flops 750000000 | tf_op jit(solution)/shard_map/add_arrived/pallas_call | solution.py:313
  80.7 2.7 %collective-permute-start.13 = (f32[32,40,128]{2,1,0:T(8,128)}, f32[32,40,128]{2,1,0:T(8,128)}, u32[]{:S(2)}, u32[]{:S(2)}) collective-permute-start(f32[32,40,128]{2,1,0:T(8,128)} %get-tuple-element.82), channel_id=1, source_target_pairs={{0,6},{2,0},{4,2},{6,4},{1,7},{3,1},{5,3},{7,5},{8,14},{10,8},{12,... | collective-permute-start | bytes 1966088 | tf_op jit(solution)/shard_map/ppermute | solution.py:290
  83.4 0.8 collective-permute-done.8.refs_3_
  84.2 3.2 %place_slots.2 = (f32[32,1,40,128]{3,2,1,0:T(8,128)}, f32[32,40,128]{2,1,0:T(8,128)}) custom-call(s32[1]{0:T(128)} %bitcast.5.place_ref.refs_0_, s32[8,128]{1,0:T(8,128)} %get-tuple-element.57.refs_1_, f32[32,40,128]{2,1,0:T(8,128)} %bitcast.58, f32[32,40,128]{2,1,0:T(8,128)} %collective-permute-done.8.refs_3_, ...), custom_call_target="tpu_custom_call" | custom-call | flops 750000000 | tf_op jit(solution)/shard_map/place_slots/pallas_call | solution.py:361
  87.4 9.0 %all-to-all-start.2 = ((f32[32,1,40,128]{3,2,1,0:T(8,128)}), f32[32,1,40,128]{3,2,1,0:T(8,128)}, u32[]{:S(2)}, u32[]{:S(2)}) async-start(f32[32,1,40,128]{3,2,1,0:T(8,128)} %get-tuple-element.77), calls=%async_computation.2 | async-start | bytes 1310720 | tf_op jit(solution)/shard_map/all_to_all | solution.py:375
  96.4 1.2 slice.6
  98.3 0.3 conditional.1
  98.6 3.7 %place_slots.3.refs_5_ = f32[32,2,40,128]{3,2,1,0:T(8,128)} custom-call(s32[1]{0:T(128)} %bitcast.5.place_ref.refs_0_, s32[8,128]{1,0:T(8,128)} %get-tuple-element.57.refs_1_, f32[32,40,128]{2,1,0:T(8,128)} %get-tuple-element.80.refs_2_, f32[32,40,128]{2,1,0:T(8,128)S(1)} %get-tuple-element.85.refs_3_, f32[32,40,128]{2,1,0:T(8,128)} %bitcast.43, ...), custom_call_target="tpu_custom_call" | custom-call | flops 750000000 | tf_op jit(solution)/shard_map/place_slots/pallas_call | solution.py:361
  102.3 7.2 %all-to-all-done.2 = f32[32,1,40,128]{3,2,1,0:T(8,128)} async-done(((f32[32,1,40,128]{3,2,1,0:T(8,128)}), f32[32,1,40,128]{3,2,1,0:T(8,128)}, u32[]{:S(2)}, u32[]{:S(2)}) %all-to-all-start.2) | async-done | bytes 655392 | tf_op jit(solution)/shard_map/all_to_all | solution.py:375
  109.5 3.7 %all-to-all-start.3 = ((f32[32,2,40,128]{3,2,1,0:T(8,128)}), f32[32,2,40,128]{3,2,1,0:T(8,128)S(1)}, u32[]{:S(2)}, u32[]{:S(2)}) async-start(f32[32,2,40,128]{3,2,1,0:T(8,128)} %place_slots.3.refs_5_), calls=%async_computation.3 | async-start | bytes 2621440 | tf_op jit(solution)/shard_map/all_to_all | solution.py:375
  113.3 2.7 %collective-permute-start.15 = (f32[32,40,128]{2,1,0:T(8,128)S(1)}, f32[32,40,128]{2,1,0:T(8,128)S(1)}, u32[]{:S(2)}, u32[]{:S(2)}) collective-permute-start(f32[32,40,128]{2,1,0:T(8,128)S(1)} %copy-done.8), channel_id=1, source_target_pairs={{0,6},{2,0},{4,2},{6,4},{1,7},{3,1},{5,3},{7,5},{8,14},{10,8},{12,... | collective-permute-start | bytes 1966088 | tf_op jit(solution)/shard_map/ppermute | solution.py:290
  116.0 13.9 %collective-permute-done.15 = f32[32,40,128]{2,1,0:T(8,128)S(1)} collective-permute-done((f32[32,40,128]{2,1,0:T(8,128)S(1)}, f32[32,40,128]{2,1,0:T(8,128)S(1)}, u32[]{:S(2)}, u32[]{:S(2)}) %collective-permute-start.15) | collective-permute-done | bytes 655392 | tf_op jit(solution)/shard_map/ppermute | solution.py:290
  129.9 3.1 %collective-permute-done.14 = f32[32,40,128]{2,1,0:T(8,128)S(1)} collective-permute-done((f32[32,40,128]{2,1,0:T(8,128)S(1)}, f32[32,40,128]{2,1,0:T(8,128)S(1)}, u32[]{:S(2)}, u32[]{:S(2)}) %collective-permute-start.14) | collective-permute-done | bytes 655392 | tf_op jit(solution)/shard_map/ppermute | solution.py:286
  133.1 0.9 add_add_fusion.1
  134.0 8.2 %all-to-all-start.4 = ((f32[32,40,128]{2,1,0:T(8,128)}), f32[32,40,128]{2,1,0:T(8,128)S(1)}, u32[]{:S(2)}, u32[]{:S(2)}) async-start(f32[32,40,128]{2,1,0:T(8,128)} %add_add_fusion.1), calls=%async_computation.4 | async-start | bytes 1310720 | tf_op jit(solution)/shard_map/all_to_all | solution.py:375
  142.3 3.3 %vector_matrices.1 = (bf16[4,256,256]{2,1,0:T(8,128)(2,1)}, bf16[4,256,256]{2,1,0:T(8,128)(2,1)}) custom-call(bf16[4,256,128]{2,1,0:T(8,128)(2,1)} %bitcast.65), custom_call_target="tpu_custom_call" | custom-call | flops 500000000 | tf_op jit(solution)/shard_map/vector_matrices/pallas_call | solution.py:486
  145.5 0.7 dynamic-slice_reduce_fusion.refs_0_
  146.2 2.8 %curvature.3.refs_5_ = f32[1,128]{1,0:T(1,128)} custom-call(f32[4]{0:T(128)} %dynamic-slice_reduce_fusion.refs_0_, f32[1280,128]{1,0:T(8,128)} %bitcast.27.refs_1_, bf16[4,256,256]{2,1,0:T(8,128)(2,1)} %get-tuple-element.78.refs_2_, bf16[4,256,256]{2,1,0:T(8,128)(2,1)} %get-tuple-element.79.refs_3_, s32[4,128]{1,0:T(4,128)} %refs_4_.5, ...), custom_call_target="tpu_custom_call" | custom-call | flops 625000000 | tf_op jit(solution)/shard_map/curvature/pallas_call | solution.py:440
  149.0 4.1 %curvature.4.refs_5_ = f32[1,128]{1,0:T(1,128)} custom-call(f32[4]{0:T(128)} %dynamic-slice_reduce_fusion.refs_0_, f32[2560,128]{1,0:T(8,128)} %bitcast.44, bf16[4,256,256]{2,1,0:T(8,128)(2,1)} %get-tuple-element.78.refs_2_, bf16[4,256,256]{2,1,0:T(8,128)(2,1)} %get-tuple-element.79.refs_3_, s32[4,128]{1,0:T(4,128)} %refs_4_.5, f32[1,128]{1,0:T(1,128)} %curvature.3.refs_5_), custom_call_target="tpu_custom_call" | custom-call | flops 1250000000 | tf_op jit(solution)/shard_map/curvature/pallas_call | solution.py:440
  153.2 2.0 %all-to-all-done.4 = f32[32,40,128]{2,1,0:T(8,128)S(1)} async-done(((f32[32,40,128]{2,1,0:T(8,128)}), f32[32,40,128]{2,1,0:T(8,128)S(1)}, u32[]{:S(2)}, u32[]{:S(2)}) %all-to-all-start.4) | async-done | bytes 655392 | tf_op jit(solution)/shard_map/all_to_all | solution.py:375
  155.2 0.8 copy-done.4
  156.0 2.7 %curvature.5 = f32[1,128]{1,0:T(1,128)} custom-call(f32[4]{0:T(128)} %dynamic-slice_reduce_fusion.refs_0_, f32[1280,128]{1,0:T(8,128)} %bitcast.47, bf16[4,256,256]{2,1,0:T(8,128)(2,1)} %get-tuple-element.78.refs_2_, bf16[4,256,256]{2,1,0:T(8,128)(2,1)} %get-tuple-element.79.refs_3_, s32[4,128]{1,0:T(4,128)} %refs_4_.5, f32[1,128]{1,0:T(1,128)} %curvature.4.refs_5_), custom_call_target="tpu_custom_call" | custom-call | flops 625000000 | tf_op jit(solution)/shard_map/curvature/pallas_call | solution.py:440
  158.8 0.7 add_add_fusion.2
  159.4 0.5 slice_bitcast_fusion
  (42 shorter events, 0.1 us)
Async XLA Ops:
  0.0 9.1 %copy-start = (f32[8,3]{0,1:T(4,128)S(1)}, f32[8,3]{0,1:T(4,128)}, u32[]{:S(2)}) copy-start(f32[8,3]{0,1:T(4,128)} %param.9) | copy-start | bytes 292
  0.0 9.0 %copy-start.12 = (s32[512,3]{0,1:T(4,128)S(1)}, s32[512,3]{0,1:T(4,128)}, u32[]{:S(2)}) copy-start(s32[512,3]{0,1:T(4,128)} %param.12) | copy-start | bytes 18436
  0.0 9.8 %copy-start.15 = (s32[8]{0:T(128)S(1)}, s32[8]{0:T(128)}, u32[]{:S(2)}) copy-start(s32[8]{0:T(128)} %param.10) | copy-start | bytes 100
  7.6 30.6 %collective-permute-start.5 = (f32[3,2,512,512]{3,2,1,0:T(8,128)}, f32[3,2,512,512]{3,2,1,0:T(8,128)}, u32[]{:S(2)}, u32[]{:S(2)}) collective-permute-start(f32[3,2,512,512]{3,2,1,0:T(8,128)} %get-tuple-element.60), channel_id=1, source_target_pairs={{0,1},{1,0},{2,3},{3,2},{4,5},{5,4},{6,7},{7,6},{8,9},{9,8},{10,11... | collective-permute-start | bytes 18874376 | tf_op jit(solution)/shard_map/ppermute | solution.py:515
  9.0 20.0 %collective-permute-start.4 = (f32[8,512]{1,0:T(8,128)S(1)}, f32[8,512]{1,0:T(8,128)S(1)}, u32[]{:S(2)}, u32[]{:S(2)}) collective-permute-start(f32[8,512]{1,0:T(8,128)S(1)} %pad.9), channel_id=1, source_target_pairs={{0,1},{1,0},{2,3},{3,2},{4,5},{5,4},{6,7},{7,6},{8,9},{9,8},{10,11... | collective-permute-start | bytes 49160 | tf_op jit(solution)/shard_map/ppermute | solution.py:517
  21.2 14.3 %all-to-all-start.1 = ((f32[16,8,128]{2,1,0:T(8,128)}), f32[16,8,128]{2,1,0:T(8,128)S(1)}, u32[]{:S(2)}, u32[]{:S(2)}) async-start(f32[16,8,128]{2,1,0:T(8,128)} %broadcast_in_dim.26), calls=%async_computation.1 | async-start | bytes 131072 | tf_op jit(solution)/shard_map/all_to_all | solution.py:520
  35.5 0.6 copy-start.11
  47.4 23.1 %copy-start.1 = (bf16[3,1024,512]{2,1,0:T(8,128)(2,1)}, bf16[3,1024,512]{2,1,0:T(8,128)(2,1)S(1)}, u32[]{:S(2)}) copy-start(bf16[3,1024,512]{2,1,0:T(8,128)(2,1)S(1)} %get-tuple-element.61.refs_3_) | copy-start | bytes 9437188
  47.4 11.8 %collective-permute-start.6 = (f32[16,40,128]{2,1,0:T(8,128)}, f32[16,40,128]{2,1,0:T(8,128)}, u32[]{:S(2)}, u32[]{:S(2)}) collective-permute-start(f32[16,40,128]{2,1,0:T(8,128)} %bitcast.62), channel_id=1, source_target_pairs={{0,2},{2,4},{4,6},{6,0},{1,3},{3,5},{5,7},{7,1},{8,10},{10,12},{12... | collective-permute-start | bytes 983048 | tf_op jit(solution)/shard_map/ppermute | solution.py:286
  47.7 11.5 %collective-permute-start.7 = (f32[16,40,128]{2,1,0:T(8,128)}, f32[16,40,128]{2,1,0:T(8,128)}, u32[]{:S(2)}, u32[]{:S(2)}) collective-permute-start(f32[16,40,128]{2,1,0:T(8,128)} %bitcast.61), channel_id=1, source_target_pairs={{0,6},{2,0},{4,2},{6,4},{1,7},{3,1},{5,3},{7,5},{8,14},{10,8},{12,... | collective-permute-start | bytes 983048 | tf_op jit(solution)/shard_map/ppermute | solution.py:290
  50.1 26.8 %collective-permute-start.10 = (f32[32,40,128]{2,1,0:T(8,128)}, f32[32,40,128]{2,1,0:T(8,128)S(1)}, u32[]{:S(2)}, u32[]{:S(2)}) collective-permute-start(f32[32,40,128]{2,1,0:T(8,128)} %bitcast.60), channel_id=1, source_target_pairs={{0,2},{2,4},{4,6},{6,0},{1,3},{3,5},{5,7},{7,1},{8,10},{10,12},{12... | collective-permute-start | bytes 1966088 | tf_op jit(solution)/shard_map/ppermute | solution.py:286
  50.1 26.8 %collective-permute-start.11 = (f32[32,40,128]{2,1,0:T(8,128)}, f32[32,40,128]{2,1,0:T(8,128)S(1)}, u32[]{:S(2)}, u32[]{:S(2)}) collective-permute-start(f32[32,40,128]{2,1,0:T(8,128)} %bitcast.59), channel_id=1, source_target_pairs={{0,6},{2,0},{4,2},{6,4},{1,7},{3,1},{5,3},{7,5},{8,14},{10,8},{12,... | collective-permute-start | bytes 1966088 | tf_op jit(solution)/shard_map/ppermute | solution.py:290
  61.4 22.8 %collective-permute-start.8 = (f32[32,40,128]{2,1,0:T(8,128)}, f32[32,40,128]{2,1,0:T(8,128)}, u32[]{:S(2)}, u32[]{:S(2)}) collective-permute-start(f32[32,40,128]{2,1,0:T(8,128)} %get-tuple-element.67.refs_4_), channel_id=1, source_target_pairs={{0,2},{2,4},{4,6},{6,0},{1,3},{3,5},{5,7},{7,1},{8,10},{10,12},{12... | collective-permute-start | bytes 1966088 | tf_op jit(solution)/shard_map/ppermute | solution.py:286
  61.4 22.8 %collective-permute-start.9 = (f32[32,40,128]{2,1,0:T(8,128)}, f32[32,40,128]{2,1,0:T(8,128)}, u32[]{:S(2)}, u32[]{:S(2)}) collective-permute-start(f32[32,40,128]{2,1,0:T(8,128)} %get-tuple-element.68), channel_id=1, source_target_pairs={{0,6},{2,0},{4,2},{6,4},{1,7},{3,1},{5,3},{7,5},{8,14},{10,8},{12,... | collective-permute-start | bytes 1966088 | tf_op jit(solution)/shard_map/ppermute | solution.py:290
  76.9 0.9 copy-start.5
  76.9 1.1 copy-start.6
  80.7 17.8 %collective-permute-start.12 = (f32[32,40,128]{2,1,0:T(8,128)}, f32[32,40,128]{2,1,0:T(8,128)}, u32[]{:S(2)}, u32[]{:S(2)}) collective-permute-start(f32[32,40,128]{2,1,0:T(8,128)} %get-tuple-element.81), channel_id=1, source_target_pairs={{0,2},{2,4},{4,6},{6,0},{1,3},{3,5},{5,7},{7,1},{8,10},{10,12},{12... | collective-permute-start | bytes 1966088 | tf_op jit(solution)/shard_map/ppermute | solution.py:286
  80.7 17.9 %collective-permute-start.13 = (f32[32,40,128]{2,1,0:T(8,128)}, f32[32,40,128]{2,1,0:T(8,128)}, u32[]{:S(2)}, u32[]{:S(2)}) collective-permute-start(f32[32,40,128]{2,1,0:T(8,128)} %get-tuple-element.82), channel_id=1, source_target_pairs={{0,6},{2,0},{4,2},{6,4},{1,7},{3,1},{5,3},{7,5},{8,14},{10,8},{12,... | collective-permute-start | bytes 1966088 | tf_op jit(solution)/shard_map/ppermute | solution.py:290
  87.4 22.1 %all-to-all-start.2 = ((f32[32,1,40,128]{3,2,1,0:T(8,128)}), f32[32,1,40,128]{3,2,1,0:T(8,128)}, u32[]{:S(2)}, u32[]{:S(2)}) async-start(f32[32,1,40,128]{3,2,1,0:T(8,128)} %get-tuple-element.77), calls=%async_computation.2 | async-start | bytes 1310720 | tf_op jit(solution)/shard_map/all_to_all | solution.py:375
  98.6 14.7 %copy-start.8 = (f32[32,40,128]{2,1,0:T(8,128)S(1)}, f32[32,40,128]{2,1,0:T(8,128)}, u32[]{:S(2)}) copy-start(f32[32,40,128]{2,1,0:T(8,128)} %get-tuple-element.84) | copy-start | bytes 1966084
  98.6 17.4 %copy-start.7 = (f32[32,40,128]{2,1,0:T(8,128)S(1)}, f32[32,40,128]{2,1,0:T(8,128)}, u32[]{:S(2)}) copy-start(f32[32,40,128]{2,1,0:T(8,128)} %get-tuple-element.76.refs_5_) | copy-start | bytes 1966084
  98.6 34.4 %copy-start.3 = (f32[1280,128]{1,0:T(8,128)S(1)}, f32[1280,128]{1,0:T(8,128)}, u32[]{:S(2)}) copy-start(f32[1280,128]{1,0:T(8,128)} %get-tuple-element.83) | copy-start | bytes 1966084
  109.5 24.5 %all-to-all-start.3 = ((f32[32,2,40,128]{3,2,1,0:T(8,128)}), f32[32,2,40,128]{3,2,1,0:T(8,128)S(1)}, u32[]{:S(2)}, u32[]{:S(2)}) async-start(f32[32,2,40,128]{3,2,1,0:T(8,128)} %place_slots.3.refs_5_), calls=%async_computation.3 | async-start | bytes 2621440 | tf_op jit(solution)/shard_map/all_to_all | solution.py:375
  113.2 32.3 %copy-start.14 = (f32[8,128]{1,0:T(8,128)S(1)}, f32[8,128]{1,0:T(8,128)}, u32[]{:S(2)}) copy-start(f32[8,128]{1,0:T(8,128)} %get-tuple-element.56) | copy-start | bytes 12292
  113.3 16.7 %collective-permute-start.15 = (f32[32,40,128]{2,1,0:T(8,128)S(1)}, f32[32,40,128]{2,1,0:T(8,128)S(1)}, u32[]{:S(2)}, u32[]{:S(2)}) collective-permute-start(f32[32,40,128]{2,1,0:T(8,128)S(1)} %copy-done.8), channel_id=1, source_target_pairs={{0,6},{2,0},{4,2},{6,4},{1,7},{3,1},{5,3},{7,5},{8,14},{10,8},{12,... | collective-permute-start | bytes 1966088 | tf_op jit(solution)/shard_map/ppermute | solution.py:290
  116.0 17.0 %collective-permute-start.14 = (f32[32,40,128]{2,1,0:T(8,128)S(1)}, f32[32,40,128]{2,1,0:T(8,128)S(1)}, u32[]{:S(2)}, u32[]{:S(2)}) collective-permute-start(f32[32,40,128]{2,1,0:T(8,128)S(1)} %copy-done.7), channel_id=1, source_target_pairs={{0,2},{2,4},{4,6},{6,0},{1,3},{3,5},{5,7},{7,1},{8,10},{10,12},{12... | collective-permute-start | bytes 1966088 | tf_op jit(solution)/shard_map/ppermute | solution.py:286
  134.0 15.0 %copy-start.2 = (f32[32,2,40,128]{3,2,1,0:T(8,128)}, f32[32,2,40,128]{3,2,1,0:T(8,128)S(1)}, u32[]{:S(2)}) copy-start(f32[32,2,40,128]{3,2,1,0:T(8,128)S(1)} %all-to-all-done.3) | copy-start | bytes 3932164
  134.0 21.2 %all-to-all-start.4 = ((f32[32,40,128]{2,1,0:T(8,128)}), f32[32,40,128]{2,1,0:T(8,128)S(1)}, u32[]{:S(2)}, u32[]{:S(2)}) async-start(f32[32,40,128]{2,1,0:T(8,128)} %add_add_fusion.1), calls=%async_computation.4 | async-start | bytes 1310720 | tf_op jit(solution)/shard_map/all_to_all | solution.py:375
  149.0 9.7 %copy-start.13 = (f32[1,128]{1,0:T(1,128)S(1)}, f32[1,128]{1,0:T(1,128)}, u32[]{:S(2)}) copy-start(f32[1,128]{1,0:T(1,128)} %curvature.3.refs_5_) | copy-start | bytes 1540
  155.2 0.8 copy-start.4

commit v3 on v2

--- a/solution.py
+++ b/solution.py
@@ -27,8 +27,8 @@
 BLOCKS = 128
 
 
-def params(**more):
-    return pltpu.CompilerParams(vmem_limit_bytes=56 << 20, **more)
+def params(mebibytes):
+    return pltpu.CompilerParams(vmem_limit_bytes=mebibytes << 20)
 
 
 ANY = pl.BlockSpec(memory_space=pl.ANY)
@@ -74,8 +74,7 @@
     seat = jnp.where(away == 1, 0, jnp.where(away == 3, 1, 2))
 
     def row_of(chunk, within):
-        half = within // (OWNERS // 2)
-        opposite = jnp.where(chunk == 0, within, OWNERS // 2 * (1 + chunk + half) + within)
+        opposite = OWNERS * chunk + within
         apart = 3 * OWNERS * (1 + chunk) + seat * OWNERS + within
         spare = 12 * OWNERS + jnp.where(away == 2, 0, 1 + seat) * OWNERS + within
         return jnp.where(chunk == 3, spare, jnp.where(away == 2, opposite, apart))
@@ -124,15 +123,15 @@
         ),
         in_specs=[SMEM, VMEM],
         out_specs=(VMEM, VMEM, VMEM),
-        compiler_params=params(),
+        compiler_params=params(8),
         cost_estimate=cost(2),
         interpret=INTERPRET,
         name="find_points",
     )(plane, table)
 
 
-def split_kernel(core_ref, space_ref, own_ref, send_ref, wide_ref):
-    core = core_ref[0]
+def split_kernel(dtype, core_ref, space_ref, out_ref, wide_ref):
+    core = core_ref[0] if dtype == bf16 else 1 - core_ref[0]
     depth, rows, width = space_ref.shape
     half = rows // 12
     pitch = wide_ref.shape[0] // depth
@@ -143,29 +142,24 @@
     for matrix in range(3):
         for part in range(2):
             for r in range(half):
+                at = matrix * (rows // 3) + 2 * (half * core + r) + part
                 lanes = slice(r * width, (r + 1) * width)
-                own_at = matrix * (rows // 3) + 2 * (half * core + r) + part
-                send_at = matrix * (rows // 3) + 2 * (half * (1 - core) + r) + part
-                own = wide_ref[pl.ds(own_at, depth, stride=pitch), :]
-                own_ref[matrix, part, :, lanes] = own.astype(bf16)
-                send_ref[matrix, part, :, lanes] = wide_ref[pl.ds(send_at, depth, stride=pitch), :]
-
-
-def split_rows(space, core):
+                out_ref[matrix, part, :, lanes] = wide_ref[pl.ds(at, depth, stride=pitch), :].astype(dtype)
+
+
+def split_rows(space, core, dtype, microseconds):
     depth, rows, width = space.shape
     block = min(depth, 128)
     lanes = rows // 12 * width
-    shape = (3, 2, depth, lanes)
-    spec = pl.BlockSpec((3, 2, block, lanes), lambda i: (0, 0, i, 0))
     return pl.pallas_call(
-        split_kernel,
+        lambda *refs: split_kernel(dtype, *refs),
         grid=(depth // block,),
-        out_shape=(jax.ShapeDtypeStruct(shape, bf16), jax.ShapeDtypeStruct(shape, f32)),
+        out_shape=jax.ShapeDtypeStruct((3, 2, depth, lanes), dtype),
         in_specs=[SMEM, pl.BlockSpec((block, rows, width), lambda i: (i, 0, 0))],
-        out_specs=(spec, spec),
+        out_specs=pl.BlockSpec((3, 2, block, lanes), lambda i: (0, 0, i, 0)),
         scratch_shapes=[pltpu.VMEM((block * (rows + 8), width), f32)],
-        compiler_params=params(),
-        cost_estimate=cost(8),
+        compiler_params=params(16),
+        cost_estimate=cost(microseconds),
         interpret=INTERPRET,
         name="split_rows",
     )(core, space)
@@ -274,7 +268,7 @@
         + [ANY] * len(after),
         out_specs=tuple(specs),
         scratch_shapes=[pltpu.VMEM((6 * (high - low), 2 * depth2), bf16)],
-        compiler_params=params(),
+        compiler_params=params(20),
         cost_estimate=cost(microseconds),
         interpret=INTERPRET,
         name="fourier",
@@ -291,7 +285,9 @@
 
 
 def first_hop(near, far):
-    return to_right(near), to_left(far)
+    near = to_right(near)
+    far = to_left(far)
+    return near, far
 
 
 def add_kernel(chunks, waits, near_ref, far_ref, *refs):
@@ -317,7 +313,7 @@
         in_specs=[whole, whole] + [lower, upper] * chunks + [ANY] * len(after),
         out_specs=(lower, upper) * chunks,
         input_output_aliases={2 + i: i for i in range(2 * chunks)},
-        compiler_params=params(),
+        compiler_params=params(8),
         cost_estimate=cost(1.5 * chunks),
         interpret=INTERPRET,
         name="add_arrived",
@@ -364,7 +360,7 @@
         in_specs=[SMEM, SMEM] + [VMEM] * (len(tables) + 3) + [ANY] * len(after),
         out_specs=(VMEM, VMEM) if keep_table else (VMEM,),
         scratch_shapes=[] if keep_table else [pltpu.VMEM(table.shape, f32)],
-        compiler_params=params(),
+        compiler_params=params(14),
         cost_estimate=cost(3),
         interpret=INTERPRET,
         name="place_slots",
@@ -380,8 +376,9 @@
     return high, (value - high.astype(f32)).astype(bf16)
 
 
-def curvature_kernel(first, units, weight_ref, field_ref, turn_ref, back_ref, occupied_ref, *refs):
+def curvature_kernel(first, units, adding, weight_ref, field_ref, turn_ref, back_ref, occupied_ref, *refs):
     out_ref = refs[-1]
+    previous = refs[0][...] if adding else 0.0
     unit = pl.program_id(0)
     sources = field_ref.shape[0] // (units * 40)
     n = field_ref.shape[1]
@@ -429,16 +426,16 @@
     weight = weight_ref[s]
     lane = iota((1, BLOCKS), 1)
     result = jnp.where((lane == s) & (weight > 0.0), weight * berry, 0.0)
-    before = jnp.where(unit == 0, 0.0, out_ref[...])
+    before = jnp.where(unit == 0, previous, out_ref[...])
     out_ref[...] = result + before
 
 
-def curvature(first, units, weight, arrived, vectors, adjoint, occupied, after=()):
+def curvature(first, units, weight, arrived, vectors, adjoint, occupied, previous=(), after=()):
     width = arrived.shape[-1]
     flat = arrived.reshape(-1, width)
     matrix = pl.BlockSpec((1, 2 * width, 2 * width), lambda u: (first + u, 0, 0))
     return pl.pallas_call(
-        lambda *refs: curvature_kernel(first, units, *refs),
+        lambda *refs: curvature_kernel(first, units, len(previous), *refs),
         grid=(units,),
         out_shape=jax.ShapeDtypeStruct((1, BLOCKS), f32),
         in_specs=[
@@ -448,13 +445,14 @@
             matrix,
             pl.BlockSpec(occupied.shape, lambda u: (0, 0)),
         ]
+        + [pl.BlockSpec((1, BLOCKS), lambda u: (0, 0))] * len(previous)
         + [ANY] * len(after),
         out_specs=pl.BlockSpec((1, BLOCKS), lambda u: (0, 0)),
-        compiler_params=params(),
+        compiler_params=params(12),
         cost_estimate=cost(2.5 * units),
         interpret=INTERPRET,
         name="curvature",
-    )(weight, flat, vectors, adjoint, occupied, *after)
+    )(weight, flat, vectors, adjoint, occupied, *previous, *after)
 
 
 def vector_kernel(eigvecs_ref, turn_ref, back_ref, wide_ref):
@@ -490,7 +488,7 @@
         in_specs=[pl.BlockSpec((1, 2 * width, width), lambda i: (i, 0, 0))],
         out_specs=(square, square),
         scratch_shapes=[pltpu.VMEM((2 * width, width), f32)],
-        compiler_params=params(),
+        compiler_params=params(4),
         cost_estimate=cost(2),
         interpret=INTERPRET,
         name="vector_matrices",
@@ -508,16 +506,16 @@
     own_count = lax.dynamic_slice_in_dim(counts, row, 1, 0).astype(f32)[:, None]
     mine = jnp.concatenate([own_base, own_count, block_order.astype(f32)[:, None]], axis=1)
     mine = jnp.pad(mine, ((0, 0), (0, BLOCKS - 5)))
-    line = lax.all_to_all(jnp.broadcast_to(mine[None], (8, 1, BLOCKS)), ROW, 0, 0, tiled=True)
-
-    own, send = split_rows(real_space.reshape(depth, 6 * slab, width), core_ref)
+    space = real_space.reshape(depth, 6 * slab, width)
     swap = [(0, 1), (1, 0)]
+    send = split_rows(space, core_ref, f32, 5)
     other = lax.ppermute(send, "row_1", swap)
     own_coords = jnp.pad(lattice.T.astype(f32), ((0, 5), (0, 0)))
     coords = jnp.concatenate([own_coords, lax.ppermute(own_coords, "row_1", swap)], axis=1)
 
-    lines = jnp.broadcast_to(line.reshape(1, 8, BLOCKS), (16, 8, BLOCKS))
-    table = lax.all_to_all(lines, KA, 0, 0, tiled=True).reshape(BLOCKS, BLOCKS)
+    table = lax.all_to_all(jnp.broadcast_to(mine[None], (BLOCKS, 1, BLOCKS)), KA_ROW, 0, 0, tiled=True)
+    table = table.reshape(BLOCKS, BLOCKS)
+    own = split_rows(space, core_ref, bf16, 4)
     turning, back = vector_matrices(eigvecs)
     points, slots, weights = find_points(table, plane_ref)
     position = (lax.axis_index(KA) * 8 + row).astype(jnp.int32)
@@ -526,46 +524,45 @@
     own = own.reshape(3, 2 * depth, -1)
     other = other.reshape(3, 2 * depth, -1)
     half = OWNERS // 2
-    opposite = (half, half, OWNERS, OWNERS)
     others = (OWNERS, OWNERS, OWNERS)
 
+    def sums(low, sizes, microseconds, after=(), narrowing=False):
+        return fourier(points, low, low + sum(sizes), sizes, coords, own, other, microseconds, after, narrowing)
+
     def rest(chunk, after):
-        low = 3 * OWNERS * (1 + chunk)
-        return fourier(points, low, low + 3 * OWNERS, others, coords, own, other, 6, after)
-
-    near0, far0, near13, far13, other = fourier(
-        points, 0, 3 * OWNERS, opposite, coords, own, other, 6, narrowing=True
-    )
+        return sums(3 * OWNERS * (1 + chunk), others, 5, after)
+
+    near0, far0, other = sums(0, (half, half), 5, (), True)
     hop0 = first_hop(near0, far0)
-    hop13 = first_hop(near13, far13)
-    right0, left0, keep0 = rest(0, ())
+    near1, far1, near3, far3 = sums(OWNERS, (half,) * 4, 4, (near0,))
+    hop1 = first_hop(near1, far1)
+    right0, left0, keep0 = rest(0, (near1,))
     right0, left0 = add_arrived(*hop0, (right0, left0))
     ring0 = second_hop(right0, left0)
     right1, left1, keep1 = rest(1, (right0,))
-    right3, left3, keep3 = rest(2, (keep1,))
-    right1, left1, right3, left3 = add_arrived(*hop13, (right1, left1, right3, left3))
+    right1, left1 = add_arrived(*hop1, (right1, left1))
     ring1 = second_hop(right1, left1)
-    ring3 = second_hop(right3, left3)
+    hop3 = first_hop(near3, far3)
+    right3, left3, keep3 = rest(2, (right1,))
 
     def further(_):
         low = 12 * OWNERS
-        near, far, right, left, keep = fourier(
-            points, low, low + 4 * OWNERS, (half, half) + others, coords, own, other, 8
-        )
+        near, far, right, left, keep = sums(low, (half, half) + others, 8)
         right, left = second_hop(*add_arrived(*first_hop(near, far), (right, left)))
         return keep + right + left
 
     extra = lax.cond(slots[0, 0] > 2 * OWNERS, further, lambda _: jnp.zeros(keep0.shape, f32), 0)
 
-    placed1, sum0 = place_slots((1,), plane_ref, slots, [], (keep0, *ring0), True, (right3,))
+    placed1, sum0 = place_slots((1,), plane_ref, slots, [], (keep0, *ring0), True, (keep3,))
     unit1 = to_owners(placed1)
     (placed23,) = place_slots((2, 3), plane_ref, slots, [sum0, extra], (keep1, *ring1), False)
     unit23 = to_owners(placed23)
-    curve1 = curvature(1, 1, weight, unit1, turning, back, occupied, (placed23,))
+    right3, left3 = add_arrived(*hop3, (right3, left3), (placed23,))
+    ring3 = second_hop(right3, left3)
+    curve1 = curvature(1, 1, weight, unit1, turning, back, occupied, (), (right3,))
     unit0 = to_owners(keep3 + ring3[0] + ring3[1])
     curve23 = curvature(2, 2, weight, unit23, turning, back, occupied, (curve1,))
-    curve0 = curvature(0, 1, weight, unit0, turning, back, occupied, (curve23,))
-    return (curve1 + curve23 + curve0)[0, :SUB]
+    return curvature(0, 1, weight, unit0, turning, back, occupied, (curve23,)).reshape(BLOCKS)[:SUB]
 
 
 def solution(mesh):

time: 161 us -> 162 us (level)
  Pallas kernels: 62.9 us -> 51.1 us
  local copies, waits for them, and re-layouts: 6.42 us -> 16.9 us
  blocking collectives: 9.29 us -> 0 us
  waiting for transfers between devices: 33.6 us -> 41.1 us
  starting transfers between devices: 43.7 us -> 48.4 us
    unnamed x28 -> x46, local copies, waits for them, and re-layouts: 2.58 us -> 13.3 us
    all_to_all x1 -> x0, blocking collectives: 9.29 us -> none  [body(): lax.all_to_all(jnp.broadcast_to(mine[None], (8, 1, BLOCKS)), ROW, 0, 0, t...]
    ppermute x5 -> x6, waiting for transfers between devices: 3.95 us -> 12.9 us  [to_right(): return lax.ppermute(value, 'row_0', [(i, (i + 1) % NX) for i in range(NX)])]
    pallas_call x4 -> x5, Pallas kernels: 17.2 us -> 11.8 us  [the longest x2 6.04 us: split_rows(): pl.pallas_call(lambda *refs: split_kernel(dtype, *refs), grid=(depth // b...]
    all_to_all x1, waiting for transfers between devices: 6.51 us -> 3.2 us  [body(): lax.all_to_all(jnp.broadcast_to(mine[None], (BLOCKS, 1, BLOCKS)), KA_ROW,...]
    pallas_call x1, Pallas kernels: 3.25 us -> 0.56 us  [vector_matrices(): pl.pallas_call(vector_kernel, grid=(slots,), out_shape=(shape, shape), in...]
    all_to_all x1, starting transfers between devices: 7.77 us -> 10.2 us  [body(): lax.all_to_all(jnp.broadcast_to(mine[None], (BLOCKS, 1, BLOCKS)), KA_ROW,...]
    pallas_call x2 -> x3, Pallas kernels: 4.94 us -> 3.14 us  [add_arrived(): pl.pallas_call(lambda *refs: add_kernel(chunks, len(after), *refs), grid=...]
  transfers between devices with their start and end apart: 16 -> 18, of which waited for: 6 -> 6; matrix products, arithmetic and copies ran while one was open for 3% -> 3% of each run, Pallas kernels for 27% -> 24%
where the time goes in v3:
time: 162 us; the launch traced here: 161 us
  Pallas kernels  51.1 us (32%)
  starting transfers between devices  48.4 us (30%)
  waiting for transfers between devices  41.1 us (25%)
  local copies, waits for them, and re-layouts  16.9 us (10%)
  between operations  2.29 us (1%)
    pallas_call x5, Pallas kernels, fourier(): pl.pallas_call(lambda *refs: fourier_kernel(low, high, int(narrowing), le...  29.3 us
    all_to_all x3, starting transfers between devices, to_owners(): return lax.all_to_all(value, PLANE, split_axis=0, concat_axis=0, tiled=True)  20.6 us
    ppermute x6, waiting for transfers between devices, to_left(): return lax.ppermute(value, 'row_0', [(i, (i - 1) % NX) for i in range(NX)])  14.6 us
    ppermute x6, starting transfers between devices, to_left(): return lax.ppermute(value, 'row_0', [(i, (i - 1) % NX) for i in range(NX)])  13.4 us
    unnamed x46, local copies, waits for them, and re-layouts  13.3 us
    ppermute x6, waiting for transfers between devices, to_right(): return lax.ppermute(value, 'row_0', [(i, (i + 1) % NX) for i in range(NX)])  12.9 us
    all_to_all x3, waiting for transfers between devices, to_owners(): return lax.all_to_all(value, PLANE, split_axis=0, concat_axis=0, tiled=True)  10.4 us
    all_to_all x1, starting transfers between devices, body(): lax.all_to_all(jnp.broadcast_to(mine[None], (BLOCKS, 1, BLOCKS)), KA_ROW,...  10.2 us
  transfers between devices with their start and end apart: 18, of which 6 were waited for; matrix products, arithmetic and copies ran while one was open for 3% of the time, Pallas kernels for 24%

profile of v3, /device:TPU:1, one launch (start us, length us, event | category | flops | bytes accessed | tf_op | source)
XLA Modules:
  0.0 160.9 jit_solution(6905965130133239691)
XLA Ops:
  0.0 2.8 %copy-done.1 = bf16[512,3,8,2,128]{4,3,2,1,0:T(2,128)(2,1)S(1)} copy-done((bf16[512,3,8,2,128]{4,3,2,1,0:T(2,128)(2,1)S(1)}, bf16[512,3,8,2,128]{4,3,2,1,0:T(2,128)(2,1)}, u32[]{:S(2)}) %copy-start.1) | copy-done | bytes 6291480
  2.8 3.7 %split_rows.3 = f32[3,2,512,512]{3,2,1,0:T(8,128)} custom-call(s32[1]{0:T(128)} %bitcast.10.refs_0_, bf16[512,48,128]{2,1,0:T(8,128)(2,1)S(1)} %bitcast.37), custom_call_target="tpu_custom_call" | custom-call | flops 1250000000 | tf_op jit(solution)/shard_map/split_rows/pallas_call | solution.py:154
  6.5 1.4 collective-permute-start.5
  8.6 0.6 dynamic_slice.10
  10.0 0.7 broadcast_in_dim.17
  10.7 10.2 %all-to-all-start = ((f32[128,1,128]{2,1,0:T(1,128)}), f32[128,1,128]{2,1,0:T(1,128)S(1)}, u32[]{:S(2)}, u32[]{:S(2)}) async-start(f32[128,1,128]{2,1,0:T(1,128)} %broadcast_in_dim.17), calls=%async_computation | async-start | bytes 131072 | tf_op jit(solution)/shard_map/all_to_all | solution.py:516
  21.0 1.1 collective-permute-start.4
  22.1 2.8 %copy-done.2 = bf16[512,3,8,2,128]{4,3,2,1,0:T(2,128)(2,1)S(1)} copy-done((bf16[512,3,8,2,128]{4,3,2,1,0:T(2,128)(2,1)S(1)}, bf16[512,3,8,2,128]{4,3,2,1,0:T(2,128)(2,1)}, u32[]{:S(2)}) %copy-start.2) | copy-done | bytes 6291480
  24.9 2.3 %split_rows.2 = bf16[3,2,512,512]{3,2,1,0:T(8,128)(2,1)S(1)} custom-call(s32[1]{0:T(128)} %bitcast.10.refs_0_, bf16[512,48,128]{2,1,0:T(8,128)(2,1)S(1)} %bitcast.38), custom_call_target="tpu_custom_call" | custom-call | flops 1000000000 | tf_op jit(solution)/shard_map/split_rows/pallas_call | solution.py:154
  27.3 3.2 %all-to-all-done = f32[128,1,128]{2,1,0:T(1,128)S(1)} async-done(((f32[128,1,128]{2,1,0:T(1,128)}), f32[128,1,128]{2,1,0:T(1,128)S(1)}, u32[]{:S(2)}, u32[]{:S(2)}) %all-to-all-start) | async-done | bytes 65568 | tf_op jit(solution)/shard_map/all_to_all | solution.py:516
  30.5 0.7 find_points.1
  31.2 6.3 %fourier.7 = (f32[640,128]{1,0:T(8,128)S(1)}, f32[640,128]{1,0:T(8,128)S(1)}, bf16[3,1024,512]{2,1,0:T(8,128)(2,1)S(1)}) custom-call(f32[512,128]{1,0:T(8,128)S(1)} %get-tuple-element.57.refs_0_, f32[8,1024]{1,0:T(8,128)S(1)} %pad_maximum_fusion.refs_1_, bf16[3,1024,512]{2,1,0:T(8,128)(2,1)S(1)} %bitcast.66, f32[3,1024,512]{2,1,0:T(8,128)} %bitcast.13.refs_3_), custom_call_target="tpu_custom_call" | custom-call | flops 1250000000 | tf_op jit(solution)/shard_map/fourier/pallas_call | solution.py:258
  37.9 2.4 %collective-permute-start.9 = (f32[16,40,128]{2,1,0:T(8,128)S(1)}, f32[16,40,128]{2,1,0:T(8,128)S(1)}, u32[]{:S(2)}, u32[]{:S(2)}) collective-permute-start(f32[16,40,128]{2,1,0:T(8,128)S(1)} %bitcast.62), channel_id=1, source_target_pairs={{0,6},{2,0},{4,2},{6,4},{1,7},{3,1},{5,3},{7,5},{8,14},{10,8},{12,... | collective-permute-start | bytes 983048 | tf_op jit(solution)/shard_map/ppermute | solution.py:284
  40.3 6.2 %fourier.8 = (f32[640,128]{1,0:T(8,128)S(1)}, f32[640,128]{1,0:T(8,128)S(1)}, f32[640,128]{1,0:T(8,128)S(1)}, f32[640,128]{1,0:T(8,128)S(1)}) custom-call(f32[512,128]{1,0:T(8,128)S(1)} %get-tuple-element.57.refs_0_, f32[8,1024]{1,0:T(8,128)S(1)} %pad_maximum_fusion.refs_1_, bf16[3,1024,512]{2,1,0:T(8,128)(2,1)} %bitcast.67, ...), custom_call_target="tpu_custom_call" | custom-call | flops 1000000000 | tf_op jit(solution)/shard_map/fourier/pallas_call | solution.py:258
  46.5 0.7 copy-done.14
  47.2 0.7 copy-done.15
  48.0 5.1 %fourier.9 = (f32[1280,128]{1,0:T(8,128)S(1)}, f32[1280,128]{1,0:T(8,128)S(1)}, f32[1280,128]{1,0:T(8,128)S(1)}) custom-call(f32[512,128]{1,0:T(8,128)S(1)} %get-tuple-element.57.refs_0_, f32[8,1024]{1,0:T(8,128)S(1)} %pad_maximum_fusion.refs_1_, bf16[3,1024,512]{2,1,0:T(8,128)(2,1)S(1)} %bitcast.69, bf16[3,1024,512]{2,1,0:T(8,128)(2,1)S(1)} %get-tuple-element.58.refs_3_, ...), custom_call_target="tpu_custom_call" | custom-call | flops 1250000000 | tf_op jit(solution)/shard_map/fourier/pallas_call | solution.py:258
  53.3 2.7 %collective-permute-start.13 = (f32[32,40,128]{2,1,0:T(8,128)S(1)}, f32[32,40,128]{2,1,0:T(8,128)S(1)}, u32[]{:S(2)}, u32[]{:S(2)}) collective-permute-start(f32[32,40,128]{2,1,0:T(8,128)S(1)} %get-tuple-element.76), channel_id=1, source_target_pairs={{0,6},{2,0},{4,2},{6,4},{1,7},{3,1},{5,3},{7,5},{8,14},{10,8},{12,... | collective-permute-start | bytes 1966088 | tf_op jit(solution)/shard_map/ppermute | solution.py:284
  56.0 2.7 %collective-permute-start.7 = (f32[16,40,128]{2,1,0:T(8,128)S(1)}, f32[16,40,128]{2,1,0:T(8,128)S(1)}, u32[]{:S(2)}, u32[]{:S(2)}) collective-permute-start(f32[16,40,128]{2,1,0:T(8,128)S(1)} %bitcast.61), channel_id=1, source_target_pairs={{0,6},{2,0},{4,2},{6,4},{1,7},{3,1},{5,3},{7,5},{8,14},{10,8},{12,... | collective-permute-start | bytes 983048 | tf_op jit(solution)/shard_map/ppermute | solution.py:284
  58.6 6.0 %fourier.10 = (f32[1280,128]{1,0:T(8,128)S(1)}, f32[1280,128]{1,0:T(8,128)}, f32[1280,128]{1,0:T(8,128)S(1)}) custom-call(f32[512,128]{1,0:T(8,128)S(1)} %get-tuple-element.57.refs_0_, f32[8,1024]{1,0:T(8,128)S(1)} %pad_maximum_fusion.refs_1_, bf16[3,1024,512]{2,1,0:T(8,128)(2,1)S(1)} %bitcast.70, bf16[3,1024,512]{2,1,0:T(8,128)(2,1)S(1)} %get-tuple-element.58.refs_3_, ...), custom_call_target="tpu_custom_call" | custom-call | flops 1250000000 | tf_op jit(solution)/shard_map/fourier/pallas_call | solution.py:258
  64.6 11.8 %collective-permute-done.6.refs_0_ = f32[16,40,128]{2,1,0:T(8,128)S(1)} collective-permute-done((f32[16,40,128]{2,1,0:T(8,128)S(1)}, f32[16,40,128]{2,1,0:T(8,128)S(1)}, u32[]{:S(2)}, u32[]{:S(2)}) %collective-permute-start.6) | collective-permute-done | bytes 327712 | tf_op jit(solution)/shard_map/ppermute | solution.py:280
  76.4 1.8 %add_arrived.6 = (f32[32,40,128]{2,1,0:T(8,128)S(1)}, f32[32,40,128]{2,1,0:T(8,128)}) custom-call(f32[16,40,128]{2,1,0:T(8,128)S(1)} %collective-permute-done.6.refs_0_, f32[16,40,128]{2,1,0:T(8,128)S(1)} %collective-permute-done.7.refs_1_, f32[32,40,128]{2,1,0:T(8,128)S(1)} %bitcast.42, ...), custom_call_target="tpu_custom_call", output_to_operand_aliasing={{0}: (2, {}), {1}: (3, {})} | custom-call | flops 375000000 | tf_op jit(solution)/shard_map/add_arrived/pallas_call | solution.py:309
  78.2 2.7 %collective-permute-start.15 = (f32[32,40,128]{2,1,0:T(8,128)}, f32[32,40,128]{2,1,0:T(8,128)}, u32[]{:S(2)}, u32[]{:S(2)}) collective-permute-start(f32[32,40,128]{2,1,0:T(8,128)} %get-tuple-element.79), channel_id=1, source_target_pairs={{0,6},{2,0},{4,2},{6,4},{1,7},{3,1},{5,3},{7,5},{8,14},{10,8},{12,... | collective-permute-start | bytes 1966088 | tf_op jit(solution)/shard_map/ppermute | solution.py:284
  80.9 5.8 %fourier.11 = (f32[1280,128]{1,0:T(8,128)S(1)}, f32[1280,128]{1,0:T(8,128)S(1)}, f32[1280,128]{1,0:T(8,128)S(1)}) custom-call(f32[512,128]{1,0:T(8,128)S(1)} %get-tuple-element.57.refs_0_, f32[8,1024]{1,0:T(8,128)} %copy-done.20, bf16[3,1024,512]{2,1,0:T(8,128)(2,1)S(1)} %bitcast.71, bf16[3,1024,512]{2,1,0:T(8,128)(2,1)S(1)} %get-tuple-element.58.refs_3_, ...), custom_call_target="tpu_custom_call" | custom-call | flops 1250000000 | tf_op jit(solution)/shard_map/fourier/pallas_call | solution.py:258
  86.7 2.1 %place_slots.2 = (f32[32,1,40,128]{3,2,1,0:T(8,128)}, f32[32,40,128]{2,1,0:T(8,128)S(1)}) custom-call(s32[1]{0:T(128)} %bitcast.5.place_ref.refs_0_, s32[8,128]{1,0:T(8,128)S(1)} %get-tuple-element.74.refs_1_, f32[32,40,128]{2,1,0:T(8,128)S(1)} %bitcast.58, f32[32,40,128]{2,1,0:T(8,128)S(1)} %collective-permute-done.12.refs_3_, ...), custom_call_target="tpu_custom_call" | custom-call | flops 750000000 | tf_op jit(solution)/shard_map/place_slots/pallas_call | solution.py:357
  88.8 0.8 copy-done.7
  89.6 6.7 %all-to-all-start.3 = ((f32[32,1,40,128]{3,2,1,0:T(8,128)}), f32[32,1,40,128]{3,2,1,0:T(8,128)S(1)}, u32[]{:S(2)}, u32[]{:S(2)}) async-start(f32[32,1,40,128]{3,2,1,0:T(8,128)} %get-tuple-element.84), calls=%async_computation.3 | async-start | bytes 1310720 | tf_op jit(solution)/shard_map/all_to_all | solution.py:371
  97.6 1.0 conditional.1
  97.6 0.9 broadcast.3
  98.6 2.6 %collective-permute-start.11 = (f32[16,40,128]{2,1,0:T(8,128)}, f32[16,40,128]{2,1,0:T(8,128)}, u32[]{:S(2)}, u32[]{:S(2)}) collective-permute-start(f32[16,40,128]{2,1,0:T(8,128)} %bitcast.59), channel_id=1, source_target_pairs={{0,6},{2,0},{4,2},{6,4},{1,7},{3,1},{5,3},{7,5},{8,14},{10,8},{12,... | collective-permute-start | bytes 983048 | tf_op jit(solution)/shard_map/ppermute | solution.py:284
  101.2 1.1 copy-done.6
  102.3 1.1 copy-done.8
  103.4 3.4 %place_slots.3.refs_4_ = f32[32,2,40,128]{3,2,1,0:T(8,128)} custom-call(s32[1]{0:T(128)} %bitcast.5.place_ref.refs_0_, s32[8,128]{1,0:T(8,128)S(1)} %get-tuple-element.74.refs_1_, f32[32,40,128]{2,1,0:T(8,128)S(1)} %copy-done.8, f32[32,40,128]{2,1,0:T(8,128)} %get-tuple-element.85.refs_3_, f32[32,40,128]{2,1,0:T(8,128)S(1)} %bitcast.52, ...), custom_call_target="tpu_custom_call" | custom-call | flops 750000000 | tf_op jit(solution)/shard_map/place_slots/pallas_call | solution.py:357
  106.8 2.4 %all-to-all-done.3 = f32[32,1,40,128]{3,2,1,0:T(8,128)S(1)} async-done(((f32[32,1,40,128]{3,2,1,0:T(8,128)}), f32[32,1,40,128]{3,2,1,0:T(8,128)S(1)}, u32[]{:S(2)}, u32[]{:S(2)}) %all-to-all-start.3) | async-done | bytes 655392 | tf_op jit(solution)/shard_map/all_to_all | solution.py:371
  109.3 5.5 %all-to-all-start.2 = ((f32[32,2,40,128]{3,2,1,0:T(8,128)}), f32[32,2,40,128]{3,2,1,0:T(8,128)S(1)}, u32[]{:S(2)}, u32[]{:S(2)}) async-start(f32[32,2,40,128]{3,2,1,0:T(8,128)} %place_slots.3.refs_4_), calls=%async_computation.2 | async-start | bytes 2621440 | tf_op jit(solution)/shard_map/all_to_all | solution.py:371
  114.8 1.1 copy-done.4
  115.9 1.2 add_arrived.7
  117.5 1.2 collective-permute-start.16
  118.7 14.6 %collective-permute-done.17 = f32[32,40,128]{2,1,0:T(8,128)S(1)} collective-permute-done((f32[32,40,128]{2,1,0:T(8,128)S(1)}, f32[32,40,128]{2,1,0:T(8,128)S(1)}, u32[]{:S(2)}, u32[]{:S(2)}) %collective-permute-start.17) | collective-permute-done | bytes 655392 | tf_op jit(solution)/shard_map/ppermute | solution.py:284
  133.3 1.2 collective-permute-done.16
  134.4 1.0 add_add_fusion.1
  135.4 8.4 %all-to-all-start.1 = ((f32[32,40,128]{2,1,0:T(8,128)}), f32[32,40,128]{2,1,0:T(8,128)S(1)}, u32[]{:S(2)}, u32[]{:S(2)}) async-start(f32[32,40,128]{2,1,0:T(8,128)} %add_add_fusion.1), calls=%async_computation.1 | async-start | bytes 1310720 | tf_op jit(solution)/shard_map/all_to_all | solution.py:371
  144.6 1.6 curvature.3.refs_5_
  146.2 2.6 %curvature.4.refs_5_ = f32[1,128]{1,0:T(1,128)S(1)} custom-call(f32[4]{0:T(128)S(1)} %dynamic-slice_reduce_fusion.refs_0_, f32[2560,128]{1,0:T(8,128)S(1)} %bitcast.43, bf16[4,256,256]{2,1,0:T(8,128)(2,1)S(1)} %get-tuple-element.82.refs_2_, bf16[4,256,256]{2,1,0:T(8,128)(2,1)S(1)} %get-tuple-element.83.refs_3_, s32[4,128]{1,0:T(4,128)S(1)} %copy-done.13, ...), custom_call_target="tpu_custom_call" | custom-call | flops 1250000000 | tf_op jit(solution)/shard_map/curvature/pallas_call | solution.py:437
  148.8 7.9 %all-to-all-done.1 = f32[32,40,128]{2,1,0:T(8,128)S(1)} async-done(((f32[32,40,128]{2,1,0:T(8,128)}), f32[32,40,128]{2,1,0:T(8,128)S(1)}, u32[]{:S(2)}, u32[]{:S(2)}) %all-to-all-start.1) | async-done | bytes 655392 | tf_op jit(solution)/shard_map/all_to_all | solution.py:371
  156.7 1.0 copy-done.10
  157.7 1.0 copy-done.12
  158.8 1.6 curvature.5
  (64 shorter events, 3.1 us)
Async XLA Ops:
  0.0 9.8 %copy-start = (f32[8,3]{0,1:T(4,128)S(1)}, f32[8,3]{0,1:T(4,128)}, u32[]{:S(2)}) copy-start(f32[8,3]{0,1:T(4,128)} %param.9) | copy-start | bytes 292
  0.0 2.8 %copy-start.1 = (bf16[512,3,8,2,128]{4,3,2,1,0:T(2,128)(2,1)S(1)}, bf16[512,3,8,2,128]{4,3,2,1,0:T(2,128)(2,1)}, u32[]{:S(2)}) copy-start(bf16[512,3,8,2,128]{4,3,2,1,0:T(2,128)(2,1)} %param.13) | copy-start | bytes 18874372
  2.8 5.8 %copy-start.22 = (s32[8]{0:T(128)S(1)}, s32[8]{0:T(128)}, u32[]{:S(2)}) copy-start(s32[8]{0:T(128)} %param.10) | copy-start | bytes 100
  2.8 18.1 %copy-start.21 = (s32[512,3]{0,1:T(4,128)S(1)}, s32[512,3]{0,1:T(4,128)}, u32[]{:S(2)}) copy-start(s32[512,3]{0,1:T(4,128)} %param.12) | copy-start | bytes 18436
  6.5 24.7 %collective-permute-start.5 = (f32[3,2,512,512]{3,2,1,0:T(8,128)}, f32[3,2,512,512]{3,2,1,0:T(8,128)}, u32[]{:S(2)}, u32[]{:S(2)}) collective-permute-start(f32[3,2,512,512]{3,2,1,0:T(8,128)} %split_rows.3), channel_id=1, source_target_pairs={{0,1},{1,0},{2,3},{3,2},{4,5},{5,4},{6,7},{7,6},{8,9},{9,8},{10,11... | collective-permute-start | bytes 18874376 | tf_op jit(solution)/shard_map/ppermute | solution.py:512
  10.7 19.7 %all-to-all-start = ((f32[128,1,128]{2,1,0:T(1,128)}), f32[128,1,128]{2,1,0:T(1,128)S(1)}, u32[]{:S(2)}, u32[]{:S(2)}) async-start(f32[128,1,128]{2,1,0:T(1,128)} %broadcast_in_dim.17), calls=%async_computation | async-start | bytes 131072 | tf_op jit(solution)/shard_map/all_to_all | solution.py:516
  21.0 6.3 %collective-permute-start.4 = (f32[8,512]{1,0:T(8,128)S(1)}, f32[8,512]{1,0:T(8,128)S(1)}, u32[]{:S(2)}, u32[]{:S(2)}) collective-permute-start(f32[8,512]{1,0:T(8,128)S(1)} %pad.9), channel_id=1, source_target_pairs={{0,1},{1,0},{2,3},{3,2},{4,5},{5,4},{6,7},{7,6},{8,9},{9,8},{10,11... | collective-permute-start | bytes 49160 | tf_op jit(solution)/shard_map/ppermute | solution.py:514
  22.1 2.8 %copy-start.2 = (bf16[512,3,8,2,128]{4,3,2,1,0:T(2,128)(2,1)S(1)}, bf16[512,3,8,2,128]{4,3,2,1,0:T(2,128)(2,1)}, u32[]{:S(2)}) copy-start(bf16[512,3,8,2,128]{4,3,2,1,0:T(2,128)(2,1)} %param.13) | copy-start | bytes 18874372
  27.2 10.3 %copy-start.17 = (bf16[3,2,512,512]{3,2,1,0:T(8,128)(2,1)}, bf16[3,2,512,512]{3,2,1,0:T(8,128)(2,1)S(1)}, u32[]{:S(2)}) copy-start(bf16[3,2,512,512]{3,2,1,0:T(8,128)(2,1)S(1)} %split_rows.2) | copy-start | bytes 9437188
  27.3 31.4 %copy-start.20 = (f32[8,1024]{1,0:T(8,128)}, f32[8,1024]{1,0:T(8,128)S(1)}, u32[]{:S(2)}) copy-start(f32[8,1024]{1,0:T(8,128)S(1)} %pad_maximum_fusion.refs_1_) | copy-start | bytes 98308
  37.5 43.3 %copy-start.19 = (bf16[3,1024,512]{2,1,0:T(8,128)(2,1)}, bf16[3,1024,512]{2,1,0:T(8,128)(2,1)S(1)}, u32[]{:S(2)}) copy-start(bf16[3,1024,512]{2,1,0:T(8,128)(2,1)S(1)} %get-tuple-element.58.refs_3_) | copy-start | bytes 9437188
  37.5 15.5 %collective-permute-start.8 = (f32[16,40,128]{2,1,0:T(8,128)S(1)}, f32[16,40,128]{2,1,0:T(8,128)S(1)}, u32[]{:S(2)}, u32[]{:S(2)}) collective-permute-start(f32[16,40,128]{2,1,0:T(8,128)S(1)} %bitcast.55), channel_id=1, source_target_pairs={{0,2},{2,4},{4,6},{6,0},{1,3},{3,5},{5,7},{7,1},{8,10},{10,12},{12... | collective-permute-start | bytes 983048 | tf_op jit(solution)/shard_map/ppermute | solution.py:280
  37.9 15.2 %collective-permute-start.9 = (f32[16,40,128]{2,1,0:T(8,128)S(1)}, f32[16,40,128]{2,1,0:T(8,128)S(1)}, u32[]{:S(2)}, u32[]{:S(2)}) collective-permute-start(f32[16,40,128]{2,1,0:T(8,128)S(1)} %bitcast.62), channel_id=1, source_target_pairs={{0,6},{2,0},{4,2},{6,4},{1,7},{3,1},{5,3},{7,5},{8,14},{10,8},{12,... | collective-permute-start | bytes 983048 | tf_op jit(solution)/shard_map/ppermute | solution.py:284
  40.3 7.7 %copy-start.18 = (bf16[3,2,512,512]{3,2,1,0:T(8,128)(2,1)S(1)}, bf16[3,2,512,512]{3,2,1,0:T(8,128)(2,1)}, u32[]{:S(2)}) copy-start(bf16[3,2,512,512]{3,2,1,0:T(8,128)(2,1)} %copy-done.17) | copy-start | bytes 9437188
  46.5 0.7 copy-start.14
  47.2 0.7 copy-start.15
  53.2 33.4 %collective-permute-start.12 = (f32[32,40,128]{2,1,0:T(8,128)S(1)}, f32[32,40,128]{2,1,0:T(8,128)S(1)}, u32[]{:S(2)}, u32[]{:S(2)}) collective-permute-start(f32[32,40,128]{2,1,0:T(8,128)S(1)} %get-tuple-element.65.refs_4_), channel_id=1, source_target_pairs={{0,2},{2,4},{4,6},{6,0},{1,3},{3,5},{5,7},{7,1},{8,10},{10,12},{12... | collective-permute-start | bytes 1966088 | tf_op jit(solution)/shard_map/ppermute | solution.py:280
  53.3 33.4 %collective-permute-start.13 = (f32[32,40,128]{2,1,0:T(8,128)S(1)}, f32[32,40,128]{2,1,0:T(8,128)S(1)}, u32[]{:S(2)}, u32[]{:S(2)}) collective-permute-start(f32[32,40,128]{2,1,0:T(8,128)S(1)} %get-tuple-element.76), channel_id=1, source_target_pairs={{0,6},{2,0},{4,2},{6,4},{1,7},{3,1},{5,3},{7,5},{8,14},{10,8},{12,... | collective-permute-start | bytes 1966088 | tf_op jit(solution)/shard_map/ppermute | solution.py:284
  56.0 20.4 %collective-permute-start.6 = (f32[16,40,128]{2,1,0:T(8,128)S(1)}, f32[16,40,128]{2,1,0:T(8,128)S(1)}, u32[]{:S(2)}, u32[]{:S(2)}) collective-permute-start(f32[16,40,128]{2,1,0:T(8,128)S(1)} %bitcast.54), channel_id=1, source_target_pairs={{0,2},{2,4},{4,6},{6,0},{1,3},{3,5},{5,7},{7,1},{8,10},{10,12},{12... | collective-permute-start | bytes 983048 | tf_op jit(solution)/shard_map/ppermute | solution.py:280
  56.0 20.4 %collective-permute-start.7 = (f32[16,40,128]{2,1,0:T(8,128)S(1)}, f32[16,40,128]{2,1,0:T(8,128)S(1)}, u32[]{:S(2)}, u32[]{:S(2)}) collective-permute-start(f32[16,40,128]{2,1,0:T(8,128)S(1)} %bitcast.61), channel_id=1, source_target_pairs={{0,6},{2,0},{4,2},{6,4},{1,7},{3,1},{5,3},{7,5},{8,14},{10,8},{12,... | collective-permute-start | bytes 983048 | tf_op jit(solution)/shard_map/ppermute | solution.py:284
  64.6 13.6 %copy-start.5 = (f32[1280,128]{1,0:T(8,128)}, f32[1280,128]{1,0:T(8,128)S(1)}, u32[]{:S(2)}) copy-start(f32[1280,128]{1,0:T(8,128)S(1)} %get-tuple-element.78) | copy-start | bytes 1966084
  78.2 23.0 %collective-permute-start.14 = (f32[32,40,128]{2,1,0:T(8,128)S(1)}, f32[32,40,128]{2,1,0:T(8,128)}, u32[]{:S(2)}, u32[]{:S(2)}) collective-permute-start(f32[32,40,128]{2,1,0:T(8,128)S(1)} %get-tuple-element.68.refs_4_), channel_id=1, source_target_pairs={{0,2},{2,4},{4,6},{6,0},{1,3},{3,5},{5,7},{7,1},{8,10},{10,12},{12... | collective-permute-start | bytes 1966088 | tf_op jit(solution)/shard_map/ppermute | solution.py:280
  78.2 23.0 %collective-permute-start.15 = (f32[32,40,128]{2,1,0:T(8,128)}, f32[32,40,128]{2,1,0:T(8,128)}, u32[]{:S(2)}, u32[]{:S(2)}) collective-permute-start(f32[32,40,128]{2,1,0:T(8,128)} %get-tuple-element.79), channel_id=1, source_target_pairs={{0,6},{2,0},{4,2},{6,4},{1,7},{3,1},{5,3},{7,5},{8,14},{10,8},{12,... | collective-permute-start | bytes 1966088 | tf_op jit(solution)/shard_map/ppermute | solution.py:284
  86.6 11.0 %copy-start.3 = (f32[1280,128]{1,0:T(8,128)}, f32[1280,128]{1,0:T(8,128)S(1)}, u32[]{:S(2)}) copy-start(f32[1280,128]{1,0:T(8,128)S(1)} %get-tuple-element.73) | copy-start | bytes 1966084
  88.8 0.8 copy-start.7
  89.6 19.6 %all-to-all-start.3 = ((f32[32,1,40,128]{3,2,1,0:T(8,128)}), f32[32,1,40,128]{3,2,1,0:T(8,128)S(1)}, u32[]{:S(2)}, u32[]{:S(2)}) async-start(f32[32,1,40,128]{3,2,1,0:T(8,128)} %get-tuple-element.84), calls=%async_computation.3 | async-start | bytes 1310720 | tf_op jit(solution)/shard_map/all_to_all | solution.py:371
  97.5 17.2 %collective-permute-start.10 = (f32[16,40,128]{2,1,0:T(8,128)}, f32[16,40,128]{2,1,0:T(8,128)}, u32[]{:S(2)}, u32[]{:S(2)}) collective-permute-start(f32[16,40,128]{2,1,0:T(8,128)} %bitcast.60), channel_id=1, source_target_pairs={{0,2},{2,4},{4,6},{6,0},{1,3},{3,5},{5,7},{7,1},{8,10},{10,12},{12... | collective-permute-start | bytes 983048 | tf_op jit(solution)/shard_map/ppermute | solution.py:280
  98.6 16.2 %collective-permute-start.11 = (f32[16,40,128]{2,1,0:T(8,128)}, f32[16,40,128]{2,1,0:T(8,128)}, u32[]{:S(2)}, u32[]{:S(2)}) collective-permute-start(f32[16,40,128]{2,1,0:T(8,128)} %bitcast.59), channel_id=1, source_target_pairs={{0,6},{2,0},{4,2},{6,4},{1,7},{3,1},{5,3},{7,5},{8,14},{10,8},{12,... | collective-permute-start | bytes 983048 | tf_op jit(solution)/shard_map/ppermute | solution.py:284
  101.2 1.1 copy-start.6
  102.3 1.1 copy-start.8
  109.3 26.2 %all-to-all-start.2 = ((f32[32,2,40,128]{3,2,1,0:T(8,128)}), f32[32,2,40,128]{3,2,1,0:T(8,128)S(1)}, u32[]{:S(2)}, u32[]{:S(2)}) async-start(f32[32,2,40,128]{3,2,1,0:T(8,128)} %place_slots.3.refs_4_), calls=%async_computation.2 | async-start | bytes 2621440 | tf_op jit(solution)/shard_map/all_to_all | solution.py:371
  114.8 1.1 copy-start.4
  115.9 27.9 %copy-start.16 = (bf16[4,128,2,128]{3,2,1,0:T(2,128)(2,1)S(1)}, bf16[4,128,2,128]{3,2,1,0:T(2,128)(2,1)}, u32[]{:S(2)}) copy-start(bf16[4,128,2,128]{3,2,1,0:T(2,128)(2,1)} %param.14) | copy-start | bytes 786436
  117.1 27.5 %copy-start.13 = (s32[4,128]{1,0:T(4,128)S(1)}, s32[4,128]{1,0:T(4,128)}, u32[]{:S(2)}) copy-start(s32[4,128]{1,0:T(4,128)} %refs_4_.5) | copy-start | bytes 6148
  117.1 16.1 %collective-permute-start.17 = (f32[32,40,128]{2,1,0:T(8,128)S(1)}, f32[32,40,128]{2,1,0:T(8,128)S(1)}, u32[]{:S(2)}, u32[]{:S(2)}) collective-permute-start(f32[32,40,128]{2,1,0:T(8,128)S(1)} %get-tuple-element.81), channel_id=1, source_target_pairs={{0,6},{2,0},{4,2},{6,4},{1,7},{3,1},{5,3},{7,5},{8,14},{10,8},{12,... | collective-permute-start | bytes 1966088 | tf_op jit(solution)/shard_map/ppermute | solution.py:284
  117.5 17.0 %collective-permute-start.16 = (f32[32,40,128]{2,1,0:T(8,128)S(1)}, f32[32,40,128]{2,1,0:T(8,128)S(1)}, u32[]{:S(2)}, u32[]{:S(2)}) collective-permute-start(f32[32,40,128]{2,1,0:T(8,128)S(1)} %get-tuple-element.80.refs_5_), channel_id=1, source_target_pairs={{0,2},{2,4},{4,6},{6,0},{1,3},{3,5},{5,7},{7,1},{8,10},{10,12},{12... | collective-permute-start | bytes 1966088 | tf_op jit(solution)/shard_map/ppermute | solution.py:280
  135.4 21.3 %all-to-all-start.1 = ((f32[32,40,128]{2,1,0:T(8,128)}), f32[32,40,128]{2,1,0:T(8,128)S(1)}, u32[]{:S(2)}, u32[]{:S(2)}) async-start(f32[32,40,128]{2,1,0:T(8,128)} %add_add_fusion.1), calls=%async_computation.1 | async-start | bytes 1310720 | tf_op jit(solution)/shard_map/all_to_all | solution.py:371
  144.4 1.8 %copy-start.9 = (bf16[4,256,256]{2,1,0:T(8,128)(2,1)}, bf16[4,256,256]{2,1,0:T(8,128)(2,1)S(1)}, u32[]{:S(2)}) copy-start(bf16[4,256,256]{2,1,0:T(8,128)(2,1)S(1)} %get-tuple-element.82.refs_2_) | copy-start | bytes 1572868
  144.4 1.8 %copy-start.11 = (bf16[4,256,256]{2,1,0:T(8,128)(2,1)}, bf16[4,256,256]{2,1,0:T(8,128)(2,1)S(1)}, u32[]{:S(2)}) copy-start(bf16[4,256,256]{2,1,0:T(8,128)(2,1)S(1)} %get-tuple-element.83.refs_3_) | copy-start | bytes 1572868
  156.7 1.0 copy-start.10
  157.7 1.0 copy-start.12

commit v4 on v3

v4 whole, which is shorter than its diff:
```python
import math

import jax
import jax.numpy as jnp
from jax import lax
from jax.experimental import pallas as pl
from jax.experimental.pallas import tpu as pltpu
from jax.sharding import Mesh
from jax.sharding import PartitionSpec as P

SUB = 4
KA = ("ka_0", "ka_1")
KA_ROW = ("ka_0", "ka_1", "row_0", "row_1")
ROW = ("row_0", "row_1")
PLANE = ("ka_0", "ka_1", "row_1")
INTERPRET = False

broadening = 1.0
refine_step = (0.05, 0.03, 0.02)

f32 = jnp.float32
bf16 = jnp.bfloat16
VMEM = pl.BlockSpec(memory_space=pltpu.VMEM)
SMEM = pl.BlockSpec(memory_space=pltpu.SMEM)
NX = 4
OWNERS = 32
SECOND = 28
SPARE = 40
BLOCKS = 128


def params(mebibytes):
    return pltpu.CompilerParams(vmem_limit_bytes=mebibytes << 20)


ANY = pl.BlockSpec(memory_space=pl.ANY)
HBM = pl.BlockSpec(memory_space=pltpu.HBM)


def cost(microseconds):
    return pl.CostEstimate(flops=int(microseconds * 2.5e8), bytes_accessed=0, transcendentals=0)


def iota(shape, dim):
    return lax.broadcasted_iota(jnp.int32, shape, dim)


def place_of(position):
    plane = (position % 8) // 2
    owner = (position // 8) * 2 + position % 2
    return plane, owner


def index_kernel(place_ref, table_ref, points_ref, slots_ref, weight_ref):
    my_plane = place_ref[0]
    table = table_ref[...]
    turned = table.T
    square = (BLOCKS, BLOCKS)
    order_down = table[:, 4:5].astype(jnp.int32)
    order_along = turned[4:5, :].astype(jnp.int32)
    here_down = order_down == iota(square, 1)
    here_along = iota(square, 0) == order_along

    def along(column):
        return jnp.sum(jnp.where(here_along, table[:, column : column + 1], 0.0), axis=0, keepdims=True)

    base = [along(axis) for axis in range(3)]
    count = along(3)
    count_down = jnp.sum(jnp.where(here_down, turned[3:4, :], 0.0), axis=1, keepdims=True)

    plane_down, owner_down = place_of(iota(square, 0))
    plane_along, owner_along = place_of(iota(square, 1))
    mates = plane_down == plane_along
    ahead = mates & (owner_down < owner_along)
    plane_row, owner_row = place_of(iota((1, BLOCKS), 1))
    away = (plane_row - my_plane + NX) % NX
    seat = jnp.where(away == 1, 0, jnp.where(away == 3, 1, 2))

    def row_of(chunk, within):
        opposite = OWNERS * chunk + within
        apart = 3 * OWNERS * (1 + chunk) + seat * OWNERS + within
        spare = 12 * OWNERS + jnp.where(away == 2, 0, 1 + seat) * SPARE + within
        return jnp.where(chunk == 3, spare, jnp.where(away == 2, opposite, apart))

    rows = 12 * OWNERS + NX * SPARE
    entry = iota((rows, BLOCKS), 0)
    lane = iota((rows, BLOCKS), 1)
    gathered = [jnp.zeros((rows, BLOCKS), f32) for _ in range(3)]
    before = jnp.zeros((1, BLOCKS), f32)
    slots_ref[...] = jnp.zeros((8, BLOCKS), jnp.int32)
    weight_ref[...] = jnp.zeros((8, BLOCKS), f32)
    for s in range(SUB):
        fraction = (s + 0.5) / count - 0.5
        points = [base[axis] + fraction * refine_step[axis] for axis in range(3)]
        alive = count > s
        weight_ref[s : s + 1, :] = jnp.where(alive, 1.0 / count, 0.0)
        if s == 0:
            chunk, within = jnp.full((1, BLOCKS), 2, jnp.int32), owner_row
        else:
            live_down = count_down > s
            rank = before + jnp.sum(jnp.where(ahead & live_down, 1.0, 0.0), axis=0, keepdims=True)
            before = before + jnp.sum(jnp.where(mates & live_down, 1.0, 0.0), axis=0, keepdims=True)
            rank = jnp.where(alive, rank, 0.0).astype(jnp.int32)
            slots_ref[s : s + 1, :] = rank
            chunk = jnp.where(rank < OWNERS, 0, jnp.where(rank < OWNERS + SECOND, 1, 3))
            within = rank - jnp.where(chunk == 0, 0, jnp.where(chunk == 1, OWNERS, OWNERS + SECOND))
        match = entry == jnp.where(alive, row_of(chunk, within), -1)
        for axis in range(3):
            gathered[axis] = gathered[axis] + jnp.where(match, points[axis], 0.0)
    most = jnp.max(before, axis=1, keepdims=True)
    slots_ref[0:1, :] = jnp.broadcast_to(most, (1, BLOCKS)).astype(jnp.int32)
    points = jnp.zeros((rows, BLOCKS), f32)
    for axis in range(3):
        points = jnp.where(lane == axis, jnp.sum(gathered[axis], axis=1, keepdims=True), points)
    points_ref[...] = points


def find_points(table, plane):
    rows = 12 * OWNERS + NX * SPARE
    return pl.pallas_call(
        index_kernel,
        out_shape=(
            jax.ShapeDtypeStruct((rows, BLOCKS), f32),
            jax.ShapeDtypeStruct((8, BLOCKS), jnp.int32),
            jax.ShapeDtypeStruct((8, BLOCKS), f32),
        ),
        in_specs=[SMEM, VMEM],
        out_specs=(VMEM, VMEM, VMEM),
        compiler_params=params(8),
        cost_estimate=cost(2),
        interpret=INTERPRET,
        name="find_points",
    )(plane, table)


def pieces_of(depth):
    return [(matrix, slice(half * depth // 2, (half + 1) * depth // 2)) for matrix in range(3) for half in range(2)]


def coming_rows(core, space_ref, in_buffer, sems):
    _, depth, rows, _ = in_buffer.shape
    copies = []
    for k, (matrix, at) in enumerate(pieces_of(depth)):
        first = pl.multiple_of(rows * (2 * matrix + core), rows)
        copies.append(
            pltpu.make_async_copy(space_ref.at[at, pl.ds(first, rows), :], in_buffer.at[matrix, at], sems.at[k])
        )
    return copies


def turn_rows(in_buffer, wide_ref, matrix, at, store):
    _, _, rows, width = in_buffer.shape
    size = at.stop - at.start
    for first in range(0, size, 8):
        wide = in_buffer[matrix, at.start + first : at.start + first + 8].astype(f32)
        for r in range(8):
            wide_ref[(first + r) * rows : (first + r + 1) * rows, :] = wide[r]
    for part in range(2):
        for r in range(rows // 2):
            store(part, slice(r * width, (r + 1) * width), wide_ref[pl.ds(2 * r + part, size, stride=rows), :])


def send_kernel(core_ref, space_ref, out_ref, token_ref, in_buffer, out_buffer, wide_ref, in_sems, out_sems):
    token_ref[...] = jnp.zeros(token_ref.shape, f32)
    depth = in_buffer.shape[1]
    coming = coming_rows(core_ref[0], space_ref, in_buffer, in_sems)
    places = pieces_of(depth)
    going = [
        pltpu.make_async_copy(out_buffer.at[matrix, :, at], out_ref.at[matrix, :, at], out_sems.at[k])
        for k, (matrix, at) in enumerate(places)
    ]
    for copy in coming:
        copy.start()
    for k, (matrix, at) in enumerate(places):
        coming[k].wait()

        def store(part, lanes, value):
            out_buffer[matrix, part, at, lanes] = value

        turn_rows(in_buffer, wide_ref, matrix, at, store)
        going[k].start()
    for copy in going:
        copy.wait()


def send_rows(space, core):
    depth, rows, width = space.shape
    half = rows // 6
    shape = (3, 2, depth, half // 2 * width)
    return pl.pallas_call(
        send_kernel,
        out_shape=(jax.ShapeDtypeStruct(shape, f32), jax.ShapeDtypeStruct((8, BLOCKS), f32)),
        in_specs=[SMEM, HBM],
        out_specs=(HBM, VMEM),
        scratch_shapes=[
            pltpu.VMEM((3, depth, half, width), bf16),
            pltpu.VMEM(shape, f32),
            pltpu.VMEM((depth // 2 * half, width), f32),
            pltpu.SemaphoreType.DMA((6,)),
            pltpu.SemaphoreType.DMA((6,)),
        ],
        compiler_params=params(58),
        cost_estimate=cost(5),
        interpret=INTERPRET,
        name="send_rows",
    )(core, space)


def join_kernel(core_ref, space_ref, other_ref, out_ref, in_buffer, other_buffer, wide_ref, in_sems, other_sems):
    depth = in_buffer.shape[1]
    coming = coming_rows(core_ref[0], space_ref, in_buffer, in_sems)
    places = pieces_of(depth)
    others = [
        pltpu.make_async_copy(other_ref.at[matrix, :, at], other_buffer.at[matrix, :, at], other_sems.at[k])
        for k, (matrix, at) in enumerate(places)
    ]
    for k in range(6):
        coming[k].start()
        others[k].start()
    for k, (matrix, at) in enumerate(places):
        coming[k].wait()

        def store(part, lanes, value):
            rows = slice(part * depth + at.start, part * depth + at.stop)
            out_ref[matrix, rows, lanes] = value.astype(bf16)

        turn_rows(in_buffer, wide_ref, matrix, at, store)
        others[k].wait()
        for part in range(2):
            rows = slice((2 + part) * depth + at.start, (2 + part) * depth + at.stop)
            out_ref[matrix, rows, :] = other_buffer[matrix, part, at, :].astype(bf16)


def join_rows(space, core, other):
    depth, rows, width = space.shape
    half = rows // 6
    lanes = half // 2 * width
    return pl.pallas_call(
        join_kernel,
        out_shape=jax.ShapeDtypeStruct((3, 4 * depth, lanes), bf16),
        in_specs=[SMEM, HBM, HBM],
        out_specs=VMEM,
        scratch_shapes=[
            pltpu.VMEM((3, depth, half, width), bf16),
            pltpu.VMEM((3, 2, depth, lanes), f32),
            pltpu.VMEM((depth // 2 * half, width), f32),
            pltpu.SemaphoreType.DMA((6,)),
            pltpu.SemaphoreType.DMA((6,)),
        ],
        compiler_params=params(54),
        cost_estimate=cost(5),
        interpret=INTERPRET,
        name="join_rows",
    )(core, space, other)


def pack_kernel(row_ref, base_ref, counts_ref, order_ref, *refs):
    out_ref = refs[-1]
    row = row_ref[0]
    lane = iota((1, 1, BLOCKS), 2)
    value = jnp.zeros((1, 1, BLOCKS), f32)
    for axis in range(3):
        value = jnp.where(lane == axis, base_ref[row, axis], value)
    value = jnp.where(lane == 3, counts_ref[row].astype(f32), value)
    value = jnp.where(lane == 4, order_ref[0].astype(f32), value)
    out_ref[...] = jnp.broadcast_to(value, out_ref.shape)


def pack(row, base_k, counts, block_order, after):
    return pl.pallas_call(
        pack_kernel,
        out_shape=jax.ShapeDtypeStruct((BLOCKS, 1, BLOCKS), f32),
        in_specs=[SMEM] * 4 + [ANY] * len(after),
        out_specs=VMEM,
        compiler_params=params(4),
        cost_estimate=cost(1),
        interpret=INTERPRET,
        name="pack",
    )(row, base_k, counts, block_order, *after)


def turn(points, coords):
    turns = points[:, 0:1] * coords[0:1, :] + points[:, 1:2] * coords[1:2, :] + points[:, 2:3] * coords[2:3, :]
    rest = turns - jnp.floor(turns + 0.5)
    quarter = jnp.floor(4.0 * rest + 0.5)
    angle = (rest - 0.25 * quarter) * (2.0 * math.pi)
    square = angle * angle
    sine = angle * (1.0 + square * (-1.0 / 6 + square * (1.0 / 120 + square * (-1.0 / 5040 + square * (1.0 / 362880)))))
    cosine = 1.0 + square * (-0.5 + square * (1.0 / 24 + square * (-1.0 / 720 + square * (1.0 / 40320 - square / 3628800))))
    odd = jnp.abs(quarter) == 1.0
    first = jnp.where(odd, sine, cosine)
    second = jnp.where(odd, cosine, sine)
    cos_sign = jnp.where((quarter == 1.0) | (jnp.abs(quarter) == 2.0), -1.0, 1.0)
    sin_sign = jnp.where((quarter == -1.0) | (jnp.abs(quarter) == 2.0), -1.0, 1.0)
    return first * cos_sign, second * sin_sign


def store_phases(low, count, points_ref, coords_ref, phase_ref):
    depth = coords_ref.shape[1] // 2
    tile = 16

    def rows_of(i, carry):
        first = pl.multiple_of(i * tile, tile)
        points = points_ref[pl.ds(low + first, tile), :]
        for source in range(2):
            coords = coords_ref[:, source * depth : (source + 1) * depth]
            cosine, sine = turn(points, coords)
            at_real = slice(source * 2 * depth, source * 2 * depth + depth)
            at_imag = slice(source * 2 * depth + depth, source * 2 * depth + 2 * depth)
            pairs = [(cosine, sine)]
            for axis in range(2):
                coord = coords[axis : axis + 1, :]
                pairs.append((-coord * sine, coord * cosine))
            for kind, (real, imag) in enumerate(pairs):
                real_rows = pl.ds(2 * kind * count + first, tile)
                imag_rows = pl.ds((2 * kind + 1) * count + first, tile)
                phase_ref[real_rows, at_real] = real.astype(bf16)
                phase_ref[real_rows, at_imag] = (-imag).astype(bf16)
                phase_ref[imag_rows, at_real] = imag.astype(bf16)
                phase_ref[imag_rows, at_imag] = real.astype(bf16)
        return carry

    lax.fori_loop(0, count // tile, rows_of, 0)


def store_sums(phase_ref, matrices, count, kinds, first_kind, first_row, out_refs, pitches):
    product = jnp.dot(phase_ref[: kinds * count, :], matrices, preferred_element_type=f32)
    width = product.shape[1] // 2
    for kind in range(kinds):
        for half in range(2):
            block = product[kind * count : (kind + 1) * count, half * width : (half + 1) * width]
            at = (first_kind + kind) * 4 + first_row + half
            start = 0
            for ref, pitch in zip(out_refs, pitches):
                size = ref.shape[0] // 40
                ref[pl.ds(at, size, stride=40), :] = block[start : start + size]
                start += pitch


PLACES = tuple((matrix, part) for matrix in range(3) for part in range(2))


def fourier_kernel(low, pitches, waits, streamed, points_ref, coords_ref, matrices_ref, *refs):
    refs = refs[waits:]
    outs = len(pitches)
    out_refs, token_ref, phase_ref = refs[:outs], refs[outs], refs[outs + 1]
    token_ref[...] = jnp.zeros(token_ref.shape, f32)
    count = sum(pitches)
    lanes = matrices_ref.shape[2] // 2
    copies = []
    if streamed:
        buffer_ref, sems = refs[outs + 2 :]
        for k, (matrix, part) in enumerate(PLACES):
            source = matrices_ref.at[matrix, :, pl.ds(part * lanes, lanes)]
            copies.append(pltpu.make_async_copy(source, buffer_ref.at[k], sems.at[k]))
        for copy in copies:
            copy.start()
    store_phases(low, count, points_ref, coords_ref, phase_ref)
    for k, (matrix, part) in enumerate(PLACES):
        kinds, first_kind = (6, 0) if matrix == 0 else (2, 4 + 2 * matrix)
        if streamed:
            copies[k].wait()
            block = buffer_ref[k]
        else:
            block = matrices_ref[matrix, :, part * lanes : (part + 1) * lanes]
        store_sums(phase_ref, block, count, kinds, first_kind, 2 * part, out_refs, pitches)


def fourier(points, low, sizes, pitches, coords, matrices, microseconds, after=(), streamed=False):
    depth4 = matrices.shape[1]
    width = matrices.shape[2] // 4
    shapes = tuple(jax.ShapeDtypeStruct((size * 40, width), f32) for size in sizes)
    scratch = [pltpu.VMEM((6 * sum(pitches), depth4), bf16)]
    if streamed:
        scratch += [pltpu.VMEM((6, depth4, 2 * width), bf16), pltpu.SemaphoreType.DMA((6,))]
    outs = pl.pallas_call(
        lambda *refs: fourier_kernel(low, pitches, len(after), streamed, *refs),
        out_shape=shapes + (jax.ShapeDtypeStruct((8, BLOCKS), f32),),
        in_specs=[VMEM, VMEM, HBM if streamed else VMEM] + [ANY] * len(after),
        out_specs=(VMEM,) * (len(shapes) + 1),
        scratch_shapes=scratch,
        compiler_params=params(18),
        cost_estimate=cost(microseconds),
        interpret=INTERPRET,
        name="fourier",
    )(points, coords, matrices, *after)
    return tuple(out.reshape(-1, 40, width) for out in outs[:-1]) + (outs[-1],)


def to_right(value):
    return lax.ppermute(value, "row_0", [(i, (i + 1) % NX) for i in range(NX)])


def to_left(value):
    return lax.ppermute(value, "row_0", [(i, (i - 1) % NX) for i in range(NX)])


def first_hop(near, far):
    near = to_right(near)
    far = to_left(far)
    return near, far


def add_kernel(waits, near_ref, far_ref, right_ref, left_ref, *refs):
    right_out, left_out, token_ref = refs[waits:]
    half = near_ref.shape[0]
    right_out[:half] = right_ref[:half] + near_ref[...]
    right_out[half:] = right_ref[half:]
    left_out[:half] = left_ref[:half]
    left_out[half:] = left_ref[half:] + far_ref[...]
    token_ref[...] = jnp.zeros(token_ref.shape, f32)


def add_arrived(near, far, right, left, after=()):
    shape = jax.ShapeDtypeStruct(right.shape, f32)
    return pl.pallas_call(
        lambda *refs: add_kernel(len(after), *refs),
        out_shape=(shape, shape, jax.ShapeDtypeStruct((8, BLOCKS), f32)),
        in_specs=[VMEM] * 4 + [ANY] * len(after),
        out_specs=(VMEM,) * 3,
        input_output_aliases={2: 0, 3: 1},
        compiler_params=params(6),
        cost_estimate=cost(1.5),
        interpret=INTERPRET,
        name="add_arrived",
    )(near, far, right, left, *after)


def second_hop(right, left):
    right = to_right(right)
    left = to_left(left)
    return right, left


def place_kernel(place_ref, slots_ref, *refs):
    keep0, right0, left0, keep1, right1, left1, extra = refs[:7]
    out_ref, token_ref, table_ref = refs[-3:]
    token_ref[...] = jnp.zeros(token_ref.shape, f32)
    plane = place_ref[0]
    first, second = keep0.shape[0], keep0.shape[0] + keep1.shape[0]
    table_ref[:first] = keep0[...] + right0[...] + left0[...]
    table_ref[first:second] = keep1[...] + right1[...] + left1[...]
    table_ref[second:] = extra[...]

    def body(owner, carry):
        position = (owner // 2) * 8 + 2 * plane + owner % 2
        for s in range(1, SUB):
            out_ref[owner, s - 1] = table_ref[slots_ref[s, position]]
        return carry

    lax.fori_loop(0, OWNERS, body, 0)


def place_slots(plane, slots, parts0, parts1, extra, after):
    _, rows, width = extra.shape
    size = OWNERS + SECOND + SPARE
    return pl.pallas_call(
        place_kernel,
        out_shape=(
            jax.ShapeDtypeStruct((OWNERS, SUB - 1, rows, width), f32),
            jax.ShapeDtypeStruct((8, BLOCKS), f32),
        ),
        in_specs=[SMEM, SMEM] + [VMEM] * 7 + [ANY] * len(after),
        out_specs=(VMEM, VMEM),
        scratch_shapes=[pltpu.VMEM((size, rows, width), f32)],
        compiler_params=params(12),
        cost_estimate=cost(4),
        interpret=INTERPRET,
        name="place_slots",
    )(plane, slots, *parts0, *parts1, extra, *after)


def total_kernel(keep_ref, right_ref, left_ref, out_ref):
    out_ref[...] = keep_ref[...] + right_ref[...] + left_ref[...]


def total(keep, right, left):
    return pl.pallas_call(
        total_kernel,
        out_shape=jax.ShapeDtypeStruct(keep.shape, f32),
        in_specs=[VMEM] * 3,
        out_specs=VMEM,
        compiler_params=params(8),
        cost_estimate=cost(1.5),
        interpret=INTERPRET,
        name="total",
    )(keep, right, left)


def to_owners(value):
    return lax.all_to_all(value, PLANE, split_axis=0, concat_axis=0, tiled=True)


def two_terms(value):
    high = value.astype(bf16)
    return high, (value - high.astype(f32)).astype(bf16)


def curvature_kernel(first, units, adding, weight_ref, field_ref, turn_ref, back_ref, occupied_ref, *refs):
    out_ref = refs[-1]
    previous = refs[0][...] if adding else 0.0
    unit = pl.program_id(0)
    sources = field_ref.shape[0] // (units * 40)
    n = field_ref.shape[1]
    stride = units * 40

    def plane_of(kind):
        return jnp.concatenate(
            [field_ref[pl.ds(unit * 40 + kind * 4 + r, sources, stride=stride), :] for r in range(4)], axis=0
        )

    matrices = jnp.concatenate(
        [jnp.concatenate([plane_of(2 * c), plane_of(2 * c + 1)], axis=1) for c in range(5)], axis=0
    )
    high, low = two_terms(matrices)
    vectors = turn_ref[0]
    rotated = jnp.dot(high, vectors, preferred_element_type=f32) + jnp.dot(low, vectors, preferred_element_type=f32)
    stacked = jnp.concatenate(
        [
            jnp.concatenate([rotated[c * n : (c + 1) * n, :n] for c in range(5)], axis=1),
            jnp.concatenate([rotated[c * n : (c + 1) * n, n:] for c in range(5)], axis=1),
        ],
        axis=0,
    )
    back = back_ref[0]
    high, low = two_terms(stacked)
    bar = jnp.dot(back, high, preferred_element_type=f32) + jnp.dot(back, low, preferred_element_type=f32)
    bar_real, bar_imag = bar[:n], bar[n:]
    diagonal = jnp.where(iota((n, n), 0) == iota((n, n), 1), bar_real[:, :n], 0.0)
    spacing = jnp.sum(diagonal, axis=0, keepdims=True) - jnp.sum(diagonal, axis=1, keepdims=True)
    smoothed = spacing / (spacing * spacing + broadening)

    def pick(value, c):
        return value[:, (c + 1) * n : (c + 2) * n]

    xcov_real = pick(bar_real, 2) + smoothed * pick(bar_real, 0)
    xcov_imag = pick(bar_imag, 2) + smoothed * pick(bar_imag, 0)
    ycov_real = pick(bar_real, 3) + smoothed * pick(bar_real, 1)
    ycov_imag = pick(bar_imag, 3) + smoothed * pick(bar_imag, 1)
    s = first + unit
    filled = occupied_ref[pl.ds(s, 1), :].astype(f32)
    filled_down = jnp.broadcast_to(filled, (n, n)).T
    pairing = filled_down * (1.0 - filled)
    product = pairing * (xcov_real * ycov_imag.T + xcov_imag * ycov_real.T)
    berry = jnp.sum(jnp.sum(product, axis=0, keepdims=True), axis=1, keepdims=True) * (-2.0 / n)
    weight = weight_ref[s]
    lane = iota((1, SUB), 1)
    result = jnp.where((lane == s) & (weight > 0.0), weight * berry, 0.0)
    before = jnp.where(unit == 0, previous, out_ref[...])
    out_ref[...] = result + before


def curvature(first, units, weight, arrived, vectors, adjoint, occupied, previous=(), after=()):
    width = arrived.shape[-1]
    flat = arrived.reshape(-1, width)
    matrix = pl.BlockSpec((1, 2 * width, 2 * width), lambda u: (first + u, 0, 0))
    return pl.pallas_call(
        lambda *refs: curvature_kernel(first, units, len(previous), *refs),
        grid=(units,),
        out_shape=jax.ShapeDtypeStruct((1, SUB), f32),
        in_specs=[
            SMEM,
            pl.BlockSpec(flat.shape, lambda u: (0, 0)),
            matrix,
            matrix,
            pl.BlockSpec(occupied.shape, lambda u: (0, 0)),
        ]
        + [pl.BlockSpec((1, SUB), lambda u: (0, 0))] * len(previous)
        + [ANY] * len(after),
        out_specs=pl.BlockSpec((1, SUB), lambda u: (0, 0)),
        compiler_params=params(58),
        cost_estimate=cost(2.5 * units),
        interpret=INTERPRET,
        name="curvature",
    )(weight, flat, vectors, adjoint, occupied, *previous, *after)


def vector_kernel(eigvecs_ref, *refs):
    turn_ref, back_ref, wide_ref = refs[-3:]
    n = eigvecs_ref.shape[2]
    wide_ref[...] = eigvecs_ref[0].astype(f32)
    real, imag = (wide_ref[pl.ds(part, n, stride=2), :].astype(bf16) for part in range(2))
    turn_ref[0, :n, :n] = real
    turn_ref[0, :n, n:] = imag
    turn_ref[0, n:, :n] = -imag
    turn_ref[0, n:, n:] = real
    group = n // OWNERS
    for part in range(2):
        packed = jnp.concatenate(
            [wide_ref[pl.ds(2 * r + part, OWNERS, stride=2 * group), :] for r in range(group)], axis=0
        )
        turned = packed.T
        if part == 0:
            back_ref[0, :n, :n] = turned.astype(bf16)
            back_ref[0, n:, n:] = turned.astype(bf16)
        else:
            back_ref[0, :n, n:] = turned.astype(bf16)
            back_ref[0, n:, :n] = (-turned).astype(bf16)


def vector_matrices(eigvecs, after):
    slots, width = eigvecs.shape[0], eigvecs.shape[1]
    shape = jax.ShapeDtypeStruct((slots, 2 * width, 2 * width), bf16)
    square = pl.BlockSpec((1, 2 * width, 2 * width), lambda i: (i, 0, 0))
    return pl.pallas_call(
        vector_kernel,
        grid=(slots,),
        out_shape=(shape, shape),
        in_specs=[pl.BlockSpec((1, 2 * width, width), lambda i: (i, 0, 0))] + [ANY] * len(after),
        out_specs=(square, square),
        scratch_shapes=[pltpu.VMEM((2 * width, width), f32)],
        compiler_params=params(4),
        cost_estimate=cost(2),
        interpret=INTERPRET,
        name="vector_matrices",
    )(eigvecs.reshape(slots, 2 * width, width), *after)


def body(base_k, counts, block_order, lattice, real_space, eigvecs, occupied):
    plane, core = lax.axis_index("row_0"), lax.axis_index("row_1")
    row = plane * 2 + core
    plane_ref = plane.reshape(1).astype(jnp.int32)
    core_ref = core.reshape(1).astype(jnp.int32)
    depth, _, slab, _, width = real_space.shape

    space = real_space.reshape(depth, 6 * slab, width)
    swap = [(0, 1), (1, 0)]
    send, token = send_rows(space, 1 - core_ref)
    mine = pack(row.reshape(1).astype(jnp.int32), base_k, counts, block_order, (token,))
    other = lax.ppermute(send, "row_1", swap)
    own_coords = jnp.pad(lattice.T.astype(f32), ((0, 5), (0, 0)))
    coords = jnp.concatenate([own_coords, lax.ppermute(own_coords, "row_1", swap)], axis=1)

    table = lax.all_to_all(mine, KA_ROW, 0, 0, tiled=True)
    table = table.reshape(BLOCKS, BLOCKS)
    matrices = join_rows(space, core_ref, other)
    points, slots, weights = find_points(table, plane_ref)
    position = (lax.axis_index(KA) * 8 + row).astype(jnp.int32)
    weight = lax.dynamic_slice(weights, (jnp.int32(0), position), (SUB, 1)).reshape(SUB)

    half = OWNERS // 2

    def sums(low, sizes, pitches, microseconds, after=(), streamed=False):
        return fourier(points, low, sizes, pitches, coords, matrices, microseconds, after, streamed)

    def rest(chunk, size, after):
        return sums(3 * OWNERS * (1 + chunk), (size,) * 3, (OWNERS,) * 3, 5, after)

    near0, far0, token = sums(0, (half, half), (half, half), 4, (), True)
    hop0 = first_hop(near0, far0)
    near1, far1, near3, far3, token = sums(
        OWNERS, (half, SECOND - half, half, half), (half,) * 4, 4, (token,)
    )
    hop1 = first_hop(near1, far1)
    right0, left0, keep0, token = rest(0, OWNERS, (token,))
    right0, left0, token = add_arrived(*hop0, right0, left0)
    ring0 = second_hop(right0, left0)
    right1, left1, keep1, token = rest(1, SECOND, (token,))
    right1, left1, token = add_arrived(*hop1, right1, left1)
    ring1 = second_hop(right1, left1)
    hop3 = first_hop(near3, far3)
    right3, left3, keep3, token = rest(2, OWNERS, (token,))

    def further(_):
        parts = (24, 16, SPARE, SPARE, SPARE)
        near, far, right, left, keep, _ = sums(12 * OWNERS, parts, parts, 8)
        right, left, _ = add_arrived(*first_hop(near, far), right, left)
        right, left = second_hop(right, left)
        return keep + right + left

    empty = (SPARE,) + keep0.shape[1:]
    extra = lax.cond(slots[0, 0] > OWNERS + SECOND, further, lambda _: jnp.zeros(empty, f32), 0)

    placed, token = place_slots(plane_ref, slots, (keep0, *ring0), (keep1, *ring1), extra, (token,))
    unit123 = to_owners(placed)
    right3, left3, token = add_arrived(*hop3, right3, left3, (token,))
    ring3 = second_hop(right3, left3)
    turning, back = vector_matrices(eigvecs, (token,))
    unit0 = to_owners(total(keep3, *ring3))
    curve = curvature(1, 3, weight, unit123, turning, back, occupied)
    return curvature(0, 1, weight, unit0, turning, back, occupied, (curve,)).reshape(SUB)


def solution(mesh):
    finer = Mesh(mesh.devices.reshape(4, 4, 4, 2), ("ka_0", "ka_1", "row_0", "row_1"))
    placed = (
        P(KA, None),
        P(KA),
        P(KA_ROW),
        P(ROW, None),
        P(ROW, None, KA, None, None),
        P(KA_ROW, None, None, None),
        P(KA_ROW, None),
    )
    return jax.shard_map(body, mesh=finer, in_specs=placed, out_specs=P(KA_ROW), check_vma=False)
```

time: 162 us -> 146 us (0.901)
  local copies, waits for them, and re-layouts: 16.9 us -> 5.42 us
  waiting for transfers between devices: 41.1 us -> 49.9 us
  Pallas kernels: 51.1 us -> 43.5 us
  starting transfers between devices: 48.4 us -> 45 us
    ppermute x6, waiting for transfers between devices: 12.9 us -> 35.8 us  [to_right(): return lax.ppermute(value, 'row_0', [(i, (i + 1) % NX) for i in range(NX)])]
    ppermute x6, waiting for transfers between devices: 14.6 us -> 0.02 us  [to_left(): return lax.ppermute(value, 'row_0', [(i, (i - 1) % NX) for i in range(NX)])]
    unnamed x46 -> x23, local copies, waits for them, and re-layouts: 13.3 us -> 3.23 us
    pallas_call x13 -> x14, Pallas kernels: 44.8 us -> 34.8 us  [the longest x5 19.9 us: fourier(): pl.pallas_call(lambda *refs: fourier_kernel(low, pitches, len(after), str...]
    all_to_all x1, waiting for transfers between devices: 3.2 us -> 9.47 us  [body(): table = lax.all_to_all(mine, KA_ROW, 0, 0, tiled=True)]
    all_to_all x3 -> x2, waiting for transfers between devices: 10.4 us -> 4.63 us  [to_owners(): return lax.all_to_all(value, PLANE, split_axis=0, concat_axis=0, tiled=True)]
    all_to_all x3 -> x2, starting transfers between devices: 20.6 us -> 16.4 us  [to_owners(): return lax.all_to_all(value, PLANE, split_axis=0, concat_axis=0, tiled=True)]
    pallas_call x3 -> x2, Pallas kernels: 5.74 us -> 8.15 us  [curvature(): pl.pallas_call(lambda *refs: curvature_kernel(first, units, len(previous)...]
  transfers between devices with their start and end apart: 18 -> 17, of which waited for: 6 -> 5; matrix products, arithmetic and copies ran while one was open for 3% -> 2% of each run, Pallas kernels for 24% -> 18%
where the time goes in v4:
time: 146 us; the launch traced here: 145 us
  waiting for transfers between devices  49.9 us (34%)
  starting transfers between devices  45 us (31%)
  Pallas kernels  43.5 us (30%)
  local copies, waits for them, and re-layouts  5.42 us (4%)
  between operations  1.54 us (1%)
    ppermute x6, waiting for transfers between devices, to_right(): return lax.ppermute(value, 'row_0', [(i, (i + 1) % NX) for i in range(NX)])  35.8 us
    pallas_call x5, Pallas kernels, fourier(): pl.pallas_call(lambda *refs: fourier_kernel(low, pitches, len(after), str...  19.9 us
    all_to_all x2, starting transfers between devices, to_owners(): return lax.all_to_all(value, PLANE, split_axis=0, concat_axis=0, tiled=True)  16.4 us
    ppermute x6, starting transfers between devices, to_left(): return lax.ppermute(value, 'row_0', [(i, (i - 1) % NX) for i in range(NX)])  14.9 us
    all_to_all x1, starting transfers between devices, body(): table = lax.all_to_all(mine, KA_ROW, 0, 0, tiled=True)  10.6 us
    all_to_all x1, waiting for transfers between devices, body(): table = lax.all_to_all(mine, KA_ROW, 0, 0, tiled=True)  9.47 us
    pallas_call x2, Pallas kernels, curvature(): pl.pallas_call(lambda *refs: curvature_kernel(first, units, len(previous)...  8.15 us
    pallas_call x1, Pallas kernels, send_rows(): pl.pallas_call(send_kernel, out_shape=(jax.ShapeDtypeStruct(shape, f32),...  4.71 us
  transfers between devices with their start and end apart: 17, of which 5 were waited for; matrix products, arithmetic and copies ran while one was open for 2% of the time, Pallas kernels for 18%

profile of v4, /device:TPU:1, one launch (start us, length us, event | category | flops | bytes accessed | tf_op | source)
XLA Modules:
  0.0 145.4 jit_solution(9222377053545062248)
XLA Ops:
  0.0 4.7 %send_rows.1 = (f32[3,2,512,512]{3,2,1,0:T(8,128)}, f32[8,128]{1,0:T(8,128)}) custom-call(s32[1]{0:T(128)S(6)} %sub.3.core_ref, bf16[512,48,128]{2,1,0:T(8,128)(2,1)} %bitcast.54), custom_call_target="tpu_custom_call" | custom-call | flops 1250000000 | tf_op jit(solution)/shard_map/send_rows/pallas_call | solution.py:190
  4.7 1.5 %collective-permute-start.5 = (f32[3,2,512,512]{3,2,1,0:T(8,128)}, f32[3,2,512,512]{3,2,1,0:T(8,128)}, u32[]{:S(2)}, u32[]{:S(2)}) collective-permute-start(f32[3,2,512,512]{3,2,1,0:T(8,128)} %get-tuple-element.63), channel_id=1, source_target_pairs={{0,1},{1,0},{2,3},{3,2},{4,5},{5,4},{6,7},{7,6},{8,9},{9,8},{10,11... | collective-permute-start | bytes 18874376 | tf_op jit(solution)/shard_map/ppermute | solution.py:630
  6.2 0.1 collective-permute-start.4
  7.0 0.1 copy.20.base_ref
  7.1 0.7 copy-done.1
  7.8 1.3 pack.1
  9.0 10.6 %all-to-all-start = ((f32[128,1,128]{2,1,0:T(1,128)}), f32[128,1,128]{2,1,0:T(1,128)S(1)}, u32[]{:S(2)}, u32[]{:S(2)}) async-start(f32[128,1,128]{2,1,0:T(1,128)} %pack.1), calls=%async_computation | async-start | bytes 131072 | tf_op jit(solution)/shard_map/all_to_all | solution.py:634
  19.6 9.5 %all-to-all-done = f32[128,1,128]{2,1,0:T(1,128)S(1)} async-done(((f32[128,1,128]{2,1,0:T(1,128)}), f32[128,1,128]{2,1,0:T(1,128)S(1)}, u32[]{:S(2)}, u32[]{:S(2)}) %all-to-all-start) | async-done | bytes 65568 | tf_op jit(solution)/shard_map/all_to_all | solution.py:634
  29.1 0.7 find_points.1
  29.9 4.0 %join_rows.1.refs_2_ = bf16[3,2048,512]{2,1,0:T(8,128)(2,1)S(1)} custom-call(s32[1]{0:T(128)} %bitcast.7.core_ref, bf16[512,48,128]{2,1,0:T(8,128)(2,1)} %bitcast.55, f32[3,2,512,512]{3,2,1,0:T(8,128)} %collective-permute-done.5.other_ref), custom_call_target="tpu_custom_call" | custom-call | flops 1250000000 | tf_op jit(solution)/shard_map/join_rows/pallas_call | solution.py:238
  33.9 3.7 %fourier.7 = (f32[640,128]{1,0:T(8,128)S(1)}, f32[640,128]{1,0:T(8,128)S(1)}, f32[8,128]{1,0:T(8,128)S(1)}) custom-call(f32[544,128]{1,0:T(8,128)S(1)} %get-tuple-element.62.refs_0_, f32[8,1024]{1,0:T(8,128)S(1)} %pad_maximum_fusion.refs_1_, bf16[3,2048,512]{2,1,0:T(8,128)(2,1)S(1)} %join_rows.1.refs_2_), custom_call_target="tpu_custom_call" | custom-call | flops 1000000000 | tf_op jit(solution)/shard_map/fourier/pallas_call | solution.py:376
  37.5 0.4 collective-permute-start.8
  37.9 2.4 %collective-permute-start.9 = (f32[16,40,128]{2,1,0:T(8,128)S(1)}, f32[16,40,128]{2,1,0:T(8,128)S(1)}, u32[]{:S(2)}, u32[]{:S(2)}) collective-permute-start(f32[16,40,128]{2,1,0:T(8,128)S(1)} %bitcast.49), channel_id=1, source_target_pairs={{0,6},{2,0},{4,2},{6,4},{1,7},{3,1},{5,3},{7,5},{8,14},{10,8},{12,... | collective-permute-start | bytes 983048 | tf_op jit(solution)/shard_map/ppermute | solution.py:395
  40.3 2.5 %fourier.8 = (f32[640,128]{1,0:T(8,128)S(1)}, f32[480,128]{1,0:T(8,128)S(1)}, f32[640,128]{1,0:T(8,128)S(1)}, f32[640,128]{1,0:T(8,128)S(1)}, f32[8,128]{1,0:T(8,128)S(1)}) custom-call(f32[544,128]{1,0:T(8,128)S(1)} %get-tuple-element.62.refs_0_, f32[8,1024]{1,0:T(8,128)S(1)} %pad_maximum_fusion.refs_1_, bf16[3,2048,512]{2,1,0:T(8,128)(2,1)S(1)} %join_rows.1.refs_2_, ...), custom_call_target="tpu_custom_call" | custom-call | flops 1000000000 | tf_op jit(solution)/shard_map/fourier/pallas_call | solution.py:376
  42.8 0.1 collective-permute-start.6
  42.9 0.5 slice.3
  44.0 0.9 conditional.1
  44.0 0.9 broadcast.2
  45.0 2.7 %collective-permute-start.7 = (f32[12,40,128]{2,1,0:T(8,128)S(1)}, f32[12,40,128]{2,1,0:T(8,128)S(1)}, u32[]{:S(2)}, u32[]{:S(2)}) collective-permute-start(f32[12,40,128]{2,1,0:T(8,128)S(1)} %bitcast.53), channel_id=1, source_target_pairs={{0,6},{2,0},{4,2},{6,4},{1,7},{3,1},{5,3},{7,5},{8,14},{10,8},{12,... | collective-permute-start | bytes 737288 | tf_op jit(solution)/shard_map/ppermute | solution.py:395
  47.6 6.3 %fourier.9 = (f32[1280,128]{1,0:T(8,128)S(1)}, f32[1280,128]{1,0:T(8,128)S(1)}, f32[1280,128]{1,0:T(8,128)S(1)}, f32[8,128]{1,0:T(8,128)}) custom-call(f32[544,128]{1,0:T(8,128)S(1)} %get-tuple-element.62.refs_0_, f32[8,1024]{1,0:T(8,128)S(1)} %pad_maximum_fusion.refs_1_, bf16[3,2048,512]{2,1,0:T(8,128)(2,1)} %copy-done.5, ...), custom_call_target="tpu_custom_call" | custom-call | flops 1250000000 | tf_op jit(solution)/shard_map/fourier/pallas_call | solution.py:376
  53.9 0.2 add_arrived.5
  54.1 0.1 collective-permute-start.12
  54.2 2.7 %collective-permute-start.13 = (f32[32,40,128]{2,1,0:T(8,128)S(1)}, f32[32,40,128]{2,1,0:T(8,128)S(1)}, u32[]{:S(2)}, u32[]{:S(2)}) collective-permute-start(f32[32,40,128]{2,1,0:T(8,128)S(1)} %get-tuple-element.84), channel_id=1, source_target_pairs={{0,6},{2,0},{4,2},{6,4},{1,7},{3,1},{5,3},{7,5},{8,14},{10,8},{12,... | collective-permute-start | bytes 1966088 | tf_op jit(solution)/shard_map/ppermute | solution.py:395
  56.9 3.9 %fourier.10 = (f32[1120,128]{1,0:T(8,128)S(1)}, f32[1120,128]{1,0:T(8,128)S(1)}, f32[1120,128]{1,0:T(8,128)S(1)}, f32[8,128]{1,0:T(8,128)}) custom-call(f32[544,128]{1,0:T(8,128)S(1)} %get-tuple-element.62.refs_0_, f32[8,1024]{1,0:T(8,128)S(1)} %pad_maximum_fusion.refs_1_, bf16[3,2048,512]{2,1,0:T(8,128)(2,1)S(1)} %copy-done.6, ...), custom_call_target="tpu_custom_call" | custom-call | flops 1250000000 | tf_op jit(solution)/shard_map/fourier/pallas_call | solution.py:376
  60.8 0.2 add_arrived.6
  60.9 0.1 collective-permute-start.14
  61.0 2.7 %collective-permute-start.15 = (f32[28,40,128]{2,1,0:T(8,128)S(1)}, f32[28,40,128]{2,1,0:T(8,128)S(1)}, u32[]{:S(2)}, u32[]{:S(2)}) collective-permute-start(f32[28,40,128]{2,1,0:T(8,128)S(1)} %get-tuple-element.87), channel_id=1, source_target_pairs={{0,6},{2,0},{4,2},{6,4},{1,7},{3,1},{5,3},{7,5},{8,14},{10,8},{12,... | collective-permute-start | bytes 1720328 | tf_op jit(solution)/shard_map/ppermute | solution.py:395
  63.7 3.6 %fourier.11 = (f32[1280,128]{1,0:T(8,128)S(1)}, f32[1280,128]{1,0:T(8,128)S(1)}, f32[1280,128]{1,0:T(8,128)S(1)}, f32[8,128]{1,0:T(8,128)S(1)}) custom-call(f32[544,128]{1,0:T(8,128)S(1)} %get-tuple-element.62.refs_0_, f32[8,1024]{1,0:T(8,128)S(1)} %pad_maximum_fusion.refs_1_, bf16[3,2048,512]{2,1,0:T(8,128)(2,1)S(1)} %copy-done.6, ...), custom_call_target="tpu_custom_call" | custom-call | flops 1250000000 | tf_op jit(solution)/shard_map/fourier/pallas_call | solution.py:376
  67.3 14.7 %collective-permute-done.14.refs_4_ = f32[28,40,128]{2,1,0:T(8,128)S(1)} collective-permute-done((f32[28,40,128]{2,1,0:T(8,128)S(1)}, f32[28,40,128]{2,1,0:T(8,128)S(1)}, u32[]{:S(2)}, u32[]{:S(2)}) %collective-permute-start.14) | collective-permute-done | bytes 573472 | tf_op jit(solution)/shard_map/ppermute | solution.py:391
  82.0 2.7 %place_slots.1 = (f32[32,3,40,128]{3,2,1,0:T(8,128)}, f32[8,128]{1,0:T(8,128)S(1)}) custom-call(s32[1]{0:T(128)} %bitcast.5.place_ref, s32[8,128]{1,0:T(8,128)S(1)} %get-tuple-element.81.slots_ref, f32[32,40,128]{2,1,0:T(8,128)S(1)} %bitcast.35, f32[32,40,128]{2,1,0:T(8,128)S(1)} %collective-permute-done.12.refs_1_, ...), custom_call_target="tpu_custom_call" | custom-call | flops 1000000000 | tf_op jit(solution)/shard_map/place_slots/pallas_call | solution.py:457
  84.7 7.2 %all-to-all-start.2 = ((f32[32,3,40,128]{3,2,1,0:T(8,128)}), f32[32,3,40,128]{3,2,1,0:T(8,128)}, u32[]{:S(2)}, u32[]{:S(2)}) async-start(f32[32,3,40,128]{3,2,1,0:T(8,128)} %get-tuple-element.95), calls=%async_computation.2 | async-start | bytes 3932160 | tf_op jit(solution)/shard_map/all_to_all | solution.py:491
  92.0 0.1 collective-permute-start.10
  92.0 2.7 %collective-permute-start.11 = (f32[16,40,128]{2,1,0:T(8,128)S(1)}, f32[16,40,128]{2,1,0:T(8,128)S(1)}, u32[]{:S(2)}, u32[]{:S(2)}) collective-permute-start(f32[16,40,128]{2,1,0:T(8,128)S(1)} %bitcast.46), channel_id=1, source_target_pairs={{0,6},{2,0},{4,2},{6,4},{1,7},{3,1},{5,3},{7,5},{8,14},{10,8},{12,... | collective-permute-start | bytes 983048 | tf_op jit(solution)/shard_map/ppermute | solution.py:395
  94.8 7.4 %collective-permute-done.10.refs_0_ = f32[16,40,128]{2,1,0:T(8,128)S(1)} collective-permute-done((f32[16,40,128]{2,1,0:T(8,128)S(1)}, f32[16,40,128]{2,1,0:T(8,128)S(1)}, u32[]{:S(2)}, u32[]{:S(2)}) %collective-permute-start.10) | collective-permute-done | bytes 327712 | tf_op jit(solution)/shard_map/ppermute | solution.py:391
  102.2 0.2 add_arrived.7
  102.4 0.9 collective-permute-start.16
  103.3 1.8 %collective-permute-start.17 = (f32[32,40,128]{2,1,0:T(8,128)S(1)}, f32[32,40,128]{2,1,0:T(8,128)S(1)}, u32[]{:S(2)}, u32[]{:S(2)}) collective-permute-start(f32[32,40,128]{2,1,0:T(8,128)S(1)} %get-tuple-element.91), channel_id=1, source_target_pairs={{0,6},{2,0},{4,2},{6,4},{1,7},{3,1},{5,3},{7,5},{8,14},{10,8},{12,... | collective-permute-start | bytes 1966088 | tf_op jit(solution)/shard_map/ppermute | solution.py:395
  105.1 13.7 %collective-permute-done.16.right_ref = f32[32,40,128]{2,1,0:T(8,128)S(1)} collective-permute-done((f32[32,40,128]{2,1,0:T(8,128)S(1)}, f32[32,40,128]{2,1,0:T(8,128)S(1)}, u32[]{:S(2)}, u32[]{:S(2)}) %collective-permute-start.16) | collective-permute-done | bytes 655392 | tf_op jit(solution)/shard_map/ppermute | solution.py:391
  118.8 0.9 total.1
  119.7 9.2 %all-to-all-start.1 = ((f32[32,40,128]{2,1,0:T(8,128)}), f32[32,40,128]{2,1,0:T(8,128)S(1)}, u32[]{:S(2)}, u32[]{:S(2)}) async-start(f32[32,40,128]{2,1,0:T(8,128)} %total.1), calls=%async_computation.1 | async-start | bytes 1310720 | tf_op jit(solution)/shard_map/all_to_all | solution.py:491
  128.9 0.7 dynamic-slice_reduce_fusion.refs_0_
  129.6 0.5 vector_matrices.1
  130.2 0.8 copy-done.3
  131.0 0.8 copy-done.4
  131.8 5.4 %curvature.2.refs_5_ = f32[1,4]{1,0:T(1,128)} custom-call(f32[4]{0:T(128)} %dynamic-slice_reduce_fusion.refs_0_, f32[3840,128]{1,0:T(8,128)} %bitcast.29.refs_1_, bf16[4,256,256]{2,1,0:T(8,128)(2,1)} %copy-done.3, bf16[4,256,256]{2,1,0:T(8,128)(2,1)} %copy-done.4, s32[4,128]{1,0:T(4,128)} %refs_4_.3), custom_call_target="tpu_custom_call" | custom-call | flops 1875000064 | tf_op jit(solution)/shard_map/curvature/pallas_call | solution.py:557
  137.2 4.6 %all-to-all-done.1 = f32[32,40,128]{2,1,0:T(8,128)S(1)} async-done(((f32[32,40,128]{2,1,0:T(8,128)}), f32[32,40,128]{2,1,0:T(8,128)S(1)}, u32[]{:S(2)}, u32[]{:S(2)}) %all-to-all-start.1) | async-done | bytes 655392 | tf_op jit(solution)/shard_map/all_to_all | solution.py:491
  141.8 0.8 copy-done.8
  142.7 2.7 %curvature.3 = f32[1,4]{1,0:T(1,128)} custom-call(f32[4]{0:T(128)} %dynamic-slice_reduce_fusion.refs_0_, f32[1280,128]{1,0:T(8,128)} %bitcast.56, bf16[4,256,256]{2,1,0:T(8,128)(2,1)} %copy-done.3, bf16[4,256,256]{2,1,0:T(8,128)(2,1)} %copy-done.4, s32[4,128]{1,0:T(4,128)} %refs_4_.3, f32[1,4]{1,0:T(1,128)} %curvature.2.refs_5_), custom_call_target="tpu_custom_call" | custom-call | flops 625000000 | tf_op jit(solution)/shard_map/curvature/pallas_call | solution.py:557
  (33 shorter events, 0.1 us)
Async XLA Ops:
  0.0 6.2 %copy-start.9 = (s32[512,3]{0,1:T(4,128)S(1)}, s32[512,3]{0,1:T(4,128)}, u32[]{:S(2)}) copy-start(s32[512,3]{0,1:T(4,128)} %param.12) | copy-start | bytes 18436
  0.0 7.0 %copy-start.10 = (f32[8,3]{0,1:T(4,128)S(1)}, f32[8,3]{0,1:T(4,128)}, u32[]{:S(2)}) copy-start(f32[8,3]{0,1:T(4,128)} %param.9) | copy-start | bytes 292
  0.0 7.1 %copy-start.2 = (s32[8]{0:T(128)S(1)}, s32[8]{0:T(128)}, u32[]{:S(2)}) copy-start(s32[8]{0:T(128)} %counts_ref.1) | copy-start | bytes 100
  4.7 25.1 %collective-permute-start.5 = (f32[3,2,512,512]{3,2,1,0:T(8,128)}, f32[3,2,512,512]{3,2,1,0:T(8,128)}, u32[]{:S(2)}, u32[]{:S(2)}) collective-permute-start(f32[3,2,512,512]{3,2,1,0:T(8,128)} %get-tuple-element.63), channel_id=1, source_target_pairs={{0,1},{1,0},{2,3},{3,2},{4,5},{5,4},{6,7},{7,6},{8,9},{9,8},{10,11... | collective-permute-start | bytes 18874376 | tf_op jit(solution)/shard_map/ppermute | solution.py:630
  6.2 13.4 %collective-permute-start.4 = (f32[8,512]{1,0:T(8,128)S(1)}, f32[8,512]{1,0:T(8,128)S(1)}, u32[]{:S(2)}, u32[]{:S(2)}) collective-permute-start(f32[8,512]{1,0:T(8,128)S(1)} %pad.4), channel_id=1, source_target_pairs={{0,1},{1,0},{2,3},{3,2},{4,5},{5,4},{6,7},{7,6},{8,9},{9,8},{10,11... | collective-permute-start | bytes 49160 | tf_op jit(solution)/shard_map/ppermute | solution.py:632
  7.1 0.7 copy-start.1
  9.0 20.1 %all-to-all-start = ((f32[128,1,128]{2,1,0:T(1,128)}), f32[128,1,128]{2,1,0:T(1,128)S(1)}, u32[]{:S(2)}, u32[]{:S(2)}) async-start(f32[128,1,128]{2,1,0:T(1,128)} %pack.1), calls=%async_computation | async-start | bytes 131072 | tf_op jit(solution)/shard_map/all_to_all | solution.py:634
  33.8 10.2 %copy-start.5 = (bf16[3,2048,512]{2,1,0:T(8,128)(2,1)}, bf16[3,2048,512]{2,1,0:T(8,128)(2,1)S(1)}, u32[]{:S(2)}) copy-start(bf16[3,2048,512]{2,1,0:T(8,128)(2,1)S(1)} %join_rows.1.refs_2_) | copy-start | bytes 18874372
  37.5 16.4 %collective-permute-start.8 = (f32[16,40,128]{2,1,0:T(8,128)S(1)}, f32[16,40,128]{2,1,0:T(8,128)S(1)}, u32[]{:S(2)}, u32[]{:S(2)}) collective-permute-start(f32[16,40,128]{2,1,0:T(8,128)S(1)} %bitcast.50), channel_id=1, source_target_pairs={{0,2},{2,4},{4,6},{6,0},{1,3},{3,5},{5,7},{7,1},{8,10},{10,12},{12... | collective-permute-start | bytes 983048 | tf_op jit(solution)/shard_map/ppermute | solution.py:391
  37.9 16.0 %collective-permute-start.9 = (f32[16,40,128]{2,1,0:T(8,128)S(1)}, f32[16,40,128]{2,1,0:T(8,128)S(1)}, u32[]{:S(2)}, u32[]{:S(2)}) collective-permute-start(f32[16,40,128]{2,1,0:T(8,128)S(1)} %bitcast.49), channel_id=1, source_target_pairs={{0,6},{2,0},{4,2},{6,4},{1,7},{3,1},{5,3},{7,5},{8,14},{10,8},{12,... | collective-permute-start | bytes 983048 | tf_op jit(solution)/shard_map/ppermute | solution.py:395
  42.8 18.0 %collective-permute-start.6 = (f32[16,40,128]{2,1,0:T(8,128)S(1)}, f32[16,40,128]{2,1,0:T(8,128)S(1)}, u32[]{:S(2)}, u32[]{:S(2)}) collective-permute-start(f32[16,40,128]{2,1,0:T(8,128)S(1)} %bitcast.48), channel_id=1, source_target_pairs={{0,2},{2,4},{4,6},{6,0},{1,3},{3,5},{5,7},{7,1},{8,10},{10,12},{12... | collective-permute-start | bytes 983048 | tf_op jit(solution)/shard_map/ppermute | solution.py:391
  45.0 11.9 %copy-start.6 = (bf16[3,2048,512]{2,1,0:T(8,128)(2,1)S(1)}, bf16[3,2048,512]{2,1,0:T(8,128)(2,1)}, u32[]{:S(2)}) copy-start(bf16[3,2048,512]{2,1,0:T(8,128)(2,1)} %copy-done.5) | copy-start | bytes 18874372
  45.0 15.8 %collective-permute-start.7 = (f32[12,40,128]{2,1,0:T(8,128)S(1)}, f32[12,40,128]{2,1,0:T(8,128)S(1)}, u32[]{:S(2)}, u32[]{:S(2)}) collective-permute-start(f32[12,40,128]{2,1,0:T(8,128)S(1)} %bitcast.53), channel_id=1, source_target_pairs={{0,6},{2,0},{4,2},{6,4},{1,7},{3,1},{5,3},{7,5},{8,14},{10,8},{12,... | collective-permute-start | bytes 737288 | tf_op jit(solution)/shard_map/ppermute | solution.py:395
  54.1 27.9 %collective-permute-start.12 = (f32[32,40,128]{2,1,0:T(8,128)S(1)}, f32[32,40,128]{2,1,0:T(8,128)S(1)}, u32[]{:S(2)}, u32[]{:S(2)}) collective-permute-start(f32[32,40,128]{2,1,0:T(8,128)S(1)} %get-tuple-element.83), channel_id=1, source_target_pairs={{0,2},{2,4},{4,6},{6,0},{1,3},{3,5},{5,7},{7,1},{8,10},{10,12},{12... | collective-permute-start | bytes 1966088 | tf_op jit(solution)/shard_map/ppermute | solution.py:391
  54.2 27.8 %collective-permute-start.13 = (f32[32,40,128]{2,1,0:T(8,128)S(1)}, f32[32,40,128]{2,1,0:T(8,128)S(1)}, u32[]{:S(2)}, u32[]{:S(2)}) collective-permute-start(f32[32,40,128]{2,1,0:T(8,128)S(1)} %get-tuple-element.84), channel_id=1, source_target_pairs={{0,6},{2,0},{4,2},{6,4},{1,7},{3,1},{5,3},{7,5},{8,14},{10,8},{12,... | collective-permute-start | bytes 1966088 | tf_op jit(solution)/shard_map/ppermute | solution.py:395
  56.9 25.1 %copy-start.7 = (f32[40,40,128]{2,1,0:T(8,128)S(1)}, f32[40,40,128]{2,1,0:T(8,128)}, u32[]{:S(2)}) copy-start(f32[40,40,128]{2,1,0:T(8,128)} %get-tuple-element.96.refs_6_) | copy-start | bytes 2457604
  60.9 21.0 %collective-permute-start.14 = (f32[28,40,128]{2,1,0:T(8,128)S(1)}, f32[28,40,128]{2,1,0:T(8,128)S(1)}, u32[]{:S(2)}, u32[]{:S(2)}) collective-permute-start(f32[28,40,128]{2,1,0:T(8,128)S(1)} %get-tuple-element.86), channel_id=1, source_target_pairs={{0,2},{2,4},{4,6},{6,0},{1,3},{3,5},{5,7},{7,1},{8,10},{10,12},{12... | collective-permute-start | bytes 1720328 | tf_op jit(solution)/shard_map/ppermute | solution.py:391
  61.0 20.9 %collective-permute-start.15 = (f32[28,40,128]{2,1,0:T(8,128)S(1)}, f32[28,40,128]{2,1,0:T(8,128)S(1)}, u32[]{:S(2)}, u32[]{:S(2)}) collective-permute-start(f32[28,40,128]{2,1,0:T(8,128)S(1)} %get-tuple-element.87), channel_id=1, source_target_pairs={{0,6},{2,0},{4,2},{6,4},{1,7},{3,1},{5,3},{7,5},{8,14},{10,8},{12,... | collective-permute-start | bytes 1720328 | tf_op jit(solution)/shard_map/ppermute | solution.py:395
  82.0 47.6 %copy-start = (bf16[4,128,2,128]{3,2,1,0:T(2,128)(2,1)S(1)}, bf16[4,128,2,128]{3,2,1,0:T(2,128)(2,1)}, u32[]{:S(2)}) copy-start(bf16[4,128,2,128]{3,2,1,0:T(2,128)(2,1)} %param.14) | copy-start | bytes 786436
  84.7 35.0 %all-to-all-start.2 = ((f32[32,3,40,128]{3,2,1,0:T(8,128)}), f32[32,3,40,128]{3,2,1,0:T(8,128)}, u32[]{:S(2)}, u32[]{:S(2)}) async-start(f32[32,3,40,128]{3,2,1,0:T(8,128)} %get-tuple-element.95), calls=%async_computation.2 | async-start | bytes 3932160 | tf_op jit(solution)/shard_map/all_to_all | solution.py:491
  92.0 10.2 %collective-permute-start.10 = (f32[16,40,128]{2,1,0:T(8,128)S(1)}, f32[16,40,128]{2,1,0:T(8,128)S(1)}, u32[]{:S(2)}, u32[]{:S(2)}) collective-permute-start(f32[16,40,128]{2,1,0:T(8,128)S(1)} %bitcast.47), channel_id=1, source_target_pairs={{0,2},{2,4},{4,6},{6,0},{1,3},{3,5},{5,7},{7,1},{8,10},{10,12},{12... | collective-permute-start | bytes 983048 | tf_op jit(solution)/shard_map/ppermute | solution.py:391
  92.0 10.2 %collective-permute-start.11 = (f32[16,40,128]{2,1,0:T(8,128)S(1)}, f32[16,40,128]{2,1,0:T(8,128)S(1)}, u32[]{:S(2)}, u32[]{:S(2)}) collective-permute-start(f32[16,40,128]{2,1,0:T(8,128)S(1)} %bitcast.46), channel_id=1, source_target_pairs={{0,6},{2,0},{4,2},{6,4},{1,7},{3,1},{5,3},{7,5},{8,14},{10,8},{12,... | collective-permute-start | bytes 983048 | tf_op jit(solution)/shard_map/ppermute | solution.py:395
  102.4 16.4 %collective-permute-start.16 = (f32[32,40,128]{2,1,0:T(8,128)S(1)}, f32[32,40,128]{2,1,0:T(8,128)S(1)}, u32[]{:S(2)}, u32[]{:S(2)}) collective-permute-start(f32[32,40,128]{2,1,0:T(8,128)S(1)} %get-tuple-element.90), channel_id=1, source_target_pairs={{0,2},{2,4},{4,6},{6,0},{1,3},{3,5},{5,7},{7,1},{8,10},{10,12},{12... | collective-permute-start | bytes 1966088 | tf_op jit(solution)/shard_map/ppermute | solution.py:391
  103.3 15.5 %collective-permute-start.17 = (f32[32,40,128]{2,1,0:T(8,128)S(1)}, f32[32,40,128]{2,1,0:T(8,128)S(1)}, u32[]{:S(2)}, u32[]{:S(2)}) collective-permute-start(f32[32,40,128]{2,1,0:T(8,128)S(1)} %get-tuple-element.91), channel_id=1, source_target_pairs={{0,6},{2,0},{4,2},{6,4},{1,7},{3,1},{5,3},{7,5},{8,14},{10,8},{12,... | collective-permute-start | bytes 1966088 | tf_op jit(solution)/shard_map/ppermute | solution.py:395
  119.7 22.1 %all-to-all-start.1 = ((f32[32,40,128]{2,1,0:T(8,128)}), f32[32,40,128]{2,1,0:T(8,128)S(1)}, u32[]{:S(2)}, u32[]{:S(2)}) async-start(f32[32,40,128]{2,1,0:T(8,128)} %total.1), calls=%async_computation.1 | async-start | bytes 1310720 | tf_op jit(solution)/shard_map/all_to_all | solution.py:491
  130.2 0.8 copy-start.3
  131.0 0.8 copy-start.4
  141.8 0.8 copy-start.8

commit v5 on v4

--- a/solution.py
+++ b/solution.py
@@ -24,8 +24,8 @@
 SMEM = pl.BlockSpec(memory_space=pltpu.SMEM)
 NX = 4
 OWNERS = 32
-SECOND = 28
-SPARE = 40
+SECOND = 32
+SPARE = 32
 BLOCKS = 128
 
 
@@ -662,7 +662,7 @@
     right3, left3, keep3, token = rest(2, OWNERS, (token,))
 
     def further(_):
-        parts = (24, 16, SPARE, SPARE, SPARE)
+        parts = (half, half, SPARE, SPARE, SPARE)
         near, far, right, left, keep, _ = sums(12 * OWNERS, parts, parts, 8)
         right, left, _ = add_arrived(*first_hop(near, far), right, left)
         right, left = second_hop(right, left)

time: 146 us -> 147 us (level)
  waiting for transfers between devices: 49.9 us -> 52 us
  starting transfers between devices: 45 us -> 43.4 us
    ppermute x6, starting transfers between devices: 14.9 us -> 12.4 us  [to_left(): return lax.ppermute(value, 'row_0', [(i, (i - 1) % NX) for i in range(NX)])]
    ppermute x6, waiting for transfers between devices: 35.8 us -> 37.9 us  [to_right(): return lax.ppermute(value, 'row_0', [(i, (i + 1) % NX) for i in range(NX)])]
  transfers between devices with their start and end apart: 17 -> 17, of which waited for: 5 -> 6; matrix products, arithmetic and copies ran while one was open for 2% -> 2% of each run, Pallas kernels for 18% -> 18%
where the time goes in v5:
time: 147 us; the launch traced here: 146 us
  waiting for transfers between devices  52 us (35%)
  Pallas kernels  43.9 us (30%)
  starting transfers between devices  43.4 us (30%)
  local copies, waits for them, and re-layouts  5.36 us (4%)
  between operations  1.52 us (1%)
    ppermute x6, waiting for transfers between devices, to_right(): return lax.ppermute(value, 'row_0', [(i, (i + 1) % NX) for i in range(NX)])  37.9 us
    pallas_call x5, Pallas kernels, fourier(): pl.pallas_call(lambda *refs: fourier_kernel(low, pitches, len(after), str...  20.3 us
    all_to_all x2, starting transfers between devices, to_owners(): return lax.all_to_all(value, PLANE, split_axis=0, concat_axis=0, tiled=True)  16 us
    ppermute x6, starting transfers between devices, to_left(): return lax.ppermute(value, 'row_0', [(i, (i - 1) % NX) for i in range(NX)])  12.4 us
    all_to_all x1, starting transfers between devices, body(): table = lax.all_to_all(mine, KA_ROW, 0, 0, tiled=True)  10.6 us
    all_to_all x1, waiting for transfers between devices, body(): table = lax.all_to_all(mine, KA_ROW, 0, 0, tiled=True)  9.47 us
    pallas_call x2, Pallas kernels, curvature(): pl.pallas_call(lambda *refs: curvature_kernel(first, units, len(previous)...  8.15 us
    pallas_call x1, Pallas kernels, send_rows(): pl.pallas_call(send_kernel, out_shape=(jax.ShapeDtypeStruct(shape, f32),...  4.71 us
  transfers between devices with their start and end apart: 17, of which 6 were waited for; matrix products, arithmetic and copies ran while one was open for 2% of the time, Pallas kernels for 18%

profile of v5, /device:TPU:1, one launch (start us, length us, event | category | flops | bytes accessed | tf_op | source)
XLA Modules:
  0.0 146.2 jit_solution(1578342061561115662)
XLA Ops:
  0.0 4.7 %send_rows.1 = (f32[3,2,512,512]{3,2,1,0:T(8,128)}, f32[8,128]{1,0:T(8,128)}) custom-call(s32[1]{0:T(128)S(6)} %sub.3.core_ref, bf16[512,48,128]{2,1,0:T(8,128)(2,1)} %bitcast.54), custom_call_target="tpu_custom_call" | custom-call | flops 1250000000 | tf_op jit(solution)/shard_map/send_rows/pallas_call | solution.py:190
  4.7 1.5 collective-permute-start.5
  6.2 0.1 collective-permute-start.4
  7.0 0.1 copy.20.base_ref
  7.1 0.7 copy-done.1
  7.8 1.3 pack.1
  9.0 10.6 %all-to-all-start = ((f32[128,1,128]{2,1,0:T(1,128)}), f32[128,1,128]{2,1,0:T(1,128)S(1)}, u32[]{:S(2)}, u32[]{:S(2)}) async-start(f32[128,1,128]{2,1,0:T(1,128)} %pack.1), calls=%async_computation | async-start | bytes 131072 | tf_op jit(solution)/shard_map/all_to_all | solution.py:634
  19.6 9.5 %all-to-all-done = f32[128,1,128]{2,1,0:T(1,128)S(1)} async-done(((f32[128,1,128]{2,1,0:T(1,128)}), f32[128,1,128]{2,1,0:T(1,128)S(1)}, u32[]{:S(2)}, u32[]{:S(2)}) %all-to-all-start) | async-done | bytes 65568 | tf_op jit(solution)/shard_map/all_to_all | solution.py:634
  29.1 0.7 find_points.1
  29.8 4.0 %join_rows.1.refs_2_ = bf16[3,2048,512]{2,1,0:T(8,128)(2,1)S(1)} custom-call(s32[1]{0:T(128)} %bitcast.7.core_ref, bf16[512,48,128]{2,1,0:T(8,128)(2,1)} %bitcast.55, f32[3,2,512,512]{3,2,1,0:T(8,128)} %collective-permute-done.5.other_ref), custom_call_target="tpu_custom_call" | custom-call | flops 1250000000 | tf_op jit(solution)/shard_map/join_rows/pallas_call | solution.py:238
  33.8 3.7 %fourier.7 = (f32[640,128]{1,0:T(8,128)S(1)}, f32[640,128]{1,0:T(8,128)S(1)}, f32[8,128]{1,0:T(8,128)S(1)}) custom-call(f32[512,128]{1,0:T(8,128)S(1)} %get-tuple-element.62.refs_0_, f32[8,1024]{1,0:T(8,128)S(1)} %pad_maximum_fusion.refs_1_, bf16[3,2048,512]{2,1,0:T(8,128)(2,1)S(1)} %join_rows.1.refs_2_), custom_call_target="tpu_custom_call" | custom-call | flops 1000000000 | tf_op jit(solution)/shard_map/fourier/pallas_call | solution.py:376
  37.5 0.4 collective-permute-start.8
  37.9 2.4 %collective-permute-start.9 = (f32[16,40,128]{2,1,0:T(8,128)S(1)}, f32[16,40,128]{2,1,0:T(8,128)S(1)}, u32[]{:S(2)}, u32[]{:S(2)}) collective-permute-start(f32[16,40,128]{2,1,0:T(8,128)S(1)} %bitcast.49), channel_id=1, source_target_pairs={{0,6},{2,0},{4,2},{6,4},{1,7},{3,1},{5,3},{7,5},{8,14},{10,8},{12,... | collective-permute-start | bytes 983048 | tf_op jit(solution)/shard_map/ppermute | solution.py:395
  40.3 0.5 slice.3
  41.4 2.5 %fourier.8 = (f32[640,128]{1,0:T(8,128)S(1)}, f32[640,128]{1,0:T(8,128)S(1)}, f32[640,128]{1,0:T(8,128)S(1)}, f32[640,128]{1,0:T(8,128)S(1)}, f32[8,128]{1,0:T(8,128)S(1)}) custom-call(f32[512,128]{1,0:T(8,128)S(1)} %get-tuple-element.62.refs_0_, f32[8,1024]{1,0:T(8,128)S(1)} %pad_maximum_fusion.refs_1_, bf16[3,2048,512]{2,1,0:T(8,128)(2,1)S(1)} %join_rows.1.refs_2_, ...), custom_call_target="tpu_custom_call" | custom-call | flops 1000000000 | tf_op jit(solution)/shard_map/fourier/pallas_call | solution.py:376
  43.9 0.1 collective-permute-start.7
  44.0 0.9 conditional.1
  44.0 0.9 broadcast.2
  44.9 1.4 collective-permute-start.6
  46.3 6.6 %fourier.9 = (f32[1280,128]{1,0:T(8,128)S(1)}, f32[1280,128]{1,0:T(8,128)S(1)}, f32[1280,128]{1,0:T(8,128)S(1)}, f32[8,128]{1,0:T(8,128)}) custom-call(f32[512,128]{1,0:T(8,128)S(1)} %get-tuple-element.62.refs_0_, f32[8,1024]{1,0:T(8,128)S(1)} %pad_maximum_fusion.refs_1_, bf16[3,2048,512]{2,1,0:T(8,128)(2,1)} %copy-done.5, ...), custom_call_target="tpu_custom_call" | custom-call | flops 1250000000 | tf_op jit(solution)/shard_map/fourier/pallas_call | solution.py:376
  53.0 0.2 add_arrived.5
  53.2 0.1 collective-permute-start.12
  53.3 2.7 %collective-permute-start.13 = (f32[32,40,128]{2,1,0:T(8,128)S(1)}, f32[32,40,128]{2,1,0:T(8,128)S(1)}, u32[]{:S(2)}, u32[]{:S(2)}) collective-permute-start(f32[32,40,128]{2,1,0:T(8,128)S(1)} %get-tuple-element.84), channel_id=1, source_target_pairs={{0,6},{2,0},{4,2},{6,4},{1,7},{3,1},{5,3},{7,5},{8,14},{10,8},{12,... | collective-permute-start | bytes 1966088 | tf_op jit(solution)/shard_map/ppermute | solution.py:395
  56.0 3.9 %fourier.10 = (f32[1280,128]{1,0:T(8,128)S(1)}, f32[1280,128]{1,0:T(8,128)S(1)}, f32[1280,128]{1,0:T(8,128)S(1)}, f32[8,128]{1,0:T(8,128)}) custom-call(f32[512,128]{1,0:T(8,128)S(1)} %get-tuple-element.62.refs_0_, f32[8,1024]{1,0:T(8,128)S(1)} %pad_maximum_fusion.refs_1_, bf16[3,2048,512]{2,1,0:T(8,128)(2,1)S(1)} %copy-done.6, ...), custom_call_target="tpu_custom_call" | custom-call | flops 1250000000 | tf_op jit(solution)/shard_map/fourier/pallas_call | solution.py:376
  59.9 0.2 add_arrived.6
  60.1 0.1 collective-permute-start.14
  60.2 2.7 %collective-permute-start.15 = (f32[32,40,128]{2,1,0:T(8,128)S(1)}, f32[32,40,128]{2,1,0:T(8,128)S(1)}, u32[]{:S(2)}, u32[]{:S(2)}) collective-permute-start(f32[32,40,128]{2,1,0:T(8,128)S(1)} %get-tuple-element.87), channel_id=1, source_target_pairs={{0,6},{2,0},{4,2},{6,4},{1,7},{3,1},{5,3},{7,5},{8,14},{10,8},{12,... | collective-permute-start | bytes 1966088 | tf_op jit(solution)/shard_map/ppermute | solution.py:395
  62.8 3.6 %fourier.11 = (f32[1280,128]{1,0:T(8,128)S(1)}, f32[1280,128]{1,0:T(8,128)S(1)}, f32[1280,128]{1,0:T(8,128)S(1)}, f32[8,128]{1,0:T(8,128)S(1)}) custom-call(f32[512,128]{1,0:T(8,128)S(1)} %get-tuple-element.62.refs_0_, f32[8,1024]{1,0:T(8,128)S(1)} %pad_maximum_fusion.refs_1_, bf16[3,2048,512]{2,1,0:T(8,128)(2,1)S(1)} %copy-done.6, ...), custom_call_target="tpu_custom_call" | custom-call | flops 1250000000 | tf_op jit(solution)/shard_map/fourier/pallas_call | solution.py:376
  66.4 2.7 %collective-permute-done.12.refs_1_ = f32[32,40,128]{2,1,0:T(8,128)S(1)} collective-permute-done((f32[32,40,128]{2,1,0:T(8,128)S(1)}, f32[32,40,128]{2,1,0:T(8,128)S(1)}, u32[]{:S(2)}, u32[]{:S(2)}) %collective-permute-start.12) | collective-permute-done | bytes 655392 | tf_op jit(solution)/shard_map/ppermute | solution.py:391
  69.2 14.0 %collective-permute-done.14.refs_4_ = f32[32,40,128]{2,1,0:T(8,128)S(1)} collective-permute-done((f32[32,40,128]{2,1,0:T(8,128)S(1)}, f32[32,40,128]{2,1,0:T(8,128)S(1)}, u32[]{:S(2)}, u32[]{:S(2)}) %collective-permute-start.14) | collective-permute-done | bytes 655392 | tf_op jit(solution)/shard_map/ppermute | solution.py:391
  83.2 2.7 %place_slots.1 = (f32[32,3,40,128]{3,2,1,0:T(8,128)}, f32[8,128]{1,0:T(8,128)S(1)}) custom-call(s32[1]{0:T(128)} %bitcast.5.place_ref, s32[8,128]{1,0:T(8,128)S(1)} %get-tuple-element.81.slots_ref, f32[32,40,128]{2,1,0:T(8,128)S(1)} %bitcast.32, f32[32,40,128]{2,1,0:T(8,128)S(1)} %collective-permute-done.12.refs_1_, ...), custom_call_target="tpu_custom_call" | custom-call | flops 1000000000 | tf_op jit(solution)/shard_map/place_slots/pallas_call | solution.py:457
  86.0 6.8 %all-to-all-start.2 = ((f32[32,3,40,128]{3,2,1,0:T(8,128)}), f32[32,3,40,128]{3,2,1,0:T(8,128)}, u32[]{:S(2)}, u32[]{:S(2)}) async-start(f32[32,3,40,128]{3,2,1,0:T(8,128)} %get-tuple-element.95), calls=%async_computation.2 | async-start | bytes 3932160 | tf_op jit(solution)/shard_map/all_to_all | solution.py:491
  92.9 2.7 %collective-permute-start.11 = (f32[16,40,128]{2,1,0:T(8,128)S(1)}, f32[16,40,128]{2,1,0:T(8,128)S(1)}, u32[]{:S(2)}, u32[]{:S(2)}) collective-permute-start(f32[16,40,128]{2,1,0:T(8,128)S(1)} %bitcast.45), channel_id=1, source_target_pairs={{0,6},{2,0},{4,2},{6,4},{1,7},{3,1},{5,3},{7,5},{8,14},{10,8},{12,... | collective-permute-start | bytes 983048 | tf_op jit(solution)/shard_map/ppermute | solution.py:395
  95.6 7.4 %collective-permute-done.10.refs_0_ = f32[16,40,128]{2,1,0:T(8,128)S(1)} collective-permute-done((f32[16,40,128]{2,1,0:T(8,128)S(1)}, f32[16,40,128]{2,1,0:T(8,128)S(1)}, u32[]{:S(2)}, u32[]{:S(2)}) %collective-permute-start.10) | collective-permute-done | bytes 327712 | tf_op jit(solution)/shard_map/ppermute | solution.py:391
  103.0 0.2 add_arrived.7
  103.2 0.9 collective-permute-start.16
  104.1 1.8 %collective-permute-start.17 = (f32[32,40,128]{2,1,0:T(8,128)S(1)}, f32[32,40,128]{2,1,0:T(8,128)S(1)}, u32[]{:S(2)}, u32[]{:S(2)}) collective-permute-start(f32[32,40,128]{2,1,0:T(8,128)S(1)} %get-tuple-element.91), channel_id=1, source_target_pairs={{0,6},{2,0},{4,2},{6,4},{1,7},{3,1},{5,3},{7,5},{8,14},{10,8},{12,... | collective-permute-start | bytes 1966088 | tf_op jit(solution)/shard_map/ppermute | solution.py:395
  106.0 13.7 %collective-permute-done.16.right_ref = f32[32,40,128]{2,1,0:T(8,128)S(1)} collective-permute-done((f32[32,40,128]{2,1,0:T(8,128)S(1)}, f32[32,40,128]{2,1,0:T(8,128)S(1)}, u32[]{:S(2)}, u32[]{:S(2)}) %collective-permute-start.16) | collective-permute-done | bytes 655392 | tf_op jit(solution)/shard_map/ppermute | solution.py:391
  119.6 0.9 total.1
  120.5 9.2 %all-to-all-start.1 = ((f32[32,40,128]{2,1,0:T(8,128)}), f32[32,40,128]{2,1,0:T(8,128)S(1)}, u32[]{:S(2)}, u32[]{:S(2)}) async-start(f32[32,40,128]{2,1,0:T(8,128)} %total.1), calls=%async_computation.1 | async-start | bytes 1310720 | tf_op jit(solution)/shard_map/all_to_all | solution.py:491
  129.7 0.7 dynamic-slice_reduce_fusion.refs_0_
  130.4 0.5 vector_matrices.1
  131.0 0.8 copy-done.3
  131.8 0.8 copy-done.4
  132.6 5.4 %curvature.2.refs_5_ = f32[1,4]{1,0:T(1,128)} custom-call(f32[4]{0:T(128)} %dynamic-slice_reduce_fusion.refs_0_, f32[3840,128]{1,0:T(8,128)} %bitcast.29.refs_1_, bf16[4,256,256]{2,1,0:T(8,128)(2,1)} %copy-done.3, bf16[4,256,256]{2,1,0:T(8,128)(2,1)} %copy-done.4, s32[4,128]{1,0:T(4,128)} %refs_4_.3), custom_call_target="tpu_custom_call" | custom-call | flops 1875000064 | tf_op jit(solution)/shard_map/curvature/pallas_call | solution.py:557
  138.0 4.6 %all-to-all-done.1 = f32[32,40,128]{2,1,0:T(8,128)S(1)} async-done(((f32[32,40,128]{2,1,0:T(8,128)}), f32[32,40,128]{2,1,0:T(8,128)S(1)}, u32[]{:S(2)}, u32[]{:S(2)}) %all-to-all-start.1) | async-done | bytes 655392 | tf_op jit(solution)/shard_map/all_to_all | solution.py:491
  142.6 0.8 copy-done.8
  143.5 2.7 %curvature.3 = f32[1,4]{1,0:T(1,128)} custom-call(f32[4]{0:T(128)} %dynamic-slice_reduce_fusion.refs_0_, f32[1280,128]{1,0:T(8,128)} %bitcast.56, bf16[4,256,256]{2,1,0:T(8,128)(2,1)} %copy-done.3, bf16[4,256,256]{2,1,0:T(8,128)(2,1)} %copy-done.4, s32[4,128]{1,0:T(4,128)} %refs_4_.3, f32[1,4]{1,0:T(1,128)} %curvature.2.refs_5_), custom_call_target="tpu_custom_call" | custom-call | flops 625000000 | tf_op jit(solution)/shard_map/curvature/pallas_call | solution.py:557
  (33 shorter events, 0.2 us)
Async XLA Ops:
  0.0 6.2 %copy-start.9 = (s32[512,3]{0,1:T(4,128)S(1)}, s32[512,3]{0,1:T(4,128)}, u32[]{:S(2)}) copy-start(s32[512,3]{0,1:T(4,128)} %param.12) | copy-start | bytes 18436
  0.0 7.0 %copy-start.10 = (f32[8,3]{0,1:T(4,128)S(1)}, f32[8,3]{0,1:T(4,128)}, u32[]{:S(2)}) copy-start(f32[8,3]{0,1:T(4,128)} %param.9) | copy-start | bytes 292
  0.0 7.1 %copy-start.2 = (s32[8]{0:T(128)S(1)}, s32[8]{0:T(128)}, u32[]{:S(2)}) copy-start(s32[8]{0:T(128)} %counts_ref.1) | copy-start | bytes 100
  4.7 25.1 %collective-permute-start.5 = (f32[3,2,512,512]{3,2,1,0:T(8,128)}, f32[3,2,512,512]{3,2,1,0:T(8,128)}, u32[]{:S(2)}, u32[]{:S(2)}) collective-permute-start(f32[3,2,512,512]{3,2,1,0:T(8,128)} %get-tuple-element.63), channel_id=1, source_target_pairs={{0,1},{1,0},{2,3},{3,2},{4,5},{5,4},{6,7},{7,6},{8,9},{9,8},{10,11... | collective-permute-start | bytes 18874376 | tf_op jit(solution)/shard_map/ppermute | solution.py:630
  6.2 13.4 %collective-permute-start.4 = (f32[8,512]{1,0:T(8,128)S(1)}, f32[8,512]{1,0:T(8,128)S(1)}, u32[]{:S(2)}, u32[]{:S(2)}) collective-permute-start(f32[8,512]{1,0:T(8,128)S(1)} %pad.4), channel_id=1, source_target_pairs={{0,1},{1,0},{2,3},{3,2},{4,5},{5,4},{6,7},{7,6},{8,9},{9,8},{10,11... | collective-permute-start | bytes 49160 | tf_op jit(solution)/shard_map/ppermute | solution.py:632
  7.1 0.7 copy-start.1
  9.0 20.1 %all-to-all-start = ((f32[128,1,128]{2,1,0:T(1,128)}), f32[128,1,128]{2,1,0:T(1,128)S(1)}, u32[]{:S(2)}, u32[]{:S(2)}) async-start(f32[128,1,128]{2,1,0:T(1,128)} %pack.1), calls=%async_computation | async-start | bytes 131072 | tf_op jit(solution)/shard_map/all_to_all | solution.py:634
  33.8 10.2 %copy-start.5 = (bf16[3,2048,512]{2,1,0:T(8,128)(2,1)}, bf16[3,2048,512]{2,1,0:T(8,128)(2,1)S(1)}, u32[]{:S(2)}) copy-start(bf16[3,2048,512]{2,1,0:T(8,128)(2,1)S(1)} %join_rows.1.refs_2_) | copy-start | bytes 18874372
  37.5 15.5 %collective-permute-start.8 = (f32[16,40,128]{2,1,0:T(8,128)S(1)}, f32[16,40,128]{2,1,0:T(8,128)S(1)}, u32[]{:S(2)}, u32[]{:S(2)}) collective-permute-start(f32[16,40,128]{2,1,0:T(8,128)S(1)} %bitcast.50), channel_id=1, source_target_pairs={{0,2},{2,4},{4,6},{6,0},{1,3},{3,5},{5,7},{7,1},{8,10},{10,12},{12... | collective-permute-start | bytes 983048 | tf_op jit(solution)/shard_map/ppermute | solution.py:391
  37.9 15.1 %collective-permute-start.9 = (f32[16,40,128]{2,1,0:T(8,128)S(1)}, f32[16,40,128]{2,1,0:T(8,128)S(1)}, u32[]{:S(2)}, u32[]{:S(2)}) collective-permute-start(f32[16,40,128]{2,1,0:T(8,128)S(1)} %bitcast.49), channel_id=1, source_target_pairs={{0,6},{2,0},{4,2},{6,4},{1,7},{3,1},{5,3},{7,5},{8,14},{10,8},{12,... | collective-permute-start | bytes 983048 | tf_op jit(solution)/shard_map/ppermute | solution.py:395
  43.9 16.0 %collective-permute-start.7 = (f32[16,40,128]{2,1,0:T(8,128)S(1)}, f32[16,40,128]{2,1,0:T(8,128)S(1)}, u32[]{:S(2)}, u32[]{:S(2)}) collective-permute-start(f32[16,40,128]{2,1,0:T(8,128)S(1)} %bitcast.48), channel_id=1, source_target_pairs={{0,6},{2,0},{4,2},{6,4},{1,7},{3,1},{5,3},{7,5},{8,14},{10,8},{12,... | collective-permute-start | bytes 983048 | tf_op jit(solution)/shard_map/ppermute | solution.py:395
  44.9 11.0 %copy-start.6 = (bf16[3,2048,512]{2,1,0:T(8,128)(2,1)S(1)}, bf16[3,2048,512]{2,1,0:T(8,128)(2,1)}, u32[]{:S(2)}) copy-start(bf16[3,2048,512]{2,1,0:T(8,128)(2,1)} %copy-done.5) | copy-start | bytes 18874372
  44.9 15.0 %collective-permute-start.6 = (f32[16,40,128]{2,1,0:T(8,128)S(1)}, f32[16,40,128]{2,1,0:T(8,128)S(1)}, u32[]{:S(2)}, u32[]{:S(2)}) collective-permute-start(f32[16,40,128]{2,1,0:T(8,128)S(1)} %bitcast.47), channel_id=1, source_target_pairs={{0,2},{2,4},{4,6},{6,0},{1,3},{3,5},{5,7},{7,1},{8,10},{10,12},{12... | collective-permute-start | bytes 983048 | tf_op jit(solution)/shard_map/ppermute | solution.py:391
  53.2 15.9 %collective-permute-start.12 = (f32[32,40,128]{2,1,0:T(8,128)S(1)}, f32[32,40,128]{2,1,0:T(8,128)S(1)}, u32[]{:S(2)}, u32[]{:S(2)}) collective-permute-start(f32[32,40,128]{2,1,0:T(8,128)S(1)} %get-tuple-element.83), channel_id=1, source_target_pairs={{0,2},{2,4},{4,6},{6,0},{1,3},{3,5},{5,7},{7,1},{8,10},{10,12},{12... | collective-permute-start | bytes 1966088 | tf_op jit(solution)/shard_map/ppermute | solution.py:391
  53.3 15.9 %collective-permute-start.13 = (f32[32,40,128]{2,1,0:T(8,128)S(1)}, f32[32,40,128]{2,1,0:T(8,128)S(1)}, u32[]{:S(2)}, u32[]{:S(2)}) collective-permute-start(f32[32,40,128]{2,1,0:T(8,128)S(1)} %get-tuple-element.84), channel_id=1, source_target_pairs={{0,6},{2,0},{4,2},{6,4},{1,7},{3,1},{5,3},{7,5},{8,14},{10,8},{12,... | collective-permute-start | bytes 1966088 | tf_op jit(solution)/shard_map/ppermute | solution.py:395
  56.0 27.2 %copy-start.7 = (f32[32,40,128]{2,1,0:T(8,128)S(1)}, f32[32,40,128]{2,1,0:T(8,128)}, u32[]{:S(2)}) copy-start(f32[32,40,128]{2,1,0:T(8,128)} %get-tuple-element.96.refs_6_) | copy-start | bytes 1966084
  60.1 23.1 %collective-permute-start.14 = (f32[32,40,128]{2,1,0:T(8,128)S(1)}, f32[32,40,128]{2,1,0:T(8,128)S(1)}, u32[]{:S(2)}, u32[]{:S(2)}) collective-permute-start(f32[32,40,128]{2,1,0:T(8,128)S(1)} %get-tuple-element.86), channel_id=1, source_target_pairs={{0,2},{2,4},{4,6},{6,0},{1,3},{3,5},{5,7},{7,1},{8,10},{10,12},{12... | collective-permute-start | bytes 1966088 | tf_op jit(solution)/shard_map/ppermute | solution.py:391
  60.2 23.0 %collective-permute-start.15 = (f32[32,40,128]{2,1,0:T(8,128)S(1)}, f32[32,40,128]{2,1,0:T(8,128)S(1)}, u32[]{:S(2)}, u32[]{:S(2)}) collective-permute-start(f32[32,40,128]{2,1,0:T(8,128)S(1)} %get-tuple-element.87), channel_id=1, source_target_pairs={{0,6},{2,0},{4,2},{6,4},{1,7},{3,1},{5,3},{7,5},{8,14},{10,8},{12,... | collective-permute-start | bytes 1966088 | tf_op jit(solution)/shard_map/ppermute | solution.py:395
  83.2 47.2 %copy-start = (bf16[4,128,2,128]{3,2,1,0:T(2,128)(2,1)S(1)}, bf16[4,128,2,128]{3,2,1,0:T(2,128)(2,1)}, u32[]{:S(2)}) copy-start(bf16[4,128,2,128]{3,2,1,0:T(2,128)(2,1)} %param.14) | copy-start | bytes 786436
  86.0 34.6 %all-to-all-start.2 = ((f32[32,3,40,128]{3,2,1,0:T(8,128)}), f32[32,3,40,128]{3,2,1,0:T(8,128)}, u32[]{:S(2)}, u32[]{:S(2)}) async-start(f32[32,3,40,128]{3,2,1,0:T(8,128)} %get-tuple-element.95), calls=%async_computation.2 | async-start | bytes 3932160 | tf_op jit(solution)/shard_map/all_to_all | solution.py:491
  92.8 10.2 %collective-permute-start.10 = (f32[16,40,128]{2,1,0:T(8,128)S(1)}, f32[16,40,128]{2,1,0:T(8,128)S(1)}, u32[]{:S(2)}, u32[]{:S(2)}) collective-permute-start(f32[16,40,128]{2,1,0:T(8,128)S(1)} %bitcast.46), channel_id=1, source_target_pairs={{0,2},{2,4},{4,6},{6,0},{1,3},{3,5},{5,7},{7,1},{8,10},{10,12},{12... | collective-permute-start | bytes 983048 | tf_op jit(solution)/shard_map/ppermute | solution.py:391
  92.9 10.2 %collective-permute-start.11 = (f32[16,40,128]{2,1,0:T(8,128)S(1)}, f32[16,40,128]{2,1,0:T(8,128)S(1)}, u32[]{:S(2)}, u32[]{:S(2)}) collective-permute-start(f32[16,40,128]{2,1,0:T(8,128)S(1)} %bitcast.45), channel_id=1, source_target_pairs={{0,6},{2,0},{4,2},{6,4},{1,7},{3,1},{5,3},{7,5},{8,14},{10,8},{12,... | collective-permute-start | bytes 983048 | tf_op jit(solution)/shard_map/ppermute | solution.py:395
  103.2 16.4 %collective-permute-start.16 = (f32[32,40,128]{2,1,0:T(8,128)S(1)}, f32[32,40,128]{2,1,0:T(8,128)S(1)}, u32[]{:S(2)}, u32[]{:S(2)}) collective-permute-start(f32[32,40,128]{2,1,0:T(8,128)S(1)} %get-tuple-element.90), channel_id=1, source_target_pairs={{0,2},{2,4},{4,6},{6,0},{1,3},{3,5},{5,7},{7,1},{8,10},{10,12},{12... | collective-permute-start | bytes 1966088 | tf_op jit(solution)/shard_map/ppermute | solution.py:391
  104.1 15.5 %collective-permute-start.17 = (f32[32,40,128]{2,1,0:T(8,128)S(1)}, f32[32,40,128]{2,1,0:T(8,128)S(1)}, u32[]{:S(2)}, u32[]{:S(2)}) collective-permute-start(f32[32,40,128]{2,1,0:T(8,128)S(1)} %get-tuple-element.91), channel_id=1, source_target_pairs={{0,6},{2,0},{4,2},{6,4},{1,7},{3,1},{5,3},{7,5},{8,14},{10,8},{12,... | collective-permute-start | bytes 1966088 | tf_op jit(solution)/shard_map/ppermute | solution.py:395
  120.5 22.1 %all-to-all-start.1 = ((f32[32,40,128]{2,1,0:T(8,128)}), f32[32,40,128]{2,1,0:T(8,128)S(1)}, u32[]{:S(2)}, u32[]{:S(2)}) async-start(f32[32,40,128]{2,1,0:T(8,128)} %total.1), calls=%async_computation.1 | async-start | bytes 1310720 | tf_op jit(solution)/shard_map/all_to_all | solution.py:491
  131.0 0.8 copy-start.3
  131.8 0.8 copy-start.4
  142.6 0.8 copy-start.8

commit v6 on v5

--- a/solution.py
+++ b/solution.py
@@ -115,24 +115,6 @@
     points_ref[...] = points
 
 
-def find_points(table, plane):
-    rows = 12 * OWNERS + NX * SPARE
-    return pl.pallas_call(
-        index_kernel,
-        out_shape=(
-            jax.ShapeDtypeStruct((rows, BLOCKS), f32),
-            jax.ShapeDtypeStruct((8, BLOCKS), jnp.int32),
-            jax.ShapeDtypeStruct((8, BLOCKS), f32),
-        ),
-        in_specs=[SMEM, VMEM],
-        out_specs=(VMEM, VMEM, VMEM),
-        compiler_params=params(8),
-        cost_estimate=cost(2),
-        interpret=INTERPRET,
-        name="find_points",
-    )(plane, table)
-
-
 def pieces_of(depth):
     return [(matrix, slice(half * depth // 2, (half + 1) * depth // 2)) for matrix in range(3) for half in range(2)]
 
@@ -160,8 +142,10 @@
             store(part, slice(r * width, (r + 1) * width), wide_ref[pl.ds(2 * r + part, size, stride=rows), :])
 
 
-def send_kernel(core_ref, space_ref, out_ref, token_ref, in_buffer, out_buffer, wide_ref, in_sems, out_sems):
-    token_ref[...] = jnp.zeros(token_ref.shape, f32)
+def send_kernel(
+    core_ref, row_ref, base_ref, counts_ref, order_ref, space_ref, out_ref, told_ref, *scratch
+):
+    in_buffer, out_buffer, wide_ref, in_sems, out_sems = scratch
     depth = in_buffer.shape[1]
     coming = coming_rows(core_ref[0], space_ref, in_buffer, in_sems)
     places = pieces_of(depth)
@@ -171,6 +155,14 @@
     ]
     for copy in coming:
         copy.start()
+    lane = iota((1, BLOCKS), 1)
+    told = jnp.where(lane == 4, order_ref[...].astype(f32), 0.0)
+    own = iota((1, 8), 1) == row_ref[0]
+    told = jnp.where(lane == 3, jnp.sum(jnp.where(own, counts_ref[...].astype(f32), 0.0), axis=1, keepdims=True), told)
+    for axis in range(3):
+        part = jnp.where(own, base_ref[axis : axis + 1, :], 0.0)
+        told = jnp.where(lane == axis, jnp.sum(part, axis=1, keepdims=True), told)
+    told_ref[...] = jnp.broadcast_to(told.reshape(1, 1, BLOCKS), told_ref.shape)
     for k, (matrix, at) in enumerate(places):
         coming[k].wait()
 
@@ -183,14 +175,14 @@
         copy.wait()
 
 
-def send_rows(space, core):
+def send_rows(space, core, row, base_k, counts, block_order):
     depth, rows, width = space.shape
     half = rows // 6
     shape = (3, 2, depth, half // 2 * width)
     return pl.pallas_call(
         send_kernel,
-        out_shape=(jax.ShapeDtypeStruct(shape, f32), jax.ShapeDtypeStruct((8, BLOCKS), f32)),
-        in_specs=[SMEM, HBM],
+        out_shape=(jax.ShapeDtypeStruct(shape, f32), jax.ShapeDtypeStruct((BLOCKS, 1, BLOCKS), f32)),
+        in_specs=[SMEM, SMEM, VMEM, VMEM, VMEM, HBM],
         out_specs=(HBM, VMEM),
         scratch_shapes=[
             pltpu.VMEM((3, depth, half, width), bf16),
@@ -203,7 +195,7 @@
         cost_estimate=cost(5),
         interpret=INTERPRET,
         name="send_rows",
-    )(core, space)
+    )(core, row, base_k.T, counts.reshape(1, 8), block_order.reshape(1, 1), space)
 
 
 def join_kernel(core_ref, space_ref, other_ref, out_ref, in_buffer, other_buffer, wide_ref, in_sems, other_sems):
@@ -252,31 +244,6 @@
         interpret=INTERPRET,
         name="join_rows",
     )(core, space, other)
-
-
-def pack_kernel(row_ref, base_ref, counts_ref, order_ref, *refs):
-    out_ref = refs[-1]
-    row = row_ref[0]
-    lane = iota((1, 1, BLOCKS), 2)
-    value = jnp.zeros((1, 1, BLOCKS), f32)
-    for axis in range(3):
-        value = jnp.where(lane == axis, base_ref[row, axis], value)
-    value = jnp.where(lane == 3, counts_ref[row].astype(f32), value)
-    value = jnp.where(lane == 4, order_ref[0].astype(f32), value)
-    out_ref[...] = jnp.broadcast_to(value, out_ref.shape)
-
-
-def pack(row, base_k, counts, block_order, after):
-    return pl.pallas_call(
-        pack_kernel,
-        out_shape=jax.ShapeDtypeStruct((BLOCKS, 1, BLOCKS), f32),
-        in_specs=[SMEM] * 4 + [ANY] * len(after),
-        out_specs=VMEM,
-        compiler_params=params(4),
-        cost_estimate=cost(1),
-        interpret=INTERPRET,
-        name="pack",
-    )(row, base_k, counts, block_order, *after)
 
 
 def turn(points, coords):
@@ -340,51 +307,85 @@
 PLACES = tuple((matrix, part) for matrix in range(3) for part in range(2))
 
 
-def fourier_kernel(low, pitches, waits, streamed, points_ref, coords_ref, matrices_ref, *refs):
+def fourier_kernel(low, pitches, waits, points_ref, coords_ref, matrices_ref, *refs):
     refs = refs[waits:]
     outs = len(pitches)
     out_refs, token_ref, phase_ref = refs[:outs], refs[outs], refs[outs + 1]
     token_ref[...] = jnp.zeros(token_ref.shape, f32)
     count = sum(pitches)
     lanes = matrices_ref.shape[2] // 2
-    copies = []
-    if streamed:
-        buffer_ref, sems = refs[outs + 2 :]
-        for k, (matrix, part) in enumerate(PLACES):
-            source = matrices_ref.at[matrix, :, pl.ds(part * lanes, lanes)]
-            copies.append(pltpu.make_async_copy(source, buffer_ref.at[k], sems.at[k]))
-        for copy in copies:
-            copy.start()
     store_phases(low, count, points_ref, coords_ref, phase_ref)
-    for k, (matrix, part) in enumerate(PLACES):
+    for matrix, part in PLACES:
         kinds, first_kind = (6, 0) if matrix == 0 else (2, 4 + 2 * matrix)
-        if streamed:
-            copies[k].wait()
-            block = buffer_ref[k]
-        else:
-            block = matrices_ref[matrix, :, part * lanes : (part + 1) * lanes]
+        block = matrices_ref[matrix, :, part * lanes : (part + 1) * lanes]
         store_sums(phase_ref, block, count, kinds, first_kind, 2 * part, out_refs, pitches)
 
 
-def fourier(points, low, sizes, pitches, coords, matrices, microseconds, after=(), streamed=False):
+def fourier(points, low, sizes, pitches, coords, matrices, microseconds, after=()):
     depth4 = matrices.shape[1]
     width = matrices.shape[2] // 4
     shapes = tuple(jax.ShapeDtypeStruct((size * 40, width), f32) for size in sizes)
-    scratch = [pltpu.VMEM((6 * sum(pitches), depth4), bf16)]
-    if streamed:
-        scratch += [pltpu.VMEM((6, depth4, 2 * width), bf16), pltpu.SemaphoreType.DMA((6,))]
     outs = pl.pallas_call(
-        lambda *refs: fourier_kernel(low, pitches, len(after), streamed, *refs),
+        lambda *refs: fourier_kernel(low, pitches, len(after), *refs),
         out_shape=shapes + (jax.ShapeDtypeStruct((8, BLOCKS), f32),),
-        in_specs=[VMEM, VMEM, HBM if streamed else VMEM] + [ANY] * len(after),
+        in_specs=[VMEM, VMEM, VMEM] + [ANY] * len(after),
         out_specs=(VMEM,) * (len(shapes) + 1),
-        scratch_shapes=scratch,
+        scratch_shapes=[pltpu.VMEM((6 * sum(pitches), depth4), bf16)],
         compiler_params=params(18),
         cost_estimate=cost(microseconds),
         interpret=INTERPRET,
         name="fourier",
     )(points, coords, matrices, *after)
     return tuple(out.reshape(-1, 40, width) for out in outs[:-1]) + (outs[-1],)
+
+
+def first_kernel(place_ref, table_ref, coords_ref, matrices_ref, *refs):
+    near_ref, far_ref, points_ref, slots_ref, weight_ref, token_ref, phase_ref, buffer_ref, sems = refs
+    token_ref[...] = jnp.zeros(token_ref.shape, f32)
+    lanes = matrices_ref.shape[2] // 2
+    copies = []
+    for k, (matrix, part) in enumerate(PLACES):
+        source = matrices_ref.at[matrix, :, pl.ds(part * lanes, lanes)]
+        copies.append(pltpu.make_async_copy(source, buffer_ref.at[k], sems.at[k]))
+    for copy in copies:
+        copy.start()
+    index_kernel(place_ref, table_ref, points_ref, slots_ref, weight_ref)
+    store_phases(0, OWNERS, points_ref, coords_ref, phase_ref)
+    for k, (matrix, part) in enumerate(PLACES):
+        kinds, first_kind = (6, 0) if matrix == 0 else (2, 4 + 2 * matrix)
+        copies[k].wait()
+        store_sums(
+            phase_ref, buffer_ref[k], OWNERS, kinds, first_kind, 2 * part, (near_ref, far_ref), (OWNERS // 2,) * 2
+        )
+
+
+def first_fourier(table, plane, coords, matrices):
+    depth4 = matrices.shape[1]
+    width = matrices.shape[2] // 4
+    side = jax.ShapeDtypeStruct((OWNERS // 2 * 40, width), f32)
+    near, far, points, slots, weights, token = pl.pallas_call(
+        first_kernel,
+        out_shape=(
+            side,
+            side,
+            jax.ShapeDtypeStruct((12 * OWNERS + NX * SPARE, BLOCKS), f32),
+            jax.ShapeDtypeStruct((8, BLOCKS), jnp.int32),
+            jax.ShapeDtypeStruct((8, BLOCKS), f32),
+            jax.ShapeDtypeStruct((8, BLOCKS), f32),
+        ),
+        in_specs=[SMEM, VMEM, VMEM, HBM],
+        out_specs=(VMEM,) * 6,
+        scratch_shapes=[
+            pltpu.VMEM((6 * OWNERS, depth4), bf16),
+            pltpu.VMEM((6, depth4, 2 * width), bf16),
+            pltpu.SemaphoreType.DMA((6,)),
+        ],
+        compiler_params=params(18),
+        cost_estimate=cost(5),
+        interpret=INTERPRET,
+        name="first_fourier",
+    )(plane, table, coords, matrices)
+    return near.reshape(-1, 40, width), far.reshape(-1, 40, width), points, slots, weights, token
 
 
 def to_right(value):
@@ -625,8 +626,8 @@
 
     space = real_space.reshape(depth, 6 * slab, width)
     swap = [(0, 1), (1, 0)]
-    send, token = send_rows(space, 1 - core_ref)
-    mine = pack(row.reshape(1).astype(jnp.int32), base_k, counts, block_order, (token,))
+    row_ref = row.reshape(1).astype(jnp.int32)
+    send, mine = send_rows(space, 1 - core_ref, row_ref, base_k, counts, block_order)
     other = lax.ppermute(send, "row_1", swap)
     own_coords = jnp.pad(lattice.T.astype(f32), ((0, 5), (0, 0)))
     coords = jnp.concatenate([own_coords, lax.ppermute(own_coords, "row_1", swap)], axis=1)
@@ -634,19 +635,18 @@
     table = lax.all_to_all(mine, KA_ROW, 0, 0, tiled=True)
     table = table.reshape(BLOCKS, BLOCKS)
     matrices = join_rows(space, core_ref, other)
-    points, slots, weights = find_points(table, plane_ref)
+    near0, far0, points, slots, weights, token = first_fourier(table, plane_ref, coords, matrices)
     position = (lax.axis_index(KA) * 8 + row).astype(jnp.int32)
     weight = lax.dynamic_slice(weights, (jnp.int32(0), position), (SUB, 1)).reshape(SUB)
 
     half = OWNERS // 2
 
-    def sums(low, sizes, pitches, microseconds, after=(), streamed=False):
-        return fourier(points, low, sizes, pitches, coords, matrices, microseconds, after, streamed)
+    def sums(low, sizes, pitches, microseconds, after=()):
+        return fourier(points, low, sizes, pitches, coords, matrices, microseconds, after)
 
     def rest(chunk, size, after):
         return sums(3 * OWNERS * (1 + chunk), (size,) * 3, (OWNERS,) * 3, 5, after)
 
-    near0, far0, token = sums(0, (half, half), (half, half), 4, (), True)
     hop0 = first_hop(near0, far0)
     near1, far1, near3, far3, token = sums(
         OWNERS, (half, SECOND - half, half, half), (half,) * 4, 4, (token,)

time: 147 us -> 142 us (0.966)
  waiting for transfers between devices: 52 us -> 42.7 us
  Pallas kernels: 43.9 us -> 48.9 us
    all_to_all x1, waiting for transfers between devices: 9.47 us -> 2.8 us  [body(): table = lax.all_to_all(mine, KA_ROW, 0, 0, tiled=True)]
    pallas_call x1, Pallas kernels: 3.98 us -> 6.65 us  [join_rows(): pl.pallas_call(join_kernel, out_shape=jax.ShapeDtypeStruct((3, 4 * depth,...]
    ppermute x6, waiting for transfers between devices: 37.9 us -> 35.3 us  [to_right(): return lax.ppermute(value, 'row_0', [(i, (i + 1) % NX) for i in range(NX)])]
    pallas_call x7 -> x5, Pallas kernels: 22.3 us -> 23.9 us  [the longest x4 18.9 us: fourier(): pl.pallas_call(lambda *refs: fourier_kernel(low, pitches, len(after), *re...]
    unnamed x23 -> x18, local copies, waits for them, and re-layouts: 3.23 us -> 2.46 us
  transfers between devices with their start and end apart: 17 -> 17, of which waited for: 6 -> 5; matrix products, arithmetic and copies ran while one was open for 2% -> 2% of each run, Pallas kernels for 18% -> 23%
where the time goes in v6:
time: 142 us
  Pallas kernels  48.9 us (34%)
  starting transfers between devices  44 us (31%)
  waiting for transfers between devices  42.7 us (30%)
  local copies, waits for them, and re-layouts  4.6 us (3%)
  between operations  1.54 us (1%)
    ppermute x6, waiting for transfers between devices, to_right(): return lax.ppermute(value, 'row_0', [(i, (i + 1) % NX) for i in range(NX)])  35.3 us
    pallas_call x4, Pallas kernels, fourier(): pl.pallas_call(lambda *refs: fourier_kernel(low, pitches, len(after), *re...  18.9 us
    all_to_all x2, starting transfers between devices, to_owners(): return lax.all_to_all(value, PLANE, split_axis=0, concat_axis=0, tiled=True)  16.6 us
    ppermute x6, starting transfers between devices, to_left(): return lax.ppermute(value, 'row_0', [(i, (i - 1) % NX) for i in range(NX)])  12.1 us
    all_to_all x1, starting transfers between devices, body(): table = lax.all_to_all(mine, KA_ROW, 0, 0, tiled=True)  10.6 us
    pallas_call x2, Pallas kernels, curvature(): pl.pallas_call(lambda *refs: curvature_kernel(first, units, len(previous)...  8.15 us
    pallas_call x1, Pallas kernels, join_rows(): pl.pallas_call(join_kernel, out_shape=jax.ShapeDtypeStruct((3, 4 * depth,...  6.65 us
    pallas_call x1, Pallas kernels, send_rows(): pl.pallas_call(send_kernel, out_shape=(jax.ShapeDtypeStruct(shape, f32),...  5.41 us
  transfers between devices with their start and end apart: 17, of which 5 were waited for; matrix products, arithmetic and copies ran while one was open for 2% of the time, Pallas kernels for 23%

profile of v6, /device:TPU:1, one launch (start us, length us, event | category | flops | bytes accessed | tf_op | source)
XLA Modules:
  0.0 141.7 jit_solution(6862674520270951866)
XLA Ops:
  0.7 5.4 %send_rows.1 = (f32[3,2,512,512]{3,2,1,0:T(8,128)}, f32[128,1,128]{2,1,0:T(1,128)}) custom-call(s32[1]{0:T(128)S(6)} %sub.3.core_ref, s32[1]{0:T(128)} %bitcast.7.row_ref, f32[3,8]{1,0:T(4,128)} %bitcast.63, s32[1,8]{1,0:T(1,128)} %bitcast.64, s32[1,1]{1,0:T(1,128)} %bitcast.35.order_ref, bf16[512,48,128]{2,1,0:T(8,128)(2,1)} %bitcast.60), custom_call_target="tpu_custom_call" | custom-call | flops 1250000000 | tf_op jit(solution)/shard_map/send_rows/pallas_call | solution.py:182
  6.1 1.5 %collective-permute-start.5 = (f32[3,2,512,512]{3,2,1,0:T(8,128)}, f32[3,2,512,512]{3,2,1,0:T(8,128)}, u32[]{:S(2)}, u32[]{:S(2)}) collective-permute-start(f32[3,2,512,512]{3,2,1,0:T(8,128)} %get-tuple-element.61), channel_id=1, source_target_pairs={{0,1},{1,0},{2,3},{3,2},{4,5},{5,4},{6,7},{7,6},{8,9},{9,8},{10,11... | collective-permute-start | bytes 18874376 | tf_op jit(solution)/shard_map/ppermute | solution.py:631
  7.6 0.1 collective-permute-start.4
  7.7 10.6 %all-to-all-start = ((f32[128,1,128]{2,1,0:T(1,128)}), f32[128,1,128]{2,1,0:T(1,128)S(1)}, u32[]{:S(2)}, u32[]{:S(2)}) async-start(f32[128,1,128]{2,1,0:T(1,128)} %get-tuple-element.60), calls=%async_computation | async-start | bytes 131072 | tf_op jit(solution)/shard_map/all_to_all | solution.py:635
  18.3 6.6 %join_rows.1.matrices_ref.refs_2_ = bf16[3,2048,512]{2,1,0:T(8,128)(2,1)} custom-call(s32[1]{0:T(128)} %bitcast.6.core_ref, bf16[512,48,128]{2,1,0:T(8,128)(2,1)} %bitcast.61, f32[3,2,512,512]{3,2,1,0:T(8,128)} %collective-permute-done.5.other_ref), custom_call_target="tpu_custom_call" | custom-call | flops 1250000000 | tf_op jit(solution)/shard_map/join_rows/pallas_call | solution.py:230
  25.0 2.8 %all-to-all-done = f32[128,1,128]{2,1,0:T(1,128)S(1)} async-done(((f32[128,1,128]{2,1,0:T(1,128)}), f32[128,1,128]{2,1,0:T(1,128)S(1)}, u32[]{:S(2)}, u32[]{:S(2)}) %all-to-all-start) | async-done | bytes 65568 | tf_op jit(solution)/shard_map/all_to_all | solution.py:635
  27.8 5.0 %first_fourier.1 = (f32[640,128]{1,0:T(8,128)S(1)}, f32[640,128]{1,0:T(8,128)S(1)}, f32[512,128]{1,0:T(8,128)S(1)}, s32[8,128]{1,0:T(8,128)S(1)}, f32[8,128]{1,0:T(8,128)S(1)}, /*index=5*/f32[8,128]{1,0:T(8,128)S(1)}) custom-call(s32[1]{0:T(128)} %bitcast.5.place_ref, f32[128,128]{1,0:T(8,128)S(1)} %bitcast.48, ...), custom_call_target="tpu_custom_call" | custom-call | flops 1250000000 | tf_op jit(solution)/shard_map/first_fourier/pallas_call | solution.py:366
  32.8 0.4 collective-permute-start.8
  33.1 2.4 %collective-permute-start.9 = (f32[16,40,128]{2,1,0:T(8,128)S(1)}, f32[16,40,128]{2,1,0:T(8,128)S(1)}, u32[]{:S(2)}, u32[]{:S(2)}) collective-permute-start(f32[16,40,128]{2,1,0:T(8,128)S(1)} %bitcast.53), channel_id=1, source_target_pairs={{0,6},{2,0},{4,2},{6,4},{1,7},{3,1},{5,3},{7,5},{8,14},{10,8},{12,... | collective-permute-start | bytes 983048 | tf_op jit(solution)/shard_map/ppermute | solution.py:396
  35.5 0.5 slice.3
  36.7 2.5 %fourier.6 = (f32[640,128]{1,0:T(8,128)S(1)}, f32[640,128]{1,0:T(8,128)S(1)}, f32[640,128]{1,0:T(8,128)S(1)}, f32[640,128]{1,0:T(8,128)S(1)}, f32[8,128]{1,0:T(8,128)S(1)}) custom-call(f32[512,128]{1,0:T(8,128)S(1)} %get-tuple-element.63.refs_0_, f32[8,1024]{1,0:T(8,128)S(1)} %pad_maximum_fusion.coords_ref.refs_1_, bf16[3,2048,512]{2,1,0:T(8,128)(2,1)S(1)} %copy-done.3, ...), custom_call_target="tpu_custom_call" | custom-call | flops 1000000000 | tf_op jit(solution)/shard_map/fourier/pallas_call | solution.py:328
  39.2 0.1 collective-permute-start.7
  39.3 0.9 conditional.1
  39.3 0.9 broadcast.2
  40.2 1.4 %collective-permute-start.6 = (f32[16,40,128]{2,1,0:T(8,128)S(1)}, f32[16,40,128]{2,1,0:T(8,128)S(1)}, u32[]{:S(2)}, u32[]{:S(2)}) collective-permute-start(f32[16,40,128]{2,1,0:T(8,128)S(1)} %bitcast.51), channel_id=1, source_target_pairs={{0,2},{2,4},{4,6},{6,0},{1,3},{3,5},{5,7},{7,1},{8,10},{10,12},{12... | collective-permute-start | bytes 983048 | tf_op jit(solution)/shard_map/ppermute | solution.py:392
  41.6 6.4 %fourier.7 = (f32[1280,128]{1,0:T(8,128)S(1)}, f32[1280,128]{1,0:T(8,128)S(1)}, f32[1280,128]{1,0:T(8,128)S(1)}, f32[8,128]{1,0:T(8,128)}) custom-call(f32[512,128]{1,0:T(8,128)S(1)} %get-tuple-element.63.refs_0_, f32[8,1024]{1,0:T(8,128)S(1)} %pad_maximum_fusion.coords_ref.refs_1_, bf16[3,2048,512]{2,1,0:T(8,128)(2,1)} %join_rows.1.matrices_ref.refs_2_, ...), custom_call_target="tpu_custom_call" | custom-call | flops 1250000000 | tf_op jit(solution)/shard_map/fourier/pallas_call | solution.py:328
  48.0 0.0 collective-permute-done.8.refs_0_
  48.0 0.0 collective-permute-done.9.refs_1_
  48.0 0.2 add_arrived.5
  48.2 0.1 collective-permute-start.12
  48.3 2.7 %collective-permute-start.13 = (f32[32,40,128]{2,1,0:T(8,128)S(1)}, f32[32,40,128]{2,1,0:T(8,128)S(1)}, u32[]{:S(2)}, u32[]{:S(2)}) collective-permute-start(f32[32,40,128]{2,1,0:T(8,128)S(1)} %get-tuple-element.84), channel_id=1, source_target_pairs={{0,6},{2,0},{4,2},{6,4},{1,7},{3,1},{5,3},{7,5},{8,14},{10,8},{12,... | collective-permute-start | bytes 1966088 | tf_op jit(solution)/shard_map/ppermute | solution.py:396
  51.0 6.4 %fourier.8 = (f32[1280,128]{1,0:T(8,128)S(1)}, f32[1280,128]{1,0:T(8,128)S(1)}, f32[1280,128]{1,0:T(8,128)S(1)}, f32[8,128]{1,0:T(8,128)}) custom-call(f32[512,128]{1,0:T(8,128)S(1)} %get-tuple-element.63.refs_0_, f32[8,1024]{1,0:T(8,128)S(1)} %pad_maximum_fusion.coords_ref.refs_1_, bf16[3,2048,512]{2,1,0:T(8,128)(2,1)} %join_rows.1.matrices_ref.refs_2_, ...), custom_call_target="tpu_custom_call" | custom-call | flops 1250000000 | tf_op jit(solution)/shard_map/fourier/pallas_call | solution.py:328
  57.4 0.0 collective-permute-done.6.refs_0_
  57.4 0.2 add_arrived.6
  57.6 0.1 collective-permute-start.14
  57.7 2.7 %collective-permute-start.15 = (f32[32,40,128]{2,1,0:T(8,128)S(1)}, f32[32,40,128]{2,1,0:T(8,128)S(1)}, u32[]{:S(2)}, u32[]{:S(2)}) collective-permute-start(f32[32,40,128]{2,1,0:T(8,128)S(1)} %get-tuple-element.87), channel_id=1, source_target_pairs={{0,6},{2,0},{4,2},{6,4},{1,7},{3,1},{5,3},{7,5},{8,14},{10,8},{12,... | collective-permute-start | bytes 1966088 | tf_op jit(solution)/shard_map/ppermute | solution.py:396
  60.4 3.6 %fourier.9 = (f32[1280,128]{1,0:T(8,128)S(1)}, f32[1280,128]{1,0:T(8,128)S(1)}, f32[1280,128]{1,0:T(8,128)S(1)}, f32[8,128]{1,0:T(8,128)S(1)}) custom-call(f32[512,128]{1,0:T(8,128)S(1)} %get-tuple-element.63.refs_0_, f32[8,1024]{1,0:T(8,128)S(1)} %pad_maximum_fusion.coords_ref.refs_1_, bf16[3,2048,512]{2,1,0:T(8,128)(2,1)S(1)} %bitcast.59, ...), custom_call_target="tpu_custom_call" | custom-call | flops 1250000000 | tf_op jit(solution)/shard_map/fourier/pallas_call | solution.py:328
  64.0 0.0 collective-permute-done.13.refs_2_
  64.0 13.9 %collective-permute-done.14.refs_4_ = f32[32,40,128]{2,1,0:T(8,128)S(1)} collective-permute-done((f32[32,40,128]{2,1,0:T(8,128)S(1)}, f32[32,40,128]{2,1,0:T(8,128)S(1)}, u32[]{:S(2)}, u32[]{:S(2)}) %collective-permute-start.14) | collective-permute-done | bytes 655392 | tf_op jit(solution)/shard_map/ppermute | solution.py:392
  77.9 2.7 %place_slots.1 = (f32[32,3,40,128]{3,2,1,0:T(8,128)}, f32[8,128]{1,0:T(8,128)S(1)}) custom-call(s32[1]{0:T(128)} %bitcast.5.place_ref, s32[8,128]{1,0:T(8,128)S(1)} %get-tuple-element.81.slots_ref, f32[32,40,128]{2,1,0:T(8,128)S(1)} %bitcast.36, f32[32,40,128]{2,1,0:T(8,128)S(1)} %collective-permute-done.12.refs_1_, ...), custom_call_target="tpu_custom_call" | custom-call | flops 1000000000 | tf_op jit(solution)/shard_map/place_slots/pallas_call | solution.py:458
  80.6 7.8 %all-to-all-start.2 = ((f32[32,3,40,128]{3,2,1,0:T(8,128)}), f32[32,3,40,128]{3,2,1,0:T(8,128)}, u32[]{:S(2)}, u32[]{:S(2)}) async-start(f32[32,3,40,128]{3,2,1,0:T(8,128)} %get-tuple-element.95), calls=%async_computation.2 | async-start | bytes 3932160 | tf_op jit(solution)/shard_map/all_to_all | solution.py:492
  88.4 0.6 collective-permute-start.10
  89.0 2.1 %collective-permute-start.11 = (f32[16,40,128]{2,1,0:T(8,128)S(1)}, f32[16,40,128]{2,1,0:T(8,128)S(1)}, u32[]{:S(2)}, u32[]{:S(2)}) collective-permute-start(f32[16,40,128]{2,1,0:T(8,128)S(1)} %bitcast.49), channel_id=1, source_target_pairs={{0,6},{2,0},{4,2},{6,4},{1,7},{3,1},{5,3},{7,5},{8,14},{10,8},{12,... | collective-permute-start | bytes 983048 | tf_op jit(solution)/shard_map/ppermute | solution.py:396
  91.2 7.6 %collective-permute-done.10.refs_0_ = f32[16,40,128]{2,1,0:T(8,128)S(1)} collective-permute-done((f32[16,40,128]{2,1,0:T(8,128)S(1)}, f32[16,40,128]{2,1,0:T(8,128)S(1)}, u32[]{:S(2)}, u32[]{:S(2)}) %collective-permute-start.10) | collective-permute-done | bytes 327712 | tf_op jit(solution)/shard_map/ppermute | solution.py:392
  98.8 0.2 add_arrived.7
  99.0 0.6 collective-permute-start.16
  99.6 2.2 %collective-permute-start.17 = (f32[32,40,128]{2,1,0:T(8,128)S(1)}, f32[32,40,128]{2,1,0:T(8,128)S(1)}, u32[]{:S(2)}, u32[]{:S(2)}) collective-permute-start(f32[32,40,128]{2,1,0:T(8,128)S(1)} %get-tuple-element.91), channel_id=1, source_target_pairs={{0,6},{2,0},{4,2},{6,4},{1,7},{3,1},{5,3},{7,5},{8,14},{10,8},{12,... | collective-permute-start | bytes 1966088 | tf_op jit(solution)/shard_map/ppermute | solution.py:396
  101.7 13.8 %collective-permute-done.16.right_ref = f32[32,40,128]{2,1,0:T(8,128)S(1)} collective-permute-done((f32[32,40,128]{2,1,0:T(8,128)S(1)}, f32[32,40,128]{2,1,0:T(8,128)S(1)}, u32[]{:S(2)}, u32[]{:S(2)}) %collective-permute-start.16) | collective-permute-done | bytes 655392 | tf_op jit(solution)/shard_map/ppermute | solution.py:392
  115.5 0.9 total.1
  116.4 8.8 %all-to-all-start.1 = ((f32[32,40,128]{2,1,0:T(8,128)}), f32[32,40,128]{2,1,0:T(8,128)S(1)}, u32[]{:S(2)}, u32[]{:S(2)}) async-start(f32[32,40,128]{2,1,0:T(8,128)} %total.1), calls=%async_computation.1 | async-start | bytes 1310720 | tf_op jit(solution)/shard_map/all_to_all | solution.py:492
  125.3 0.7 dynamic-slice_reduce_fusion.refs_0_
  126.0 0.5 vector_matrices.1
  126.5 0.8 copy-done.1
  127.3 0.8 copy-done.2
  128.1 5.4 %curvature.2.refs_5_ = f32[1,4]{1,0:T(1,128)} custom-call(f32[4]{0:T(128)} %dynamic-slice_reduce_fusion.refs_0_, f32[3840,128]{1,0:T(8,128)} %bitcast.32.refs_1_, bf16[4,256,256]{2,1,0:T(8,128)(2,1)} %copy-done.1, bf16[4,256,256]{2,1,0:T(8,128)(2,1)} %copy-done.2, s32[4,128]{1,0:T(4,128)} %refs_4_.3), custom_call_target="tpu_custom_call" | custom-call | flops 1875000064 | tf_op jit(solution)/shard_map/curvature/pallas_call | solution.py:558
  133.5 4.6 %all-to-all-done.1 = f32[32,40,128]{2,1,0:T(8,128)S(1)} async-done(((f32[32,40,128]{2,1,0:T(8,128)}), f32[32,40,128]{2,1,0:T(8,128)S(1)}, u32[]{:S(2)}, u32[]{:S(2)}) %all-to-all-start.1) | async-done | bytes 655392 | tf_op jit(solution)/shard_map/all_to_all | solution.py:492
  138.2 0.8 copy-done.6
  139.0 2.7 %curvature.3 = f32[1,4]{1,0:T(1,128)} custom-call(f32[4]{0:T(128)} %dynamic-slice_reduce_fusion.refs_0_, f32[1280,128]{1,0:T(8,128)} %bitcast.62, bf16[4,256,256]{2,1,0:T(8,128)(2,1)} %copy-done.1, bf16[4,256,256]{2,1,0:T(8,128)(2,1)} %copy-done.2, s32[4,128]{1,0:T(4,128)} %refs_4_.3, f32[1,4]{1,0:T(1,128)} %curvature.2.refs_5_), custom_call_target="tpu_custom_call" | custom-call | flops 625000000 | tf_op jit(solution)/shard_map/curvature/pallas_call | solution.py:558
  (27 shorter events, 0.1 us)
Async XLA Ops:
  0.0 7.6 %copy-start.7 = (s32[512,3]{0,1:T(4,128)S(1)}, s32[512,3]{0,1:T(4,128)}, u32[]{:S(2)}) copy-start(s32[512,3]{0,1:T(4,128)} %param.12) | copy-start | bytes 18436
  6.1 12.2 %collective-permute-start.5 = (f32[3,2,512,512]{3,2,1,0:T(8,128)}, f32[3,2,512,512]{3,2,1,0:T(8,128)}, u32[]{:S(2)}, u32[]{:S(2)}) collective-permute-start(f32[3,2,512,512]{3,2,1,0:T(8,128)} %get-tuple-element.61), channel_id=1, source_target_pairs={{0,1},{1,0},{2,3},{3,2},{4,5},{5,4},{6,7},{7,6},{8,9},{9,8},{10,11... | collective-permute-start | bytes 18874376 | tf_op jit(solution)/shard_map/ppermute | solution.py:631
  7.6 10.7 %collective-permute-start.4 = (f32[8,512]{1,0:T(8,128)S(1)}, f32[8,512]{1,0:T(8,128)S(1)}, u32[]{:S(2)}, u32[]{:S(2)}) collective-permute-start(f32[8,512]{1,0:T(8,128)S(1)} %pad.4), channel_id=1, source_target_pairs={{0,1},{1,0},{2,3},{3,2},{4,5},{5,4},{6,7},{7,6},{8,9},{9,8},{10,11... | collective-permute-start | bytes 49160 | tf_op jit(solution)/shard_map/ppermute | solution.py:633
  7.7 20.1 %all-to-all-start = ((f32[128,1,128]{2,1,0:T(1,128)}), f32[128,1,128]{2,1,0:T(1,128)S(1)}, u32[]{:S(2)}, u32[]{:S(2)}) async-start(f32[128,1,128]{2,1,0:T(1,128)} %get-tuple-element.60), calls=%async_computation | async-start | bytes 131072 | tf_op jit(solution)/shard_map/all_to_all | solution.py:635
  27.8 8.9 %copy-start.3 = (bf16[3,2048,512]{2,1,0:T(8,128)(2,1)S(1)}, bf16[3,2048,512]{2,1,0:T(8,128)(2,1)}, u32[]{:S(2)}) copy-start(bf16[3,2048,512]{2,1,0:T(8,128)(2,1)} %join_rows.1.matrices_ref.refs_2_) | copy-start | bytes 18874372
  32.8 15.3 %collective-permute-start.8 = (f32[16,40,128]{2,1,0:T(8,128)S(1)}, f32[16,40,128]{2,1,0:T(8,128)S(1)}, u32[]{:S(2)}, u32[]{:S(2)}) collective-permute-start(f32[16,40,128]{2,1,0:T(8,128)S(1)} %bitcast.54), channel_id=1, source_target_pairs={{0,2},{2,4},{4,6},{6,0},{1,3},{3,5},{5,7},{7,1},{8,10},{10,12},{12... | collective-permute-start | bytes 983048 | tf_op jit(solution)/shard_map/ppermute | solution.py:392
  33.1 14.9 %collective-permute-start.9 = (f32[16,40,128]{2,1,0:T(8,128)S(1)}, f32[16,40,128]{2,1,0:T(8,128)S(1)}, u32[]{:S(2)}, u32[]{:S(2)}) collective-permute-start(f32[16,40,128]{2,1,0:T(8,128)S(1)} %bitcast.53), channel_id=1, source_target_pairs={{0,6},{2,0},{4,2},{6,4},{1,7},{3,1},{5,3},{7,5},{8,14},{10,8},{12,... | collective-permute-start | bytes 983048 | tf_op jit(solution)/shard_map/ppermute | solution.py:396
  39.2 18.2 %collective-permute-start.7 = (f32[16,40,128]{2,1,0:T(8,128)S(1)}, f32[16,40,128]{2,1,0:T(8,128)S(1)}, u32[]{:S(2)}, u32[]{:S(2)}) collective-permute-start(f32[16,40,128]{2,1,0:T(8,128)S(1)} %bitcast.52), channel_id=1, source_target_pairs={{0,6},{2,0},{4,2},{6,4},{1,7},{3,1},{5,3},{7,5},{8,14},{10,8},{12,... | collective-permute-start | bytes 983048 | tf_op jit(solution)/shard_map/ppermute | solution.py:396
  40.2 17.3 %collective-permute-start.6 = (f32[16,40,128]{2,1,0:T(8,128)S(1)}, f32[16,40,128]{2,1,0:T(8,128)S(1)}, u32[]{:S(2)}, u32[]{:S(2)}) collective-permute-start(f32[16,40,128]{2,1,0:T(8,128)S(1)} %bitcast.51), channel_id=1, source_target_pairs={{0,2},{2,4},{4,6},{6,0},{1,3},{3,5},{5,7},{7,1},{8,10},{10,12},{12... | collective-permute-start | bytes 983048 | tf_op jit(solution)/shard_map/ppermute | solution.py:392
  41.6 18.8 %slice-start = ((s8[6291456]{0:T(1024)(128)(4,1)}), s8[4194304]{0:T(1024)(128)(4,1)S(1)}, s32[]{:S(2)}) async-start(s8[6291456]{0:T(1024)(128)(4,1)} %bitcast.58), calls=%async_computation.3 | async-start | bytes 8388608
  48.2 15.7 %collective-permute-start.12 = (f32[32,40,128]{2,1,0:T(8,128)S(1)}, f32[32,40,128]{2,1,0:T(8,128)S(1)}, u32[]{:S(2)}, u32[]{:S(2)}) collective-permute-start(f32[32,40,128]{2,1,0:T(8,128)S(1)} %get-tuple-element.83), channel_id=1, source_target_pairs={{0,2},{2,4},{4,6},{6,0},{1,3},{3,5},{5,7},{7,1},{8,10},{10,12},{12... | collective-permute-start | bytes 1966088 | tf_op jit(solution)/shard_map/ppermute | solution.py:392
  48.3 15.6 %collective-permute-start.13 = (f32[32,40,128]{2,1,0:T(8,128)S(1)}, f32[32,40,128]{2,1,0:T(8,128)S(1)}, u32[]{:S(2)}, u32[]{:S(2)}) collective-permute-start(f32[32,40,128]{2,1,0:T(8,128)S(1)} %get-tuple-element.84), channel_id=1, source_target_pairs={{0,6},{2,0},{4,2},{6,4},{1,7},{3,1},{5,3},{7,5},{8,14},{10,8},{12,... | collective-permute-start | bytes 1966088 | tf_op jit(solution)/shard_map/ppermute | solution.py:396
  51.0 9.4 %slice-start.1 = ((s8[6291456]{0:T(1024)(128)(4,1)}), s8[2097152]{0:T(1024)(128)(4,1)S(1)}, s32[]{:S(2)}) async-start(s8[6291456]{0:T(1024)(128)(4,1)} %bitcast.58), calls=%async_computation.4 | async-start | bytes 4194304
  51.0 26.9 %copy-start.5 = (f32[32,40,128]{2,1,0:T(8,128)S(1)}, f32[32,40,128]{2,1,0:T(8,128)}, u32[]{:S(2)}) copy-start(f32[32,40,128]{2,1,0:T(8,128)} %get-tuple-element.96.refs_6_) | copy-start | bytes 1966084
  57.6 20.2 %collective-permute-start.14 = (f32[32,40,128]{2,1,0:T(8,128)S(1)}, f32[32,40,128]{2,1,0:T(8,128)S(1)}, u32[]{:S(2)}, u32[]{:S(2)}) collective-permute-start(f32[32,40,128]{2,1,0:T(8,128)S(1)} %get-tuple-element.86), channel_id=1, source_target_pairs={{0,2},{2,4},{4,6},{6,0},{1,3},{3,5},{5,7},{7,1},{8,10},{10,12},{12... | collective-permute-start | bytes 1966088 | tf_op jit(solution)/shard_map/ppermute | solution.py:392
  57.7 20.1 %collective-permute-start.15 = (f32[32,40,128]{2,1,0:T(8,128)S(1)}, f32[32,40,128]{2,1,0:T(8,128)S(1)}, u32[]{:S(2)}, u32[]{:S(2)}) collective-permute-start(f32[32,40,128]{2,1,0:T(8,128)S(1)} %get-tuple-element.87), channel_id=1, source_target_pairs={{0,6},{2,0},{4,2},{6,4},{1,7},{3,1},{5,3},{7,5},{8,14},{10,8},{12,... | collective-permute-start | bytes 1966088 | tf_op jit(solution)/shard_map/ppermute | solution.py:396
  77.8 48.1 %copy-start = (bf16[4,128,2,128]{3,2,1,0:T(2,128)(2,1)S(1)}, bf16[4,128,2,128]{3,2,1,0:T(2,128)(2,1)}, u32[]{:S(2)}) copy-start(bf16[4,128,2,128]{3,2,1,0:T(2,128)(2,1)} %param.14) | copy-start | bytes 786436
  80.6 35.8 %all-to-all-start.2 = ((f32[32,3,40,128]{3,2,1,0:T(8,128)}), f32[32,3,40,128]{3,2,1,0:T(8,128)}, u32[]{:S(2)}, u32[]{:S(2)}) async-start(f32[32,3,40,128]{3,2,1,0:T(8,128)} %get-tuple-element.95), calls=%async_computation.2 | async-start | bytes 3932160 | tf_op jit(solution)/shard_map/all_to_all | solution.py:492
  88.4 10.4 %collective-permute-start.10 = (f32[16,40,128]{2,1,0:T(8,128)S(1)}, f32[16,40,128]{2,1,0:T(8,128)S(1)}, u32[]{:S(2)}, u32[]{:S(2)}) collective-permute-start(f32[16,40,128]{2,1,0:T(8,128)S(1)} %bitcast.50), channel_id=1, source_target_pairs={{0,2},{2,4},{4,6},{6,0},{1,3},{3,5},{5,7},{7,1},{8,10},{10,12},{12... | collective-permute-start | bytes 983048 | tf_op jit(solution)/shard_map/ppermute | solution.py:392
  89.0 9.7 %collective-permute-start.11 = (f32[16,40,128]{2,1,0:T(8,128)S(1)}, f32[16,40,128]{2,1,0:T(8,128)S(1)}, u32[]{:S(2)}, u32[]{:S(2)}) collective-permute-start(f32[16,40,128]{2,1,0:T(8,128)S(1)} %bitcast.49), channel_id=1, source_target_pairs={{0,6},{2,0},{4,2},{6,4},{1,7},{3,1},{5,3},{7,5},{8,14},{10,8},{12,... | collective-permute-start | bytes 983048 | tf_op jit(solution)/shard_map/ppermute | solution.py:396
  99.0 16.5 %collective-permute-start.16 = (f32[32,40,128]{2,1,0:T(8,128)S(1)}, f32[32,40,128]{2,1,0:T(8,128)S(1)}, u32[]{:S(2)}, u32[]{:S(2)}) collective-permute-start(f32[32,40,128]{2,1,0:T(8,128)S(1)} %get-tuple-element.90), channel_id=1, source_target_pairs={{0,2},{2,4},{4,6},{6,0},{1,3},{3,5},{5,7},{7,1},{8,10},{10,12},{12... | collective-permute-start | bytes 1966088 | tf_op jit(solution)/shard_map/ppermute | solution.py:392
  99.6 15.9 %collective-permute-start.17 = (f32[32,40,128]{2,1,0:T(8,128)S(1)}, f32[32,40,128]{2,1,0:T(8,128)S(1)}, u32[]{:S(2)}, u32[]{:S(2)}) collective-permute-start(f32[32,40,128]{2,1,0:T(8,128)S(1)} %get-tuple-element.91), channel_id=1, source_target_pairs={{0,6},{2,0},{4,2},{6,4},{1,7},{3,1},{5,3},{7,5},{8,14},{10,8},{12,... | collective-permute-start | bytes 1966088 | tf_op jit(solution)/shard_map/ppermute | solution.py:396
  116.4 21.7 %all-to-all-start.1 = ((f32[32,40,128]{2,1,0:T(8,128)}), f32[32,40,128]{2,1,0:T(8,128)S(1)}, u32[]{:S(2)}, u32[]{:S(2)}) async-start(f32[32,40,128]{2,1,0:T(8,128)} %total.1), calls=%async_computation.1 | async-start | bytes 1310720 | tf_op jit(solution)/shard_map/all_to_all | solution.py:492
  126.5 0.8 copy-start.1
  127.3 0.8 copy-start.2
  138.2 0.8 copy-start.6

commit v7 on v6

--- a/solution.py
+++ b/solution.py
@@ -554,14 +554,14 @@
 def curvature(first, units, weight, arrived, vectors, adjoint, occupied, previous=(), after=()):
     width = arrived.shape[-1]
     flat = arrived.reshape(-1, width)
-    matrix = pl.BlockSpec((1, 2 * width, 2 * width), lambda u: (first + u, 0, 0))
+    matrix = pl.BlockSpec((1, 2 * width, 2 * width), lambda u: (u, 0, 0))
     return pl.pallas_call(
         lambda *refs: curvature_kernel(first, units, len(previous), *refs),
         grid=(units,),
         out_shape=jax.ShapeDtypeStruct((1, SUB), f32),
         in_specs=[
             SMEM,
-            pl.BlockSpec(flat.shape, lambda u: (0, 0)),
+            VMEM,
             matrix,
             matrix,
             pl.BlockSpec(occupied.shape, lambda u: (0, 0)),
@@ -569,7 +569,7 @@
         + [pl.BlockSpec((1, SUB), lambda u: (0, 0))] * len(previous)
         + [ANY] * len(after),
         out_specs=pl.BlockSpec((1, SUB), lambda u: (0, 0)),
-        compiler_params=params(58),
+        compiler_params=params(58 if units > 1 else 12),
         cost_estimate=cost(2.5 * units),
         interpret=INTERPRET,
         name="curvature",
@@ -599,15 +599,15 @@
             back_ref[0, n:, :n] = (-turned).astype(bf16)
 
 
-def vector_matrices(eigvecs, after):
+def vector_matrices(eigvecs, first, count, after):
     slots, width = eigvecs.shape[0], eigvecs.shape[1]
-    shape = jax.ShapeDtypeStruct((slots, 2 * width, 2 * width), bf16)
+    shape = jax.ShapeDtypeStruct((count, 2 * width, 2 * width), bf16)
     square = pl.BlockSpec((1, 2 * width, 2 * width), lambda i: (i, 0, 0))
     return pl.pallas_call(
         vector_kernel,
-        grid=(slots,),
+        grid=(count,),
         out_shape=(shape, shape),
-        in_specs=[pl.BlockSpec((1, 2 * width, width), lambda i: (i, 0, 0))] + [ANY] * len(after),
+        in_specs=[pl.BlockSpec((1, 2 * width, width), lambda i: (first + i, 0, 0))] + [ANY] * len(after),
         out_specs=(square, square),
         scratch_shapes=[pltpu.VMEM((2 * width, width), f32)],
         compiler_params=params(4),
@@ -675,10 +675,11 @@
     unit123 = to_owners(placed)
     right3, left3, token = add_arrived(*hop3, right3, left3, (token,))
     ring3 = second_hop(right3, left3)
-    turning, back = vector_matrices(eigvecs, (token,))
+    turning0, back0 = vector_matrices(eigvecs, 0, 1, (token,))
+    turning, back = vector_matrices(eigvecs, 1, SUB - 1, (token,))
     unit0 = to_owners(total(keep3, *ring3))
     curve = curvature(1, 3, weight, unit123, turning, back, occupied)
-    return curvature(0, 1, weight, unit0, turning, back, occupied, (curve,)).reshape(SUB)
+    return curvature(0, 1, weight, unit0, turning0, back0, occupied, (curve,)).reshape(SUB)
 
 
 def solution(mesh):

time: 142 us -> 142 us (level)
  no operation moved by 1% of the time
where the time goes in v7:
time: 142 us; the launch traced here: 141 us
  Pallas kernels  48.2 us (34%)
  starting transfers between devices  44.1 us (31%)
  waiting for transfers between devices  42.9 us (30%)
  local copies, waits for them, and re-layouts  4.33 us (3%)
  between operations  1.63 us (1%)
    ppermute x6, waiting for transfers between devices, to_right(): return lax.ppermute(value, 'row_0', [(i, (i + 1) % NX) for i in range(NX)])  35.3 us
    pallas_call x4, Pallas kernels, fourier(): pl.pallas_call(lambda *refs: fourier_kernel(low, pitches, len(after), *re...  18.9 us
    all_to_all x2, starting transfers between devices, to_owners(): return lax.all_to_all(value, PLANE, split_axis=0, concat_axis=0, tiled=True)  16.7 us
    ppermute x6, starting transfers between devices, to_left(): return lax.ppermute(value, 'row_0', [(i, (i - 1) % NX) for i in range(NX)])  12.1 us
    all_to_all x1, starting transfers between devices, body(): table = lax.all_to_all(mine, KA_ROW, 0, 0, tiled=True)  10.6 us
    pallas_call x2, Pallas kernels, curvature(): pl.pallas_call(lambda *refs: curvature_kernel(first, units, len(previous)...  7.43 us
    pallas_call x1, Pallas kernels, join_rows(): pl.pallas_call(join_kernel, out_shape=jax.ShapeDtypeStruct((3, 4 * depth,...  6.65 us
    pallas_call x1, Pallas kernels, send_rows(): pl.pallas_call(send_kernel, out_shape=(jax.ShapeDtypeStruct(shape, f32),...  5.4 us
  transfers between devices with their start and end apart: 17, of which 5 were waited for; matrix products, arithmetic and copies ran while one was open for 2% of the time, Pallas kernels for 23%

profile of v7, /device:TPU:1, one launch (start us, length us, event | category | flops | bytes accessed | tf_op | source)
XLA Modules:
  0.0 141.1 jit_solution(16451200129142500650)
XLA Ops:
  0.7 5.4 %send_rows.1 = (f32[3,2,512,512]{3,2,1,0:T(8,128)}, f32[128,1,128]{2,1,0:T(1,128)}) custom-call(s32[1]{0:T(128)S(6)} %sub.3.core_ref, s32[1]{0:T(128)} %bitcast.7.row_ref, f32[3,8]{1,0:T(4,128)} %bitcast.64, s32[1,8]{1,0:T(1,128)} %bitcast.65, s32[1,1]{1,0:T(1,128)} %bitcast.35.order_ref, bf16[512,48,128]{2,1,0:T(8,128)(2,1)} %bitcast.62), custom_call_target="tpu_custom_call" | custom-call | flops 1250000000 | tf_op jit(solution)/shard_map/send_rows/pallas_call | solution.py:182
  6.1 1.5 %collective-permute-start.5 = (f32[3,2,512,512]{3,2,1,0:T(8,128)}, f32[3,2,512,512]{3,2,1,0:T(8,128)}, u32[]{:S(2)}, u32[]{:S(2)}) collective-permute-start(f32[3,2,512,512]{3,2,1,0:T(8,128)} %get-tuple-element.63), channel_id=1, source_target_pairs={{0,1},{1,0},{2,3},{3,2},{4,5},{5,4},{6,7},{7,6},{8,9},{9,8},{10,11... | collective-permute-start | bytes 18874376 | tf_op jit(solution)/shard_map/ppermute | solution.py:631
  7.6 0.1 collective-permute-start.4
  7.7 10.6 %all-to-all-start = ((f32[128,1,128]{2,1,0:T(1,128)}), f32[128,1,128]{2,1,0:T(1,128)S(1)}, u32[]{:S(2)}, u32[]{:S(2)}) async-start(f32[128,1,128]{2,1,0:T(1,128)} %get-tuple-element.62), calls=%async_computation | async-start | bytes 131072 | tf_op jit(solution)/shard_map/all_to_all | solution.py:635
  18.3 6.7 %join_rows.1.matrices_ref.refs_2_ = bf16[3,2048,512]{2,1,0:T(8,128)(2,1)} custom-call(s32[1]{0:T(128)} %bitcast.6.core_ref, bf16[512,48,128]{2,1,0:T(8,128)(2,1)} %bitcast.63, f32[3,2,512,512]{3,2,1,0:T(8,128)} %collective-permute-done.5.other_ref), custom_call_target="tpu_custom_call" | custom-call | flops 1250000000 | tf_op jit(solution)/shard_map/join_rows/pallas_call | solution.py:230
  25.0 2.8 %all-to-all-done = f32[128,1,128]{2,1,0:T(1,128)S(1)} async-done(((f32[128,1,128]{2,1,0:T(1,128)}), f32[128,1,128]{2,1,0:T(1,128)S(1)}, u32[]{:S(2)}, u32[]{:S(2)}) %all-to-all-start) | async-done | bytes 65568 | tf_op jit(solution)/shard_map/all_to_all | solution.py:635
  27.8 5.0 %first_fourier.1 = (f32[640,128]{1,0:T(8,128)S(1)}, f32[640,128]{1,0:T(8,128)S(1)}, f32[512,128]{1,0:T(8,128)S(1)}, s32[8,128]{1,0:T(8,128)S(1)}, f32[8,128]{1,0:T(8,128)S(1)}, /*index=5*/f32[8,128]{1,0:T(8,128)S(1)}) custom-call(s32[1]{0:T(128)} %bitcast.5.place_ref, f32[128,128]{1,0:T(8,128)S(1)} %bitcast.49, ...), custom_call_target="tpu_custom_call" | custom-call | flops 1250000000 | tf_op jit(solution)/shard_map/first_fourier/pallas_call | solution.py:366
  32.8 0.4 collective-permute-start.8
  33.2 2.4 %collective-permute-start.9 = (f32[16,40,128]{2,1,0:T(8,128)S(1)}, f32[16,40,128]{2,1,0:T(8,128)S(1)}, u32[]{:S(2)}, u32[]{:S(2)}) collective-permute-start(f32[16,40,128]{2,1,0:T(8,128)S(1)} %bitcast.54), channel_id=1, source_target_pairs={{0,6},{2,0},{4,2},{6,4},{1,7},{3,1},{5,3},{7,5},{8,14},{10,8},{12,... | collective-permute-start | bytes 983048 | tf_op jit(solution)/shard_map/ppermute | solution.py:396
  35.5 0.6 slice.3
  36.8 2.5 %fourier.6 = (f32[640,128]{1,0:T(8,128)S(1)}, f32[640,128]{1,0:T(8,128)S(1)}, f32[640,128]{1,0:T(8,128)S(1)}, f32[640,128]{1,0:T(8,128)S(1)}, f32[8,128]{1,0:T(8,128)S(1)}) custom-call(f32[512,128]{1,0:T(8,128)S(1)} %get-tuple-element.65.refs_0_, f32[8,1024]{1,0:T(8,128)S(1)} %pad_maximum_fusion.coords_ref.refs_1_, bf16[3,2048,512]{2,1,0:T(8,128)(2,1)S(1)} %copy-done.6, ...), custom_call_target="tpu_custom_call" | custom-call | flops 1000000000 | tf_op jit(solution)/shard_map/fourier/pallas_call | solution.py:328
  39.3 0.1 collective-permute-start.7
  39.4 0.9 conditional.1
  39.4 0.9 broadcast.2
  40.3 1.4 %collective-permute-start.6 = (f32[16,40,128]{2,1,0:T(8,128)S(1)}, f32[16,40,128]{2,1,0:T(8,128)S(1)}, u32[]{:S(2)}, u32[]{:S(2)}) collective-permute-start(f32[16,40,128]{2,1,0:T(8,128)S(1)} %bitcast.52), channel_id=1, source_target_pairs={{0,2},{2,4},{4,6},{6,0},{1,3},{3,5},{5,7},{7,1},{8,10},{10,12},{12... | collective-permute-start | bytes 983048 | tf_op jit(solution)/shard_map/ppermute | solution.py:392
  41.7 6.4 %fourier.7 = (f32[1280,128]{1,0:T(8,128)S(1)}, f32[1280,128]{1,0:T(8,128)S(1)}, f32[1280,128]{1,0:T(8,128)S(1)}, f32[8,128]{1,0:T(8,128)}) custom-call(f32[512,128]{1,0:T(8,128)S(1)} %get-tuple-element.65.refs_0_, f32[8,1024]{1,0:T(8,128)S(1)} %pad_maximum_fusion.coords_ref.refs_1_, bf16[3,2048,512]{2,1,0:T(8,128)(2,1)} %join_rows.1.matrices_ref.refs_2_, ...), custom_call_target="tpu_custom_call" | custom-call | flops 1250000000 | tf_op jit(solution)/shard_map/fourier/pallas_call | solution.py:328
  48.2 0.2 add_arrived.5
  48.4 0.1 collective-permute-start.12
  48.5 2.7 %collective-permute-start.13 = (f32[32,40,128]{2,1,0:T(8,128)S(1)}, f32[32,40,128]{2,1,0:T(8,128)S(1)}, u32[]{:S(2)}, u32[]{:S(2)}) collective-permute-start(f32[32,40,128]{2,1,0:T(8,128)S(1)} %get-tuple-element.86), channel_id=1, source_target_pairs={{0,6},{2,0},{4,2},{6,4},{1,7},{3,1},{5,3},{7,5},{8,14},{10,8},{12,... | collective-permute-start | bytes 1966088 | tf_op jit(solution)/shard_map/ppermute | solution.py:396
  51.1 6.4 %fourier.8 = (f32[1280,128]{1,0:T(8,128)S(1)}, f32[1280,128]{1,0:T(8,128)S(1)}, f32[1280,128]{1,0:T(8,128)S(1)}, f32[8,128]{1,0:T(8,128)}) custom-call(f32[512,128]{1,0:T(8,128)S(1)} %get-tuple-element.65.refs_0_, f32[8,1024]{1,0:T(8,128)S(1)} %pad_maximum_fusion.coords_ref.refs_1_, bf16[3,2048,512]{2,1,0:T(8,128)(2,1)} %join_rows.1.matrices_ref.refs_2_, ...), custom_call_target="tpu_custom_call" | custom-call | flops 1250000000 | tf_op jit(solution)/shard_map/fourier/pallas_call | solution.py:328
  57.6 0.2 add_arrived.6
  57.8 0.1 collective-permute-start.14
  57.8 2.7 %collective-permute-start.15 = (f32[32,40,128]{2,1,0:T(8,128)S(1)}, f32[32,40,128]{2,1,0:T(8,128)S(1)}, u32[]{:S(2)}, u32[]{:S(2)}) collective-permute-start(f32[32,40,128]{2,1,0:T(8,128)S(1)} %get-tuple-element.89), channel_id=1, source_target_pairs={{0,6},{2,0},{4,2},{6,4},{1,7},{3,1},{5,3},{7,5},{8,14},{10,8},{12,... | collective-permute-start | bytes 1966088 | tf_op jit(solution)/shard_map/ppermute | solution.py:396
  60.5 3.6 %fourier.9 = (f32[1280,128]{1,0:T(8,128)S(1)}, f32[1280,128]{1,0:T(8,128)S(1)}, f32[1280,128]{1,0:T(8,128)S(1)}, f32[8,128]{1,0:T(8,128)S(1)}) custom-call(f32[512,128]{1,0:T(8,128)S(1)} %get-tuple-element.65.refs_0_, f32[8,1024]{1,0:T(8,128)S(1)} %pad_maximum_fusion.coords_ref.refs_1_, bf16[3,2048,512]{2,1,0:T(8,128)(2,1)S(1)} %bitcast.61, ...), custom_call_target="tpu_custom_call" | custom-call | flops 1250000000 | tf_op jit(solution)/shard_map/fourier/pallas_call | solution.py:328
  64.1 0.0 collective-permute-done.12.refs_1_
  64.1 13.9 %collective-permute-done.14.refs_4_ = f32[32,40,128]{2,1,0:T(8,128)S(1)} collective-permute-done((f32[32,40,128]{2,1,0:T(8,128)S(1)}, f32[32,40,128]{2,1,0:T(8,128)S(1)}, u32[]{:S(2)}, u32[]{:S(2)}) %collective-permute-start.14) | collective-permute-done | bytes 655392 | tf_op jit(solution)/shard_map/ppermute | solution.py:392
  78.0 0.0 collective-permute-done.15.refs_5_
  78.0 2.7 %place_slots.1 = (f32[32,3,40,128]{3,2,1,0:T(8,128)}, f32[8,128]{1,0:T(8,128)S(1)}) custom-call(s32[1]{0:T(128)} %bitcast.5.place_ref, s32[8,128]{1,0:T(8,128)S(1)} %get-tuple-element.83.slots_ref, f32[32,40,128]{2,1,0:T(8,128)S(1)} %bitcast.36, f32[32,40,128]{2,1,0:T(8,128)S(1)} %collective-permute-done.12.refs_1_, ...), custom_call_target="tpu_custom_call" | custom-call | flops 1000000000 | tf_op jit(solution)/shard_map/place_slots/pallas_call | solution.py:458
  80.8 7.8 %all-to-all-start.2 = ((f32[32,3,40,128]{3,2,1,0:T(8,128)}), f32[32,3,40,128]{3,2,1,0:T(8,128)}, u32[]{:S(2)}, u32[]{:S(2)}) async-start(f32[32,3,40,128]{3,2,1,0:T(8,128)} %get-tuple-element.97), calls=%async_computation.2 | async-start | bytes 3932160 | tf_op jit(solution)/shard_map/all_to_all | solution.py:492
  88.5 0.6 collective-permute-start.10
  89.2 2.1 %collective-permute-start.11 = (f32[16,40,128]{2,1,0:T(8,128)S(1)}, f32[16,40,128]{2,1,0:T(8,128)S(1)}, u32[]{:S(2)}, u32[]{:S(2)}) collective-permute-start(f32[16,40,128]{2,1,0:T(8,128)S(1)} %bitcast.50), channel_id=1, source_target_pairs={{0,6},{2,0},{4,2},{6,4},{1,7},{3,1},{5,3},{7,5},{8,14},{10,8},{12,... | collective-permute-start | bytes 983048 | tf_op jit(solution)/shard_map/ppermute | solution.py:396
  91.3 7.6 %collective-permute-done.10.refs_0_ = f32[16,40,128]{2,1,0:T(8,128)S(1)} collective-permute-done((f32[16,40,128]{2,1,0:T(8,128)S(1)}, f32[16,40,128]{2,1,0:T(8,128)S(1)}, u32[]{:S(2)}, u32[]{:S(2)}) %collective-permute-start.10) | collective-permute-done | bytes 327712 | tf_op jit(solution)/shard_map/ppermute | solution.py:392
  98.9 0.2 add_arrived.7
  99.1 0.6 collective-permute-start.16
  99.7 2.2 %collective-permute-start.17 = (f32[32,40,128]{2,1,0:T(8,128)S(1)}, f32[32,40,128]{2,1,0:T(8,128)S(1)}, u32[]{:S(2)}, u32[]{:S(2)}) collective-permute-start(f32[32,40,128]{2,1,0:T(8,128)S(1)} %get-tuple-element.93), channel_id=1, source_target_pairs={{0,6},{2,0},{4,2},{6,4},{1,7},{3,1},{5,3},{7,5},{8,14},{10,8},{12,... | collective-permute-start | bytes 1966088 | tf_op jit(solution)/shard_map/ppermute | solution.py:396
  101.8 13.8 %collective-permute-done.16.right_ref = f32[32,40,128]{2,1,0:T(8,128)S(1)} collective-permute-done((f32[32,40,128]{2,1,0:T(8,128)S(1)}, f32[32,40,128]{2,1,0:T(8,128)S(1)}, u32[]{:S(2)}, u32[]{:S(2)}) %collective-permute-start.16) | collective-permute-done | bytes 655392 | tf_op jit(solution)/shard_map/ppermute | solution.py:392
  115.6 0.0 collective-permute-done.17.left_ref
  115.6 0.9 total.1
  116.6 8.9 %all-to-all-start.1 = ((f32[32,40,128]{2,1,0:T(8,128)}), f32[32,40,128]{2,1,0:T(8,128)S(1)}, u32[]{:S(2)}, u32[]{:S(2)}) async-start(f32[32,40,128]{2,1,0:T(8,128)} %total.1), calls=%async_computation.1 | async-start | bytes 1310720 | tf_op jit(solution)/shard_map/all_to_all | solution.py:492
  125.5 0.7 dynamic-slice_reduce_fusion.refs_0_
  126.2 0.1 vector_matrices.2
  126.4 0.4 vector_matrices.3
  126.8 0.8 copy-done.3
  127.6 0.7 copy-done.4
  128.3 5.4 %curvature.2.refs_5_ = f32[1,4]{1,0:T(1,128)} custom-call(f32[4]{0:T(128)} %dynamic-slice_reduce_fusion.refs_0_, f32[3840,128]{1,0:T(8,128)} %bitcast.32.refs_1_, bf16[3,256,256]{2,1,0:T(8,128)(2,1)} %copy-done.3, bf16[3,256,256]{2,1,0:T(8,128)(2,1)} %copy-done.4, s32[4,128]{1,0:T(4,128)} %refs_4_.3), custom_call_target="tpu_custom_call" | custom-call | flops 1875000064 | tf_op jit(solution)/shard_map/curvature/pallas_call | solution.py:558
  133.7 4.8 %all-to-all-done.1 = f32[32,40,128]{2,1,0:T(8,128)S(1)} async-done(((f32[32,40,128]{2,1,0:T(8,128)}), f32[32,40,128]{2,1,0:T(8,128)S(1)}, u32[]{:S(2)}, u32[]{:S(2)}) %all-to-all-start.1) | async-done | bytes 655392 | tf_op jit(solution)/shard_map/all_to_all | solution.py:492
  138.4 0.6 copy-done.5
  139.1 2.1 %curvature.3 = f32[1,4]{1,0:T(1,128)} custom-call(f32[4]{0:T(128)S(1)} %copy-done, f32[1280,128]{1,0:T(8,128)S(1)} %bitcast.40, bf16[1,256,256]{2,1,0:T(8,128)(2,1)S(1)} %get-tuple-element.95.refs_2_, bf16[1,256,256]{2,1,0:T(8,128)(2,1)S(1)} %get-tuple-element.96.refs_3_, s32[4,128]{1,0:T(4,128)S(1)} %copy-done.2, f32[1,4]{1,0:T(1,128)S(1)} %copy-done.5), custom_call_target="tpu_custom_call" | custom-call | flops 625000000 | tf_op jit(solution)/shard_map/curvature/pallas_call | solution.py:558
  (32 shorter events, 0.1 us)
Async XLA Ops:
  0.0 7.5 %copy-start.9 = (s32[512,3]{0,1:T(4,128)S(1)}, s32[512,3]{0,1:T(4,128)}, u32[]{:S(2)}) copy-start(s32[512,3]{0,1:T(4,128)} %param.12) | copy-start | bytes 18436
  6.1 12.2 %collective-permute-start.5 = (f32[3,2,512,512]{3,2,1,0:T(8,128)}, f32[3,2,512,512]{3,2,1,0:T(8,128)}, u32[]{:S(2)}, u32[]{:S(2)}) collective-permute-start(f32[3,2,512,512]{3,2,1,0:T(8,128)} %get-tuple-element.63), channel_id=1, source_target_pairs={{0,1},{1,0},{2,3},{3,2},{4,5},{5,4},{6,7},{7,6},{8,9},{9,8},{10,11... | collective-permute-start | bytes 18874376 | tf_op jit(solution)/shard_map/ppermute | solution.py:631
  7.6 10.7 %collective-permute-start.4 = (f32[8,512]{1,0:T(8,128)S(1)}, f32[8,512]{1,0:T(8,128)S(1)}, u32[]{:S(2)}, u32[]{:S(2)}) collective-permute-start(f32[8,512]{1,0:T(8,128)S(1)} %pad.4), channel_id=1, source_target_pairs={{0,1},{1,0},{2,3},{3,2},{4,5},{5,4},{6,7},{7,6},{8,9},{9,8},{10,11... | collective-permute-start | bytes 49160 | tf_op jit(solution)/shard_map/ppermute | solution.py:633
  7.7 20.1 %all-to-all-start = ((f32[128,1,128]{2,1,0:T(1,128)}), f32[128,1,128]{2,1,0:T(1,128)S(1)}, u32[]{:S(2)}, u32[]{:S(2)}) async-start(f32[128,1,128]{2,1,0:T(1,128)} %get-tuple-element.62), calls=%async_computation | async-start | bytes 131072 | tf_op jit(solution)/shard_map/all_to_all | solution.py:635
  27.8 9.0 %copy-start.6 = (bf16[3,2048,512]{2,1,0:T(8,128)(2,1)S(1)}, bf16[3,2048,512]{2,1,0:T(8,128)(2,1)}, u32[]{:S(2)}) copy-start(bf16[3,2048,512]{2,1,0:T(8,128)(2,1)} %join_rows.1.matrices_ref.refs_2_) | copy-start | bytes 18874372
  32.8 15.4 %collective-permute-start.8 = (f32[16,40,128]{2,1,0:T(8,128)S(1)}, f32[16,40,128]{2,1,0:T(8,128)S(1)}, u32[]{:S(2)}, u32[]{:S(2)}) collective-permute-start(f32[16,40,128]{2,1,0:T(8,128)S(1)} %bitcast.55), channel_id=1, source_target_pairs={{0,2},{2,4},{4,6},{6,0},{1,3},{3,5},{5,7},{7,1},{8,10},{10,12},{12... | collective-permute-start | bytes 983048 | tf_op jit(solution)/shard_map/ppermute | solution.py:392
  33.2 15.0 %collective-permute-start.9 = (f32[16,40,128]{2,1,0:T(8,128)S(1)}, f32[16,40,128]{2,1,0:T(8,128)S(1)}, u32[]{:S(2)}, u32[]{:S(2)}) collective-permute-start(f32[16,40,128]{2,1,0:T(8,128)S(1)} %bitcast.54), channel_id=1, source_target_pairs={{0,6},{2,0},{4,2},{6,4},{1,7},{3,1},{5,3},{7,5},{8,14},{10,8},{12,... | collective-permute-start | bytes 983048 | tf_op jit(solution)/shard_map/ppermute | solution.py:396
  39.3 18.2 %collective-permute-start.7 = (f32[16,40,128]{2,1,0:T(8,128)S(1)}, f32[16,40,128]{2,1,0:T(8,128)S(1)}, u32[]{:S(2)}, u32[]{:S(2)}) collective-permute-start(f32[16,40,128]{2,1,0:T(8,128)S(1)} %bitcast.53), channel_id=1, source_target_pairs={{0,6},{2,0},{4,2},{6,4},{1,7},{3,1},{5,3},{7,5},{8,14},{10,8},{12,... | collective-permute-start | bytes 983048 | tf_op jit(solution)/shard_map/ppermute | solution.py:396
  40.3 17.3 %collective-permute-start.6 = (f32[16,40,128]{2,1,0:T(8,128)S(1)}, f32[16,40,128]{2,1,0:T(8,128)S(1)}, u32[]{:S(2)}, u32[]{:S(2)}) collective-permute-start(f32[16,40,128]{2,1,0:T(8,128)S(1)} %bitcast.52), channel_id=1, source_target_pairs={{0,2},{2,4},{4,6},{6,0},{1,3},{3,5},{5,7},{7,1},{8,10},{10,12},{12... | collective-permute-start | bytes 983048 | tf_op jit(solution)/shard_map/ppermute | solution.py:392
  41.7 18.8 %slice-start = ((s8[6291456]{0:T(1024)(128)(4,1)}), s8[4194304]{0:T(1024)(128)(4,1)S(1)}, s32[]{:S(2)}) async-start(s8[6291456]{0:T(1024)(128)(4,1)} %bitcast.60), calls=%async_computation.3 | async-start | bytes 8388608
  48.4 15.7 %collective-permute-start.12 = (f32[32,40,128]{2,1,0:T(8,128)S(1)}, f32[32,40,128]{2,1,0:T(8,128)S(1)}, u32[]{:S(2)}, u32[]{:S(2)}) collective-permute-start(f32[32,40,128]{2,1,0:T(8,128)S(1)} %get-tuple-element.85), channel_id=1, source_target_pairs={{0,2},{2,4},{4,6},{6,0},{1,3},{3,5},{5,7},{7,1},{8,10},{10,12},{12... | collective-permute-start | bytes 1966088 | tf_op jit(solution)/shard_map/ppermute | solution.py:392
  48.5 15.6 %collective-permute-start.13 = (f32[32,40,128]{2,1,0:T(8,128)S(1)}, f32[32,40,128]{2,1,0:T(8,128)S(1)}, u32[]{:S(2)}, u32[]{:S(2)}) collective-permute-start(f32[32,40,128]{2,1,0:T(8,128)S(1)} %get-tuple-element.86), channel_id=1, source_target_pairs={{0,6},{2,0},{4,2},{6,4},{1,7},{3,1},{5,3},{7,5},{8,14},{10,8},{12,... | collective-permute-start | bytes 1966088 | tf_op jit(solution)/shard_map/ppermute | solution.py:396
  51.1 9.4 %slice-start.1 = ((s8[6291456]{0:T(1024)(128)(4,1)}), s8[2097152]{0:T(1024)(128)(4,1)S(1)}, s32[]{:S(2)}) async-start(s8[6291456]{0:T(1024)(128)(4,1)} %bitcast.60), calls=%async_computation.4 | async-start | bytes 4194304
  51.1 26.9 %copy-start.8 = (f32[32,40,128]{2,1,0:T(8,128)S(1)}, f32[32,40,128]{2,1,0:T(8,128)}, u32[]{:S(2)}) copy-start(f32[32,40,128]{2,1,0:T(8,128)} %get-tuple-element.100.refs_6_) | copy-start | bytes 1966084
  57.8 20.2 %collective-permute-start.14 = (f32[32,40,128]{2,1,0:T(8,128)S(1)}, f32[32,40,128]{2,1,0:T(8,128)S(1)}, u32[]{:S(2)}, u32[]{:S(2)}) collective-permute-start(f32[32,40,128]{2,1,0:T(8,128)S(1)} %get-tuple-element.88), channel_id=1, source_target_pairs={{0,2},{2,4},{4,6},{6,0},{1,3},{3,5},{5,7},{7,1},{8,10},{10,12},{12... | collective-permute-start | bytes 1966088 | tf_op jit(solution)/shard_map/ppermute | solution.py:392
  57.8 20.2 %collective-permute-start.15 = (f32[32,40,128]{2,1,0:T(8,128)S(1)}, f32[32,40,128]{2,1,0:T(8,128)S(1)}, u32[]{:S(2)}, u32[]{:S(2)}) collective-permute-start(f32[32,40,128]{2,1,0:T(8,128)S(1)} %get-tuple-element.89), channel_id=1, source_target_pairs={{0,6},{2,0},{4,2},{6,4},{1,7},{3,1},{5,3},{7,5},{8,14},{10,8},{12,... | collective-permute-start | bytes 1966088 | tf_op jit(solution)/shard_map/ppermute | solution.py:396
  78.0 48.2 %copy-start.1 = (bf16[4,128,2,128]{3,2,1,0:T(2,128)(2,1)S(1)}, bf16[4,128,2,128]{3,2,1,0:T(2,128)(2,1)}, u32[]{:S(2)}) copy-start(bf16[4,128,2,128]{3,2,1,0:T(2,128)(2,1)} %param.14) | copy-start | bytes 786436
  80.8 35.8 %all-to-all-start.2 = ((f32[32,3,40,128]{3,2,1,0:T(8,128)}), f32[32,3,40,128]{3,2,1,0:T(8,128)}, u32[]{:S(2)}, u32[]{:S(2)}) async-start(f32[32,3,40,128]{3,2,1,0:T(8,128)} %get-tuple-element.97), calls=%async_computation.2 | async-start | bytes 3932160 | tf_op jit(solution)/shard_map/all_to_all | solution.py:492
  88.5 10.4 %collective-permute-start.10 = (f32[16,40,128]{2,1,0:T(8,128)S(1)}, f32[16,40,128]{2,1,0:T(8,128)S(1)}, u32[]{:S(2)}, u32[]{:S(2)}) collective-permute-start(f32[16,40,128]{2,1,0:T(8,128)S(1)} %bitcast.51), channel_id=1, source_target_pairs={{0,2},{2,4},{4,6},{6,0},{1,3},{3,5},{5,7},{7,1},{8,10},{10,12},{12... | collective-permute-start | bytes 983048 | tf_op jit(solution)/shard_map/ppermute | solution.py:392
  89.2 9.7 %collective-permute-start.11 = (f32[16,40,128]{2,1,0:T(8,128)S(1)}, f32[16,40,128]{2,1,0:T(8,128)S(1)}, u32[]{:S(2)}, u32[]{:S(2)}) collective-permute-start(f32[16,40,128]{2,1,0:T(8,128)S(1)} %bitcast.50), channel_id=1, source_target_pairs={{0,6},{2,0},{4,2},{6,4},{1,7},{3,1},{5,3},{7,5},{8,14},{10,8},{12,... | collective-permute-start | bytes 983048 | tf_op jit(solution)/shard_map/ppermute | solution.py:396
  99.1 16.5 %collective-permute-start.16 = (f32[32,40,128]{2,1,0:T(8,128)S(1)}, f32[32,40,128]{2,1,0:T(8,128)S(1)}, u32[]{:S(2)}, u32[]{:S(2)}) collective-permute-start(f32[32,40,128]{2,1,0:T(8,128)S(1)} %get-tuple-element.92), channel_id=1, source_target_pairs={{0,2},{2,4},{4,6},{6,0},{1,3},{3,5},{5,7},{7,1},{8,10},{10,12},{12... | collective-permute-start | bytes 1966088 | tf_op jit(solution)/shard_map/ppermute | solution.py:392
  99.7 15.9 %collective-permute-start.17 = (f32[32,40,128]{2,1,0:T(8,128)S(1)}, f32[32,40,128]{2,1,0:T(8,128)S(1)}, u32[]{:S(2)}, u32[]{:S(2)}) collective-permute-start(f32[32,40,128]{2,1,0:T(8,128)S(1)} %get-tuple-element.93), channel_id=1, source_target_pairs={{0,6},{2,0},{4,2},{6,4},{1,7},{3,1},{5,3},{7,5},{8,14},{10,8},{12,... | collective-permute-start | bytes 1966088 | tf_op jit(solution)/shard_map/ppermute | solution.py:396
  116.6 21.9 %copy-start.2 = (s32[4,128]{1,0:T(4,128)S(1)}, s32[4,128]{1,0:T(4,128)}, u32[]{:S(2)}) copy-start(s32[4,128]{1,0:T(4,128)} %refs_4_.3) | copy-start | bytes 6148
  116.6 21.9 %all-to-all-start.1 = ((f32[32,40,128]{2,1,0:T(8,128)}), f32[32,40,128]{2,1,0:T(8,128)S(1)}, u32[]{:S(2)}, u32[]{:S(2)}) async-start(f32[32,40,128]{2,1,0:T(8,128)} %total.1), calls=%async_computation.1 | async-start | bytes 1310720 | tf_op jit(solution)/shard_map/all_to_all | solution.py:492
  126.2 12.2 %copy-start = (f32[4]{0:T(128)S(1)}, f32[4]{0:T(128)}, u32[]{:S(2)}) copy-start(f32[4]{0:T(128)} %dynamic-slice_reduce_fusion.refs_0_) | copy-start | bytes 52
  126.8 0.8 copy-start.3
  127.6 0.8 copy-start.4
  138.4 0.6 copy-start.5
